TPU v7x, 32 devices: a whole 2x2x4 slice. The times are simulated.
32 devices in a mesh: dp: 8 (over z, core), fsdp: 4 (over y, x).
Axes of the slice: x: 2, y: 2, z: 4, core: 2. Of those that a mesh axis runs over, the one named last changes fastest.
Arguments:
- tokens: bfloat16 [8192, 1024], P(('dp', 'fsdp')), may hold values from -6 to 6
- cotangent: bfloat16 [8192, 1024], P(('dp', 'fsdp')), may hold values from -6 to 6
- seq_lengths: int32 [32], replicated, may hold values from 1 to 256, 5120 in all
- seq_device: int32 [32], replicated, may hold values from 0 to 31, each once
- step_count: int32 [1], replicated, may hold values from 1 to 20
- attend_in: float32 [2, 1024, 3072], P(None, ('dp', 'fsdp'))
- attend_out: float32 [2, 1024, 1024], P(None, ('dp', 'fsdp')), may hold values from -0.75 to 0.75
- expand_weight: float32 [2, 1024, 4096], P(None, ('dp', 'fsdp')), may hold values from -0.1875 to 0.1875
- reduce_weight: float32 [2, 1024, 4096], P(None, ('dp', 'fsdp')), may hold values from -0.09375 to 0.09375
- layer_vectors: float32 [2, 13312], P(None, ('dp', 'fsdp'))
- attend_in_mean: float32 [2, 1024, 3072], P(None, ('dp', 'fsdp')), may hold values from -28 to 28
- attend_out_mean: float32 [2, 1024, 1024], P(None, ('dp', 'fsdp')), may hold values from -28 to 28
- expand_mean: float32 [2, 1024, 4096], P(None, ('dp', 'fsdp')), may hold values from -28 to 28
- reduce_mean: float32 [2, 1024, 4096], P(None, ('dp', 'fsdp')), may hold values from -28 to 28
- vectors_mean: float32 [2, 13312], P(None, ('dp', 'fsdp')), may hold values from -28 to 28
- attend_in_square: float32 [2, 1024, 3072], P(None, ('dp', 'fsdp')), may hold values from 16.384 to 245.76
- attend_out_square: float32 [2, 1024, 1024], P(None, ('dp', 'fsdp')), may hold values from 16.384 to 245.76
- expand_square: float32 [2, 1024, 4096], P(None, ('dp', 'fsdp')), may hold values from 16.384 to 245.76
- reduce_square: float32 [2, 1024, 4096], P(None, ('dp', 'fsdp')), may hold values from 16.384 to 245.76
- vectors_square: float32 [2, 13312], P(None, ('dp', 'fsdp')), may hold values from 819.2 to 16384
Outputs:
- hidden_states: bfloat16 [2, 8192, 1024], P(None, ('dp', 'fsdp'))
- input_grad: bfloat16 [8192, 1024], P(('dp', 'fsdp'))
- attend_in_grad: float32 [2, 1024, 3072], P(None, ('dp', 'fsdp'))
- attend_out_grad: float32 [2, 1024, 1024], P(None, ('dp', 'fsdp'))
- expand_grad: float32 [2, 1024, 4096], P(None, ('dp', 'fsdp'))
- reduce_grad: float32 [2, 1024, 4096], P(None, ('dp', 'fsdp'))
- vectors_grad: float32 [2, 13312], P(None, ('dp', 'fsdp'))
- attend_in_step: float32 [2, 1024, 3072], P(None, ('dp', 'fsdp'))
- attend_out_step: float32 [2, 1024, 1024], P(None, ('dp', 'fsdp'))
- expand_step: float32 [2, 1024, 4096], P(None, ('dp', 'fsdp'))
- reduce_step: float32 [2, 1024, 4096], P(None, ('dp', 'fsdp'))
- vectors_step: float32 [2, 13312], P(None, ('dp', 'fsdp'))
- attend_in_mean_new: float32 [2, 1024, 3072], P(None, ('dp', 'fsdp'))
- attend_out_mean_new: float32 [2, 1024, 1024], P(None, ('dp', 'fsdp'))
- expand_mean_new: float32 [2, 1024, 4096], P(None, ('dp', 'fsdp'))
- reduce_mean_new: float32 [2, 1024, 4096], P(None, ('dp', 'fsdp'))
- vectors_mean_new: float32 [2, 13312], P(None, ('dp', 'fsdp'))
- attend_in_square_new: float32 [2, 1024, 3072], P(None, ('dp', 'fsdp'))
- attend_out_square_new: float32 [2, 1024, 1024], P(None, ('dp', 'fsdp'))
- expand_square_new: float32 [2, 1024, 4096], P(None, ('dp', 'fsdp'))
- reduce_square_new: float32 [2, 1024, 4096], P(None, ('dp', 'fsdp'))
- vectors_square_new: float32 [2, 13312], P(None, ('dp', 'fsdp'))
Inputs may be any that keep to these rules, and one draw needn't show every extreme that they name: `seq_device`: each device is dealt exactly one sequence. `seq_lengths`: the lengths add up to 32 * 256 * 5 // 8 and the longest has exactly 256.
All inputs are finite; a program needn't handle non-finite values.
Results may differ from a plain program's by a relative error of at most 0.02.
Values may be sent and summed in bfloat16 or wider, within the bound.
A program may use at most 256 MiB of HBM per device.

v0:
```python
import jax
import jax.numpy as jnp
from jax import lax
from jax.sharding import PartitionSpec as P

HEADS = 16
LAYERS = 2


NORM_EPSILON = 1e-05
ADAM_EPSILON = 1e-08
LEARNING = 0.02
BETA_FIRST = 0.9
BETA_SECOND = 0.95
DECAY_RATE = 0.1
MASKED_SCORE = -1e30
ROWS_CONTRACT = (((0,), (0,)), ((), ()))
COLS_CONTRACT = (((1,), (1,)), ((), ()))


def layer_norm(values, norm_gain, norm_shift):
    row_mean = jnp.mean(values, -1, keepdims=True)
    centred = values - row_mean
    spread = jnp.mean(centred * centred, -1, keepdims=True)
    return centred * lax.rsqrt(spread + NORM_EPSILON) * norm_gain + norm_shift


def gelu_exact(values):
    return jax.nn.gelu(values, approximate=False)


def split_vectors(vectors, model_width):
    hidden_end = vectors.shape[0] - model_width
    return (
        vectors[0:model_width],
        vectors[model_width : 2 * model_width],
        vectors[2 * model_width : 3 * model_width],
        vectors[3 * model_width : 4 * model_width],
        vectors[4 * model_width : 7 * model_width],
        vectors[7 * model_width : 8 * model_width],
        vectors[8 * model_width : hidden_end],
        vectors[hidden_end:],
    )


def rotary_tables(row_count, model_width, head_dim):
    rot_dim = head_dim // 4
    half_rot = rot_dim // 2
    column = jnp.arange(model_width, dtype=jnp.int32) % head_dim
    freq_slot = (column % half_rot).astype(jnp.float32)
    frequency = 10000.0 ** (-(freq_slot * 2.0) / rot_dim)
    angles = jnp.arange(row_count, dtype=jnp.float32)[:, None] * frequency[None, :]
    inside = (column < rot_dim)[None, :]
    first_half = (column < half_rot)[None, :]
    cosine = jnp.where(inside, jnp.cos(angles), 1.0)
    sine_table = jnp.where(inside, jnp.sin(angles), 0.0)
    return (cosine, sine_table, first_half, inside, half_rot)


def rotate(values, tables):
    cosine, sine_table, first_half, inside, half_rot = tables
    ahead_values = jnp.roll(values, -half_rot, axis=1)
    behind = jnp.roll(values, half_rot, axis=1)
    turned = jnp.where(first_half, -ahead_values, jnp.where(inside, behind, 0.0))
    return values * cosine + turned * sine_table


def head_blocks(model_width):
    head_dim = model_width // HEADS
    group_heads = min(HEADS, max(1, 128 // head_dim))
    return (head_dim, group_heads, group_heads * head_dim, HEADS // group_heads)


def block_slice(matrix, block_index, block_width, group_heads, head_dim):
    piece = lax.dynamic_slice_in_dim(matrix, block_index * block_width, block_width, 1)
    return piece.reshape(matrix.shape[0], group_heads, head_dim)


def masked_scores(query_block, key_block, key_mask, score_scale):
    scores = (
        jnp.einsum("qhd,khd->hqk", query_block, key_block, preferred_element_type=jnp.float32)
        * score_scale
    )
    return jnp.where(key_mask[None], scores, MASKED_SCORE)


def join_blocks(stacked, row_count, model_width):
    return stacked.transpose(1, 0, 2).reshape(row_count, model_width)


def attention_forward(queries, keys, values, key_mask):
    row_count, model_width = queries.shape
    head_dim, group_heads, block_width, block_count = head_blocks(model_width)
    score_scale = head_dim ** (-0.5)

    def one_block(block_index):
        query_block = block_slice(queries, block_index, block_width, group_heads, head_dim)
        key_block = block_slice(keys, block_index, block_width, group_heads, head_dim)
        value_block = block_slice(values, block_index, block_width, group_heads, head_dim)
        scores = masked_scores(query_block, key_block, key_mask, score_scale)
        top_score = jnp.max(scores, -1, keepdims=True)
        weights = jnp.exp(scores - top_score)
        row_total = jnp.sum(weights, -1, keepdims=True)
        probability = (weights / row_total).astype(jnp.bfloat16)
        context = jnp.einsum(
            "hqk,khd->qhd", probability, value_block, preferred_element_type=jnp.float32
        )
        return (context.reshape(row_count, block_width), (top_score + jnp.log(row_total))[..., 0])

    contexts, log_totals = lax.map(one_block, jnp.arange(block_count))
    return (join_blocks(contexts, row_count, model_width), log_totals)


def attention_backward(queries, keys, values, key_mask, log_totals, context_grad):
    row_count, model_width = queries.shape
    head_dim, group_heads, block_width, block_count = head_blocks(model_width)
    score_scale = head_dim ** (-0.5)

    def one_block(block_index):
        query_block = block_slice(queries, block_index, block_width, group_heads, head_dim)
        key_block = block_slice(keys, block_index, block_width, group_heads, head_dim)
        value_block = block_slice(values, block_index, block_width, group_heads, head_dim)
        grad_block = block_slice(context_grad, block_index, block_width, group_heads, head_dim)
        log_block = lax.dynamic_index_in_dim(log_totals, block_index, 0, keepdims=False)
        scores = masked_scores(query_block, key_block, key_mask, score_scale)
        probability = jnp.exp(scores - log_block[..., None])
        prob_grad = jnp.einsum(
            "qhd,khd->hqk", grad_block, value_block, preferred_element_type=jnp.float32
        )
        value_grad = jnp.einsum(
            "hqk,qhd->khd",
            probability.astype(jnp.bfloat16),
            grad_block,
            preferred_element_type=jnp.float32,
        )
        score_grad = probability * (prob_grad - jnp.sum(probability * prob_grad, -1, keepdims=True))
        score_grad = score_grad.astype(jnp.bfloat16)
        query_grad = (
            jnp.einsum("hqk,khd->qhd", score_grad, key_block, preferred_element_type=jnp.float32)
            * score_scale
        )
        key_grad = (
            jnp.einsum("hqk,qhd->khd", score_grad, query_block, preferred_element_type=jnp.float32)
            * score_scale
        )
        return (
            query_grad.reshape(row_count, block_width),
            key_grad.reshape(row_count, block_width),
            value_grad.reshape(row_count, block_width),
        )

    query_grads, key_grads, value_grads = lax.map(one_block, jnp.arange(block_count))
    return (
        join_blocks(query_grads, row_count, model_width),
        join_blocks(key_grads, row_count, model_width),
        join_blocks(value_grads, row_count, model_width),
    )


def forward_layer(layer_input, weights, key_mask, tables):
    attend_in, attend_out, expand_weight, reduce_weight, vectors = weights
    model_width = layer_input.shape[1]
    pieces = split_vectors(vectors, model_width)
    base_values = layer_input.astype(jnp.float32)
    normed_one = layer_norm(base_values, pieces[0], pieces[1]).astype(jnp.bfloat16)
    mixed = jnp.dot(normed_one, attend_in, preferred_element_type=jnp.float32) + pieces[4]
    queries = rotate(mixed[:, :model_width], tables).astype(jnp.bfloat16)
    keys = rotate(mixed[:, model_width : 2 * model_width], tables).astype(jnp.bfloat16)
    values = mixed[:, 2 * model_width :].astype(jnp.bfloat16)
    context, log_totals = attention_forward(queries, keys, values, key_mask)
    context = context.astype(jnp.bfloat16)
    attended = jnp.dot(context, attend_out, preferred_element_type=jnp.float32) + pieces[5]
    normed_two = layer_norm(base_values, pieces[2], pieces[3]).astype(jnp.bfloat16)
    expanded = jnp.dot(normed_two, expand_weight, preferred_element_type=jnp.float32) + pieces[6]
    activated = gelu_exact(expanded).astype(jnp.bfloat16)
    reduced = (
        lax.dot_general(activated, reduce_weight, COLS_CONTRACT, preferred_element_type=jnp.float32)
        + pieces[7]
    )
    layer_output = (base_values + attended + reduced).astype(jnp.bfloat16)
    stored = (
        normed_one,
        queries,
        keys,
        values,
        context,
        log_totals,
        normed_two,
        expanded,
        activated,
    )
    return (layer_output, stored)


def backward_layer(layer_input, output_grad, weights, stored, key_mask, tables):
    attend_in, attend_out, expand_weight, reduce_weight, vectors = weights
    normed_one, queries, keys, values, context, log_totals, normed_two, expanded, activated = stored
    model_width = layer_input.shape[1]
    pieces = split_vectors(vectors, model_width)
    base_values = layer_input.astype(jnp.float32)
    grad_values = output_grad.astype(jnp.float32)
    bias_sums = jnp.sum(grad_values, 0)
    reduce_grad = lax.dot_general(
        output_grad, activated, ROWS_CONTRACT, preferred_element_type=jnp.float32
    )
    activated_grad = jnp.dot(output_grad, reduce_weight, preferred_element_type=jnp.float32)
    expanded_grad = jax.vjp(gelu_exact, expanded)[1](activated_grad)[0].astype(jnp.bfloat16)
    expand_grad = lax.dot_general(
        normed_two, expanded_grad, ROWS_CONTRACT, preferred_element_type=jnp.float32
    )
    up_bias_grad = jnp.sum(expanded_grad.astype(jnp.float32), 0)
    normed_two_grad = lax.dot_general(
        expanded_grad, expand_weight, COLS_CONTRACT, preferred_element_type=jnp.float32
    )
    attend_out_grad = lax.dot_general(
        context, output_grad, ROWS_CONTRACT, preferred_element_type=jnp.float32
    )
    context_grad = lax.dot_general(
        output_grad, attend_out, COLS_CONTRACT, preferred_element_type=jnp.float32
    ).astype(jnp.bfloat16)
    query_grad, key_grad, value_grad = attention_backward(
        queries, keys, values, key_mask, log_totals, context_grad
    )
    turn_back = jax.vjp(lambda moved: rotate(moved, tables), jnp.zeros_like(query_grad))[1]
    mixed_grad = jnp.concatenate(
        [turn_back(query_grad)[0], turn_back(key_grad)[0], value_grad], 1
    ).astype(jnp.bfloat16)
    attend_in_grad = lax.dot_general(
        normed_one, mixed_grad, ROWS_CONTRACT, preferred_element_type=jnp.float32
    )
    in_bias_grad = jnp.sum(mixed_grad.astype(jnp.float32), 0)
    normed_one_grad = lax.dot_general(
        mixed_grad, attend_in, COLS_CONTRACT, preferred_element_type=jnp.float32
    )
    norm_one_pull = jax.vjp(layer_norm, base_values, pieces[0], pieces[1])[1]
    input_one, gain_one, shift_one = norm_one_pull(normed_one_grad)
    norm_two_pull = jax.vjp(layer_norm, base_values, pieces[2], pieces[3])[1]
    input_two, gain_two, shift_two = norm_two_pull(normed_two_grad)
    layer_grad = grad_values + input_one + input_two
    vector_grad = jnp.concatenate(
        [gain_one, shift_one, gain_two, shift_two, in_bias_grad, bias_sums, up_bias_grad, bias_sums]
    )
    return (layer_grad, (attend_in_grad, attend_out_grad, expand_grad, reduce_grad, vector_grad))


def layer_shards(params, layer_index):
    return (
        params[0][layer_index].astype(jnp.bfloat16),
        params[1][layer_index].astype(jnp.bfloat16),
        params[2][layer_index].astype(jnp.bfloat16),
        params[3][layer_index].astype(jnp.bfloat16),
        params[4][layer_index][None, :].astype(jnp.bfloat16),
    )


def unpack_layer(gathered):
    return (
        gathered[0],
        gathered[1],
        gathered[2],
        gathered[3],
        gathered[4].reshape(-1).astype(jnp.float32),
    )


def adam_update(weight, moment, square, gradient, first_fix, second_fix):
    moment = BETA_FIRST * moment + (1.0 - BETA_FIRST) * gradient
    square = BETA_SECOND * square + (1.0 - BETA_SECOND) * gradient * gradient
    change = -LEARNING * (
        moment / first_fix / (jnp.sqrt(square / second_fix) + ADAM_EPSILON) + DECAY_RATE * weight
    )
    return (change, moment, square)


def per_device(
    tokens,
    cotangent,
    seq_lengths,
    seq_device,
    step_count,
    attend_in,
    attend_out,
    expand_weight,
    reduce_weight,
    layer_vectors,
    attend_in_mean,
    attend_out_mean,
    expand_mean,
    reduce_mean,
    vectors_mean,
    attend_in_square,
    attend_out_square,
    expand_square,
    reduce_square,
    vectors_square,
):
    device_count = lax.axis_size(("dp", "fsdp"))
    device_index = lax.axis_index(("dp", "fsdp"))
    row_count = tokens.shape[0]
    model_width = tokens.shape[1]
    head_dim = model_width // HEADS
    length = jnp.sum(jnp.where(seq_device == device_index, seq_lengths, 0))
    row_ids = jnp.arange(row_count, dtype=jnp.int32)
    key_mask = (row_ids[None, :] <= row_ids[:, None]) & (row_ids[None, :] < length)
    valid_rows = (row_ids < length).astype(jnp.float32)[:, None]
    tables = rotary_tables(row_count, model_width, head_dim)
    params = (attend_in, attend_out, expand_weight, reduce_weight, layer_vectors)
    stored_list = []
    layer_inputs = []
    layer_outputs = []
    current = tokens
    for layer_index in range(LAYERS):
        pieces = layer_shards(params, layer_index)
        gathered = (
            lax.all_gather(pieces[0], ("dp", "fsdp"), axis=0, tiled=True),
            lax.all_gather(pieces[1], ("dp", "fsdp"), axis=0, tiled=True),
            lax.all_gather(pieces[2], ("dp", "fsdp"), axis=0, tiled=True),
            lax.all_gather(pieces[3], ("dp", "fsdp"), axis=0, tiled=True),
            lax.all_gather(pieces[4], ("dp", "fsdp"), axis=0, tiled=True),
        )
        weights = unpack_layer(gathered)
        layer_inputs.append(current)
        current, stored = forward_layer(current, weights, key_mask, tables)
        stored_list.append(stored)
        layer_outputs.append(current)
    grad_rows = (cotangent.astype(jnp.float32) * valid_rows).astype(jnp.bfloat16)
    shard_lists = [None] * LAYERS
    for layer_index in reversed(range(LAYERS)):
        pieces = layer_shards(params, layer_index)
        gathered = (
            lax.all_gather(pieces[0], ("dp", "fsdp"), axis=0, tiled=True),
            lax.all_gather(pieces[1], ("dp", "fsdp"), axis=0, tiled=True),
            lax.all_gather(pieces[2], ("dp", "fsdp"), axis=0, tiled=True),
            lax.all_gather(pieces[3], ("dp", "fsdp"), axis=0, tiled=True),
            lax.all_gather(pieces[4], ("dp", "fsdp"), axis=0, tiled=True),
        )
        weights = unpack_layer(gathered)
        layer_grad, layer_params_grad = backward_layer(
            layer_inputs[layer_index],
            grad_rows,
            weights,
            stored_list[layer_index],
            key_mask,
            tables,
        )
        grad_rows = layer_grad.astype(jnp.bfloat16)
        grad_tuple = (
            layer_params_grad[0],
            layer_params_grad[1],
            layer_params_grad[2],
            layer_params_grad[3],
            layer_params_grad[4].reshape(device_count, -1),
        )
        summed = (
            lax.psum_scatter(grad_tuple[0], ("dp", "fsdp"), scatter_dimension=0, tiled=True),
            lax.psum_scatter(grad_tuple[1], ("dp", "fsdp"), scatter_dimension=0, tiled=True),
            lax.psum_scatter(grad_tuple[2], ("dp", "fsdp"), scatter_dimension=0, tiled=True),
            lax.psum_scatter(grad_tuple[3], ("dp", "fsdp"), scatter_dimension=0, tiled=True),
            lax.psum_scatter(grad_tuple[4], ("dp", "fsdp"), scatter_dimension=0, tiled=True),
        )
        shard_lists[layer_index] = (
            summed[0],
            summed[1],
            summed[2],
            summed[3],
            summed[4].reshape(-1),
        )
    grad_stack = [
        jnp.stack([shard_lists[layer_index][param_index] for layer_index in range(LAYERS)])
        for param_index in range(5)
    ]
    step_float = step_count[0].astype(jnp.float32)
    first_fix = 1.0 - jnp.power(BETA_FIRST, step_float)
    second_fix = 1.0 - jnp.power(BETA_SECOND, step_float)
    moments = (attend_in_mean, attend_out_mean, expand_mean, reduce_mean, vectors_mean)
    squares = (attend_in_square, attend_out_square, expand_square, reduce_square, vectors_square)
    updated = [
        adam_update(
            params[param_index],
            moments[param_index],
            squares[param_index],
            grad_stack[param_index],
            first_fix,
            second_fix,
        )
        for param_index in range(5)
    ]
    return (
        jnp.stack(layer_outputs),
        grad_rows,
        grad_stack[0],
        grad_stack[1],
        grad_stack[2],
        grad_stack[3],
        grad_stack[4],
        updated[0][0],
        updated[1][0],
        updated[2][0],
        updated[3][0],
        updated[4][0],
        updated[0][1],
        updated[1][1],
        updated[2][1],
        updated[3][1],
        updated[4][1],
        updated[0][2],
        updated[1][2],
        updated[2][2],
        updated[3][2],
        updated[4][2],
    )


def solution(mesh):
    placed = (
        P(("dp", "fsdp"), None),
        P(("dp", "fsdp"), None),
        P(),
        P(),
        P(),
        P(None, ("dp", "fsdp"), None),
        P(None, ("dp", "fsdp"), None),
        P(None, ("dp", "fsdp"), None),
        P(None, ("dp", "fsdp"), None),
        P(None, ("dp", "fsdp")),
        P(None, ("dp", "fsdp"), None),
        P(None, ("dp", "fsdp"), None),
        P(None, ("dp", "fsdp"), None),
        P(None, ("dp", "fsdp"), None),
        P(None, ("dp", "fsdp")),
        P(None, ("dp", "fsdp"), None),
        P(None, ("dp", "fsdp"), None),
        P(None, ("dp", "fsdp"), None),
        P(None, ("dp", "fsdp"), None),
        P(None, ("dp", "fsdp")),
    )
    return jax.shard_map(
        per_device,
        mesh=mesh,
        in_specs=placed,
        out_specs=(
            P(None, ("dp", "fsdp"), None),
            P(("dp", "fsdp"), None),
            P(None, ("dp", "fsdp"), None),
            P(None, ("dp", "fsdp"), None),
            P(None, ("dp", "fsdp"), None),
            P(None, ("dp", "fsdp"), None),
            P(None, ("dp", "fsdp")),
            P(None, ("dp", "fsdp"), None),
            P(None, ("dp", "fsdp"), None),
            P(None, ("dp", "fsdp"), None),
            P(None, ("dp", "fsdp"), None),
            P(None, ("dp", "fsdp")),
            P(None, ("dp", "fsdp"), None),
            P(None, ("dp", "fsdp"), None),
            P(None, ("dp", "fsdp"), None),
            P(None, ("dp", "fsdp"), None),
            P(None, ("dp", "fsdp")),
            P(None, ("dp", "fsdp"), None),
            P(None, ("dp", "fsdp"), None),
            P(None, ("dp", "fsdp"), None),
            P(None, ("dp", "fsdp"), None),
            P(None, ("dp", "fsdp")),
        ),
        check_vma=False,
    )
```

profile of v0, /device:TPU:1, one launch (start us, length us, event | category | flops | bytes accessed | tf_op | source)
XLA Modules:
  0.0 2904.6 jit_solution(2383356137137703529)
XLA Ops:
  17.0 65.0 %all-gather.8 = bf16[32,1,416]{2,1,0:T(2,128)(2,1)S(1)} all-gather(bf16[1,1,416]{2,1,0:T(2,128)(2,1)S(1)} %get-tuple-element.609), channel_id=1, replica_groups=mesh['dp'=8,'fsdp'=4] {'dp','fsdp'}, dimensions={0}, use_global_device_ids=true | all-gather | bytes 27456 | tf_op jit(solution)/shard_map/all_gather | solution.py:319
  83.0 64.6 %all-gather.9 = bf16[32,1,416]{2,1,0:T(2,128)(2,1)S(1)} all-gather(bf16[1,1,416]{2,1,0:T(2,128)(2,1)S(1)} %get-tuple-element.610), channel_id=1, replica_groups=mesh['dp'=8,'fsdp'=4] {'dp','fsdp'}, dimensions={0}, use_global_device_ids=true | all-gather | bytes 27456 | tf_op jit(solution)/shard_map/all_gather | solution.py:319
  150.9 3.2 fusion.139
  154.1 4.7 fusion.74
  160.7 5.2 fusion.174
  166.4 2.0 copy.78
  168.4 23.1 while.56
  191.6 30.2 %all-gather.23.cloned.1.call-done = bf16[1,1024,4096]{2,1,0:T(8,128)(2,1)} async-done(((bf16[1,32,4096]{2,1,0:T(8,128)(2,1)}), bf16[1,1024,4096]{2,1,0:T(8,128)(2,1)}) %all-gather.23.cloned.1.call-update) | async-done | bytes 8388624 | tf_op jit(solution)/shard_map/all_gather | solution.py:317
  221.8 16.2 multiply_convert_fusion.3
  238.0 62.8 %all-gather.25.cloned.1.call-done = bf16[1,1024,4096]{2,1,0:T(8,128)(2,1)} async-done(((bf16[1,32,4096]{2,1,0:T(8,128)(2,1)}), bf16[1,1024,4096]{2,1,0:T(8,128)(2,1)}) %all-gather.25.cloned.1.call-update) | async-done | bytes 8388624 | tf_op jit(solution)/shard_map/all_gather | solution.py:318
  300.8 7.4 fusion.124
  308.2 50.8 %all-gather.21.cloned.1.call-done = bf16[1,1024,1024]{2,1,0:T(8,128)(2,1)} async-done(((bf16[1,32,1024]{2,1,0:T(8,128)(2,1)}), bf16[1,1024,1024]{2,1,0:T(8,128)(2,1)}) %all-gather.21.cloned.1.call-update) | async-done | bytes 2097168 | tf_op jit(solution)/shard_map/all_gather | solution.py:316
  359.0 2.7 convert_reduce_fusion.4
  362.0 68.5 %all-gather.27.cloned.1.call-done = bf16[1,1024,3072]{2,1,0:T(8,128)(2,1)} async-done(((bf16[1,32,3072]{2,1,0:T(8,128)(2,1)}), bf16[1,1024,3072]{2,1,0:T(8,128)(2,1)}) %all-gather.27.cloned.1.call-update) | async-done | bytes 6291472 | tf_op jit(solution)/shard_map/all_gather | solution.py:315
  430.5 4.7 fusion.77
  437.1 5.2 fusion.170
  444.3 2.0 copy.81
  446.4 30.0 %while.57 = (s32[]{:T(128)}, bf16[8,256,128]{1,2,0:T(8,128)(2,1)S(1)}, f32[8,2,256]{2,1,0:T(2,128)S(1)}, s32[8]{0:T(128)S(1)}, bf16[256,1024]{0,1:T(8,128)(2,1)}...) while((s32[]{:T(128)}, ...), condition=%wide.region_12.13_spmd.clone, body=%wide.region_9.12_spmd.clone.sunk | while | flops 34733572 | bytes 2507199 | solution.py:110
  478.6 71.0 %while.58 = (s32[]{:T(128)}, f32[8,256,128]{1,2,0:T(8,128)}, f32[8,256,128]{1,2,0:T(8,128)}, bf16[8,256,128]{1,2,0:T(8,128)(2,1)S(1)}, s32[8]{0:T(128)S(1)}, /*i...) while((s32[]{:T(128)}, f32[8,256,128]{1,2,0:T(8,128)}, ...), condition=%wide.region_15.16_spmd.clone, body=%wide.region_13.15_spmd.clone.sunk | while | flops 85261824 | bytes 6171657 | solution.py:152
  549.6 2.5 copy.106
  552.2 2.5 copy.107
  554.7 5.0 select_select_fusion.3
  559.8 1.6 split.68
  561.4 1.3 split.72
  565.2 6.1 add_convert_fusion.5
  571.4 16.4 multiply_convert_fusion.2
  588.9 10.3 convert_reduce_fusion
  599.2 2.4 fusion.32
  601.7 5.5 fusion.228
  607.1 1.4 fusion.154
  610.2 1.5 fusion.136
  612.9 70.6 %while.59 = (s32[]{:T(128)}, f32[8,256,128]{1,2,0:T(8,128)S(1)}, f32[8,256,128]{1,2,0:T(8,128)}, bf16[8,256,128]{1,2,0:T(8,128)(2,1)S(1)}, s32[8]{0:T(128)S(1)},...) while((s32[]{:T(128)}, f32[8,256,128]{1,2,0:T(8,128)S(1)}, ...), condition=%wide.region_22.23_spmd.clone, body=%wide.region_20.22_spmd.clone.sunk | while | flops 85261824 | bytes 6171657 | solution.py:152
  684.5 1.6 copy.109
  686.1 2.5 copy.110
  688.6 5.0 select_select_fusion.1
  693.7 1.7 split.76
  695.3 1.3 split.80
  699.4 6.7 add_convert_fusion.3
  706.4 9.3 convert_reduce_fusion.1
  715.9 2.4 fusion.40
  718.4 2.1 fusion.226
  723.2 2.7 fusion.252
  727.1 2.8 fusion.224
  730.6 7.8 fusion.210
  739.4 7.8 fusion.216
  747.3 9.9 fusion.213
  757.9 9.9 fusion.207
  767.8 9.8 fusion.253
  777.9 9.8 fusion.223
  788.5 6.6 fusion.127
  797.1 1.5 fusion.148
  798.6 46.9 %all-reduce.21.cloned.1.call-done = (f32[32,416]{1,0:T(8,128)}, f32[32,416]{1,0:T(8,128)}) async-done(((f32[32,416]{1,0:T(8,128)}, f32[32,416]{1,0:T(8,128)}), (f32[32,416]{1,0:T(8,128)}, f32[32,416]{1,0:T(8,128)})) %all-reduce.21.cloned.1.call-update) | async-done | bytes 106512
  847.6 139.1 %reduce-scatter.13.cloned.1.call-done = f32[32,1024]{1,0:T(8,128)} async-done(((f32[1024,1024]{1,0:T(8,128)}), f32[32,1024]{1,0:T(8,128)}) %reduce-scatter.13.cloned.1.call-update) | async-done | bytes 131088 | tf_op jit(solution)/shard_map/reduce_scatter | solution.py:356
  986.7 143.2 %reduce-scatter.15.cloned.1.call-done = f32[32,1024]{1,0:T(8,128)} async-done(((f32[1024,1024]{1,0:T(8,128)}), f32[32,1024]{1,0:T(8,128)}) %reduce-scatter.15.cloned.1.call-update) | async-done | bytes 131088 | tf_op jit(solution)/shard_map/reduce_scatter | solution.py:356
  1129.9 2.2 add_multiply_fusion.3
  1132.1 157.6 %reduce-scatter.9.cloned.1.call-done = f32[32,3072]{1,0:T(8,128)} async-done(((f32[1024,3072]{1,0:T(8,128)}), f32[32,3072]{1,0:T(8,128)}) %reduce-scatter.9.cloned.1.call-update) | async-done | bytes 393232 | tf_op jit(solution)/shard_map/reduce_scatter | solution.py:355
  1289.7 159.8 %reduce-scatter.11.cloned.1.call-done = f32[32,3072]{1,0:T(8,128)} async-done(((f32[1024,3072]{1,0:T(8,128)}), f32[32,3072]{1,0:T(8,128)}) %reduce-scatter.11.cloned.1.call-update) | async-done | bytes 393232 | tf_op jit(solution)/shard_map/reduce_scatter | solution.py:355
  1449.6 3.5 add_multiply_fusion.2
  1453.0 357.2 %reduce-scatter.19.cloned.1.call-done = f32[32,4096]{1,0:T(8,128)} async-done(((f32[1024,4096]{1,0:T(8,128)}), f32[32,4096]{1,0:T(8,128)}) %reduce-scatter.19.cloned.1.call-update) | async-done | bytes 524304 | tf_op jit(solution)/shard_map/reduce_scatter | solution.py:357
  1810.2 361.2 %reduce-scatter.17.cloned.1.call-done = f32[32,4096]{1,0:T(8,128)} async-done(((f32[1024,4096]{1,0:T(8,128)}), f32[32,4096]{1,0:T(8,128)}) %reduce-scatter.17.cloned.1.call-update) | async-done | bytes 524304 | tf_op jit(solution)/shard_map/reduce_scatter | solution.py:357
  2171.4 4.3 add_multiply_fusion.1
  2175.7 356.9 %reduce-scatter.21.cloned.1.call-done = f32[32,4096]{1,0:T(8,128)} async-done(((f32[1024,4096]{1,0:T(8,128)}), f32[32,4096]{1,0:T(8,128)}) %reduce-scatter.21.cloned.1.call-update) | async-done | bytes 524304 | tf_op jit(solution)/shard_map/reduce_scatter | solution.py:358
  2532.7 361.2 %reduce-scatter.23.cloned.1.call-done = f32[32,4096]{1,0:T(8,128)} async-done(((f32[1024,4096]{1,0:T(8,128)}), f32[32,4096]{1,0:T(8,128)}) %reduce-scatter.23.cloned.1.call-update) | async-done | bytes 524304 | tf_op jit(solution)/shard_map/reduce_scatter | solution.py:358
  2893.8 3.8 add_multiply_fusion
  (719 shorter events, 184.3 us)
Async XLA Ops:
  7.2 143.7 %all-gather.29.cloned.1.call-start = ((), (), s32[]{:S(2)}) async-start(), calls=%async_computation.21 | async-start | bytes 2162688 | tf_op jit(solution)/shard_map/all_gather | solution.py:316
  9.0 145.1 %all-gather.19.cloned.1.call-start = ((), (), s32[]{:S(2)}) async-start(), calls=%async_computation.16 | async-start | bytes 6488064 | tf_op jit(solution)/shard_map/all_gather | solution.py:315
  11.0 210.7 %all-gather.23.cloned.1.call-start = ((), (), s32[]{:S(2)}) async-start(), calls=%async_computation.18 | async-start | bytes 8650752 | tf_op jit(solution)/shard_map/all_gather | solution.py:317
  12.4 136.1 %copy-start.82 = (s32[32]{0:T(128)S(1)}, s32[32]{0:T(128)}, u32[]{:S(2)}) copy-start(s32[32]{0:T(128)} %param.30) | copy-start | bytes 388
  12.4 136.1 %copy-start.83 = (s32[32]{0:T(128)S(1)}, s32[32]{0:T(128)}, u32[]{:S(2)}) copy-start(s32[32]{0:T(128)} %param.31) | copy-start | bytes 388
  13.2 137.2 %copy-start = (bf16[256,1024]{1,0:T(8,128)(2,1)S(1)}, bf16[256,1024]{1,0:T(8,128)(2,1)}, u32[]{:S(2)}) copy-start(bf16[256,1024]{1,0:T(8,128)(2,1)} %param.28) | copy-start | bytes 1572868
  13.2 287.6 %all-gather.25.cloned.1.call-start = ((), (), s32[]{:S(2)}) async-start(), calls=%async_computation.19 | async-start | bytes 8650752 | tf_op jit(solution)/shard_map/all_gather | solution.py:318
  13.4 137.6 %copy-start.12 = (bf16[256,1024]{1,0:T(8,128)(2,1)S(1)}, bf16[256,1024]{1,0:T(8,128)(2,1)}, u32[]{:S(2)}) copy-start(bf16[256,1024]{1,0:T(8,128)(2,1)} %param.29) | copy-start | bytes 1572868
  14.2 344.7 %all-gather.21.cloned.1.call-start = ((), (), s32[]{:S(2)}) async-start(), calls=%async_computation.17 | async-start | bytes 2162688 | tf_op jit(solution)/shard_map/all_gather | solution.py:316
  14.8 415.6 %all-gather.27.cloned.1.call-start = ((), (), s32[]{:S(2)}) async-start(), calls=%async_computation.20 | async-start | bytes 6488064 | tf_op jit(solution)/shard_map/all_gather | solution.py:315
  15.4 556.0 %all-gather.31.cloned.1.call-start = ((), (), s32[]{:S(2)}) async-start(), calls=%async_computation.22 | async-start | bytes 8650752 | tf_op jit(solution)/shard_map/all_gather | solution.py:317
  16.1 572.8 %all-gather.33.cloned.1.call-start = ((), (), s32[]{:S(2)}) async-start(), calls=%async_computation.23 | async-start | bytes 8650752 | tf_op jit(solution)/shard_map/all_gather | solution.py:318
  16.9 828.6 %all-reduce.21.cloned.1.call-start = ((), (), s32[]{:S(2)}) async-start(), calls=%async_computation.24 | async-start | bytes 262144
  82.8 71.3 %copy-start.46 = (f32[1024]{0:T(1024)}, f32[1024]{0:T(1024)S(1)}, u32[]{:S(2)}) copy-start(f32[1024]{0:T(1024)S(1)} %get-tuple-element.600) | copy-start | bytes 12292
  82.8 71.3 %copy-start.48 = (f32[1024]{0:T(1024)}, f32[1024]{0:T(1024)S(1)}, u32[]{:S(2)}) copy-start(f32[1024]{0:T(1024)S(1)} %get-tuple-element.599) | copy-start | bytes 12292
  82.8 138.9 %copy-start.53 = (f32[1024]{0:T(1024)}, f32[1024]{0:T(1024)S(1)}, u32[]{:S(2)}) copy-start(f32[1024]{0:T(1024)S(1)} %get-tuple-element.597) | copy-start | bytes 12292
  82.9 77.9 %copy-start.60 = (pred[1024]{0:T(1024)(128)(4,1)}, pred[1024]{0:T(1024)(128)(4,1)S(1)}, u32[]{:S(2)}) copy-start(pred[1024]{0:T(1024)(128)(4,1)S(1)} %get-tuple-element.622) | copy-start | bytes 3076
  82.9 77.8 %copy-start.66 = (pred[1024]{0:T(1024)(128)(4,1)}, pred[1024]{0:T(1024)(128)(4,1)S(1)}, u32[]{:S(2)}) copy-start(pred[1024]{0:T(1024)(128)(4,1)S(1)} %get-tuple-element.621) | copy-start | bytes 3076
  82.9 75.9 %copy-start.1 = (bf16[8,256,128]{1,2,0:T(8,128)(2,1)}, bf16[8,256,128]{1,2,0:T(8,128)(2,1)S(1)}, u32[]{:S(2)}) copy-start(bf16[8,256,128]{1,2,0:T(8,128)(2,1)S(1)} %fusion.243) | copy-start | bytes 1572868
  147.8 11.0 copy-start.51
  150.4 8.5 copy-start.64
  150.6 71.2 %copy-start.56 = (f32[256]{0:T(256)}, f32[256]{0:T(256)S(1)}, u32[]{:S(2)}) copy-start(f32[256]{0:T(256)S(1)} %broadcast_multiply_fusion.1) | copy-start | bytes 3076
  150.9 70.9 %copy-start.58 = (f32[256]{0:T(256)}, f32[256]{0:T(256)S(1)}, u32[]{:S(2)}) copy-start(f32[256]{0:T(256)S(1)} %fusion.203) | copy-start | bytes 3076
  168.4 53.3 %slice-start.2 = ((f32[13312]{0:T(1024)}), f32[4096]{0:T(1024)S(1)}, s32[]{:S(2)}) async-start(f32[13312]{0:T(1024)} %copy-done.52), calls=%async_computation.27 | async-start | bytes 32768 | tf_op jit(solution)/shard_map/slice | solution.py:41
  191.6 46.5 %copy-start.38 = (bf16[256,1024]{0,1:T(8,128)(2,1)}, bf16[256,1024]{0,1:T(8,128)(2,1)S(1)}, u32[]{:S(2)}) copy-start(bf16[256,1024]{0,1:T(8,128)(2,1)S(1)} %get-tuple-element.1091) | copy-start | bytes 1572868
  191.6 46.5 %copy-start.39 = (bf16[256,1024]{0,1:T(8,128)(2,1)}, bf16[256,1024]{0,1:T(8,128)(2,1)S(1)}, u32[]{:S(2)}) copy-start(bf16[256,1024]{0,1:T(8,128)(2,1)S(1)} %get-tuple-element.1092) | copy-start | bytes 1572868
  191.6 167.4 %copy-start.3 = (bf16[8,256,128]{1,2,0:T(8,128)(2,1)}, bf16[8,256,128]{1,2,0:T(8,128)(2,1)S(1)}, u32[]{:S(2)}) copy-start(bf16[8,256,128]{1,2,0:T(8,128)(2,1)S(1)} %get-tuple-element.226) | copy-start | bytes 1572868
  221.8 79.0 %copy-start.79 = (f32[1024]{0:T(1024)S(1)}, f32[1024]{0:T(1024)}, u32[]{:S(2)}) copy-start(f32[1024]{0:T(1024)} %get-tuple-element.596) | copy-start | bytes 12292
  300.8 58.2 %copy-start.63 = (f32[1024]{0:T(1024)S(1)}, f32[1024]{0:T(1024)}, u32[]{:S(2)}) copy-start(f32[1024]{0:T(1024)} %get-tuple-element.595) | copy-start | bytes 12292
  308.2 122.3 %slice-start = ((f32[13312]{0:T(1024)}), f32[3072]{0:T(1024)S(1)}, s32[]{:S(2)}) async-start(f32[13312]{0:T(1024)} %copy-done.51), calls=%async_computation.25 | async-start | bytes 24576 | tf_op jit(solution)/shard_map/slice | solution.py:39
  362.0 73.2 %copy-start.74 = (f32[256]{0:T(256)}, f32[256]{0:T(256)S(1)}, u32[]{:S(2)}) copy-start(f32[256]{0:T(256)S(1)} %fusion.164) | copy-start | bytes 3076
  437.1 9.3 copy-start.8
  446.3 32.2 %copy-start.9 = (bf16[8,256,128]{1,2,0:T(8,128)(2,1)S(1)}, bf16[8,256,128]{1,2,0:T(8,128)(2,1)}, u32[]{:S(2)}) copy-start(bf16[8,256,128]{1,2,0:T(8,128)(2,1)} %copy-done.1) | copy-start | bytes 1572868
  565.1 36.5 %copy-start.18 = (bf16[256,1024]{1,0:T(8,128)(2,1)}, bf16[256,1024]{1,0:T(8,128)(2,1)S(1)}, u32[]{:S(2)}) copy-start(bf16[256,1024]{1,0:T(8,128)(2,1)S(1)} %copy.108) | copy-start | bytes 1572868
  571.3 30.3 %copy-start.23 = (bf16[256,1024]{1,0:T(8,128)(2,1)}, bf16[256,1024]{1,0:T(8,128)(2,1)S(1)}, u32[]{:S(2)}) copy-start(bf16[256,1024]{1,0:T(8,128)(2,1)S(1)} %get-tuple-element.607) | copy-start | bytes 1572868
  571.3 30.3 %copy-start.25 = (bf16[256,1024]{1,0:T(8,128)(2,1)}, bf16[256,1024]{1,0:T(8,128)(2,1)S(1)}, u32[]{:S(2)}) copy-start(bf16[256,1024]{1,0:T(8,128)(2,1)S(1)} %get-tuple-element.608) | copy-start | bytes 1572868
  571.4 17.5 copy-start.65
  588.9 10.3 copy-start.84
  688.6 8.7 copy-start.19
  688.6 8.7 copy-start.24
  688.6 8.7 copy-start.26
  699.3 16.4 slice-start.3
  699.4 18.9 slice-start.5
  706.1 12.1 copy-start.27
  706.1 12.1 copy-start.28
  706.4 9.4 slice-start.4
  706.4 11.8 slice-start.6
  723.1 263.6 %reduce-scatter.13.cloned.1.call-start = ((), (), s32[]{:S(2)}) async-start(), calls=%async_computation.10 | async-start | bytes 4325376 | tf_op jit(solution)/shard_map/reduce_scatter | solution.py:356
  725.9 404.0 %reduce-scatter.15.cloned.1.call-start = ((), (), s32[]{:S(2)}) async-start(), calls=%async_computation.11 | async-start | bytes 4325376 | tf_op jit(solution)/shard_map/reduce_scatter | solution.py:356
  729.9 559.8 %reduce-scatter.9.cloned.1.call-start = ((), (), s32[]{:S(2)}) async-start(), calls=%async_computation.8 | async-start | bytes 12976128 | tf_op jit(solution)/shard_map/reduce_scatter | solution.py:355
  738.4 711.1 %reduce-scatter.11.cloned.1.call-start = ((), (), s32[]{:S(2)}) async-start(), calls=%async_computation.9 | async-start | bytes 12976128 | tf_op jit(solution)/shard_map/reduce_scatter | solution.py:355
  747.2 1063.0 %reduce-scatter.19.cloned.1.call-start = ((), (), s32[]{:S(2)}) async-start(), calls=%async_computation.13 | async-start | bytes 17301504 | tf_op jit(solution)/shard_map/reduce_scatter | solution.py:357
  757.2 1414.2 %reduce-scatter.17.cloned.1.call-start = ((), (), s32[]{:S(2)}) async-start(), calls=%async_computation.12 | async-start | bytes 17301504 | tf_op jit(solution)/shard_map/reduce_scatter | solution.py:357
  767.8 1764.9 %reduce-scatter.21.cloned.1.call-start = ((), (), s32[]{:S(2)}) async-start(), calls=%async_computation.14 | async-start | bytes 17301504 | tf_op jit(solution)/shard_map/reduce_scatter | solution.py:358
  777.6 2116.2 %reduce-scatter.23.cloned.1.call-start = ((), (), s32[]{:S(2)}) async-start(), calls=%async_computation.15 | async-start | bytes 17301504 | tf_op jit(solution)/shard_map/reduce_scatter | solution.py:358
  795.2 51.8 %copy-start.70 = (f32[2,416]{1,0:T(2,128)S(1)}, f32[2,416]{1,0:T(2,128)}, u32[]{:S(2)}) copy-start(f32[2,416]{1,0:T(2,128)} %param.37) | copy-start | bytes 9988
  795.2 51.8 %copy-start.76 = (f32[2,416]{1,0:T(2,128)S(1)}, f32[2,416]{1,0:T(2,128)}, u32[]{:S(2)}) copy-start(f32[2,416]{1,0:T(2,128)} %param.47) | copy-start | bytes 9988
  795.2 51.8 %copy-start.77 = (f32[2,416]{1,0:T(2,128)S(1)}, f32[2,416]{1,0:T(2,128)}, u32[]{:S(2)}) copy-start(f32[2,416]{1,0:T(2,128)} %param.42) | copy-start | bytes 9988
  795.2 334.7 %copy-start.45 = (f32[2,32,1024]{2,1,0:T(8,128)S(1)}, f32[2,32,1024]{2,1,0:T(8,128)}, u32[]{:S(2)}) copy-start(f32[2,32,1024]{2,1,0:T(8,128)} %param.34) | copy-start | bytes 786436
  795.2 334.7 %copy-start.50 = (f32[2,32,1024]{2,1,0:T(8,128)S(1)}, f32[2,32,1024]{2,1,0:T(8,128)}, u32[]{:S(2)}) copy-start(f32[2,32,1024]{2,1,0:T(8,128)} %param.44) | copy-start | bytes 786436
  796.0 653.6 %copy-start.37 = (f32[2,32,3072]{2,1,0:T(8,128)S(1)}, f32[2,32,3072]{2,1,0:T(8,128)}, u32[]{:S(2)}) copy-start(f32[2,32,3072]{2,1,0:T(8,128)} %param.33) | copy-start | bytes 2359300
  1129.9 1041.5 %copy-start.29 = (f32[2,32,4096]{2,1,0:T(8,128)S(1)}, f32[2,32,4096]{2,1,0:T(8,128)}, u32[]{:S(2)}) copy-start(f32[2,32,4096]{2,1,0:T(8,128)} %param.35) | copy-start | bytes 3145732
  2171.4 722.4 %copy-start.31 = (f32[2,32,4096]{2,1,0:T(8,128)S(1)}, f32[2,32,4096]{2,1,0:T(8,128)}, u32[]{:S(2)}) copy-start(f32[2,32,4096]{2,1,0:T(8,128)} %param.36) | copy-start | bytes 3145732
  2171.4 722.4 %copy-start.44 = (f32[2,32,4096]{2,1,0:T(8,128)S(1)}, f32[2,32,4096]{2,1,0:T(8,128)}, u32[]{:S(2)}) copy-start(f32[2,32,4096]{2,1,0:T(8,128)} %param.46) | copy-start | bytes 3145732
  (45 other events, 157.2 us)
Sparse Core Ops, SparseCore 0:
  11.5 58.8 all-gather.28
  73.8 68.5 all-gather.18
  145.9 75.8 all-gather.22
  225.1 75.6 all-gather.24
  304.1 54.8 all-gather.20
  362.3 68.1 all-gather.26
  433.9 75.7 all-gather.30
  513.1 75.7 all-gather.32
  723.2 122.2 all-reduce.20
  847.6 139.0 reduce-scatter.12
  989.0 140.9 reduce-scatter.14
  1135.8 153.8 reduce-scatter.8
  1295.7 153.7 reduce-scatter.10
  1451.7 358.4 reduce-scatter.18
  1812.4 359.0 reduce-scatter.16
  2173.6 359.0 reduce-scatter.20
  2534.8 358.9 reduce-scatter.22
where the time goes:
time: 2920 us; the launch traced here: 2900 us
  waiting for transfers between devices  2300 us (79%)
  matrix products  184 us (6%)
  local copies, waits for them, and re-layouts  153 us (5%)
  blocking collectives  130 us (4%)
  other arithmetic  66.9 us (2%)
  loops' own time  53.8 us (2%)
    reduce_scatter x2, waiting for transfers between devices, per_device(): lax.psum_scatter(grad_tuple[2], ('dp', 'fsdp'), scatter_dimension=0, tile...  718 us
    reduce_scatter x2, waiting for transfers between devices, per_device(): lax.psum_scatter(grad_tuple[3], ('dp', 'fsdp'), scatter_dimension=0, tile...  718 us
    reduce_scatter x2, waiting for transfers between devices, per_device(): lax.psum_scatter(grad_tuple[0], ('dp', 'fsdp'), scatter_dimension=0, tile...  317 us
    reduce_scatter x2, waiting for transfers between devices, per_device(): lax.psum_scatter(grad_tuple[1], ('dp', 'fsdp'), scatter_dimension=0, tile...  282 us
    all_gather x2, blocking collectives, per_device(): lax.all_gather(pieces[4], ('dp', 'fsdp'), axis=0, tiled=True)  130 us
    dynamic_slice x112, local copies, waits for them, and re-layouts, block_slice(): lax.dynamic_slice_in_dim(matrix, block_index * block_width, block_width, 1)  77 us
    all_gather x2, waiting for transfers between devices, per_device(): lax.all_gather(pieces[0], ('dp', 'fsdp'), axis=0, tiled=True)  68.5 us
    all_gather x2, waiting for transfers between devices, per_device(): lax.all_gather(pieces[3], ('dp', 'fsdp'), axis=0, tiled=True)  63.9 us
  transfers between devices with their start and end apart: 17, of which 14 were waited for; matrix products, arithmetic and copies ran while one was open for 10% of the time, Pallas kernels for 0%

commit v1 on v0

v1 whole, which is shorter than its diff:
```python
import functools

import jax
import jax.numpy as jnp
from jax import lax
from jax.experimental import pallas as pl
from jax.experimental.pallas import tpu as pltpu
from jax.sharding import Mesh
from jax.sharding import PartitionSpec as P

HEADS = 16
LAYERS = 2
NORM_EPSILON = 1e-05
ADAM_EPSILON = 1e-08
LEARNING = 0.02
BETA_FIRST = 0.9
BETA_SECOND = 0.95
DECAY_RATE = 0.1
MASKED_SCORE = -1e30

TP = 8
HALF = TP // 2
BF = jnp.bfloat16
F32 = jnp.float32
MESH = pl.DeviceIdType.MESH
NT = (((1,), (1,)), ((), ()))
TN = (((0,), (0,)), ((), ()))
ANY = pl.BlockSpec(memory_space=pl.ANY)
VMEM = pl.BlockSpec(memory_space=pltpu.VMEM)
SMEM = pl.BlockSpec(memory_space=pltpu.SMEM)
VMEM_BYTES = 60 * 1024 * 1024


def place():
    return lax.axis_index("grp"), lax.axis_index("tp")


def nn_dot(a, b):
    return jnp.dot(a, b, preferred_element_type=F32)


def nt_dot(a, b):
    return lax.dot_general(a, b, NT, preferred_element_type=F32)


def tn_dot(a, b):
    return lax.dot_general(a, b, TN, preferred_element_type=F32)


def remote(src, dst, send, recv, target):
    return pltpu.make_async_remote_copy(
        src_ref=src, dst_ref=dst, send_sem=send, recv_sem=recv, device_id=target, device_id_type=MESH
    )


def greet(targets):
    barrier = pltpu.get_barrier_semaphore()
    for target in targets:
        pl.semaphore_signal(barrier, inc=1, device_id=target, device_id_type=MESH)
    pl.semaphore_wait(barrier, len(targets))


def greet_all(groups):
    grp, tp = place()
    me = grp * TP + tp
    total = groups * TP
    barrier = pltpu.get_barrier_semaphore()

    def signal(step, carry):
        other = lax.rem(me + step, total)
        pl.semaphore_signal(
            barrier, inc=1, device_id=(other // TP, lax.rem(other, TP)), device_id_type=MESH
        )
        return carry

    lax.fori_loop(1, total, signal, 0)
    pl.semaphore_wait(barrier, total - 1)


def spread_kernel(groups, owners, xh, s0, s1, wo, vec, xg, w0, w1, wog, vecg,
                  xs, xr, ss, sr, ts, tr, os, orr, vs, vr, loc):
    grp, tp = place()
    me = grp * TP + tp
    total = groups * TP
    core, chip = tp // HALF, lax.rem(tp, HALF)
    partner = lax.rem(tp + HALF, TP)
    greet_all(groups)
    own = [
        pltpu.make_async_copy(xh, xg.at[tp], loc.at[0]),
        pltpu.make_async_copy(s0.at[tp], w0.at[me], loc.at[1]),
        pltpu.make_async_copy(s1.at[tp], w1.at[tp], loc.at[2]),
        pltpu.make_async_copy(vec, vecg.at[me], loc.at[3]),
    ]
    first = []
    for step in range(1, HALF):
        peer = core * HALF + lax.rem(chip + step, HALF)
        first.append(remote(xh, xg.at[tp], xs.at[step], xr.at[step], (grp, peer)))
    first.append(remote(xh, xg.at[tp], xs.at[0], xr.at[0], (grp, partner)))
    for copy in first:
        copy.start()

    def to(step):
        other = lax.rem(me + step, total)
        return other // TP, lax.rem(other, TP)

    def block_copy(step):
        g, t = to(step)
        return remote(s0.at[t], w0.at[me], ss.at[step], sr.at[step], (g, t))

    def vec_copy(step):
        return remote(vec, vecg.at[me], vs.at[step], vr.at[step], to(step))

    def plane_copy(step):
        peer = lax.rem(tp + step, TP)
        return remote(s1.at[peer], w1.at[tp], ts.at[step], tr.at[step], (grp, peer))

    def start_all(step, carry):
        vec_copy(step).start()
        block_copy(step).start()
        return carry

    lax.fori_loop(1, total, start_all, 0)

    def start_plane(step, carry):
        plane_copy(step).start()
        return carry

    lax.fori_loop(1, TP, start_plane, 0)
    for copy in own:
        copy.start()
    slot = lax.rem(me, owners)
    user = me // owners
    for g in range(groups):
        target_self = (user == tp) & (g == grp)

        @pl.when(jnp.logical_not(target_self))
        def _():
            remote(wo, wog.at[slot], os.at[g], orr.at[slot], (g, user)).start()

        @pl.when(target_self)
        def _():
            pltpu.make_async_copy(wo, wog.at[slot], orr.at[slot]).start()

    passed = []
    for step in range(1, HALF):
        source = core * HALF + lax.rem(chip + HALF - step, HALF)
        remote(xh, xg.at[source], xs.at[step], xr.at[step], (grp, tp)).wait_recv()
        copy = remote(xg.at[source], xg.at[source], xs.at[HALF + step], xr.at[HALF + step], (grp, partner))
        copy.start()
        passed.append(copy)
    for copy in first:
        copy.wait_send()
    first[-1].wait_recv()
    for copy in passed:
        copy.wait()
    for copy in own:
        copy.wait()

    def wait_all(step, carry):
        vec_copy(step).wait()
        block_copy(step).wait()
        return carry

    lax.fori_loop(1, total, wait_all, 0)

    def wait_plane(step, carry):
        plane_copy(step).wait()
        return carry

    lax.fori_loop(1, TP, wait_plane, 0)
    for g in range(groups):

        @pl.when(jnp.logical_not((user == tp) & (g == grp)))
        def _():
            remote(wo, wog.at[slot], os.at[g], orr.at[slot], (g, user)).wait_send()

    for j in range(owners):
        pltpu.make_async_copy(wo, wog.at[j], orr.at[j]).wait()


def spread(groups, xh, s0, s1, wo, vec):
    total = groups * TP
    rows = s0.shape[1]
    owners = wo.shape[2] // TP // rows
    dma = pltpu.SemaphoreType.DMA
    return pl.pallas_call(
        functools.partial(spread_kernel, groups, owners),
        out_shape=(
            jax.ShapeDtypeStruct((TP,) + xh.shape, BF),
            jax.ShapeDtypeStruct((total,) + s0.shape[1:], BF),
            jax.ShapeDtypeStruct(s1.shape, BF),
            jax.ShapeDtypeStruct((owners,) + wo.shape, BF),
            jax.ShapeDtypeStruct((total,) + vec.shape, F32),
        ),
        in_specs=[ANY] * 5,
        out_specs=(ANY,) * 5,
        scratch_shapes=[
            dma((TP,)), dma((TP,)), dma((total,)), dma((total,)), dma((TP,)), dma((TP,)),
            dma((groups,)), dma((owners,)), dma((total,)), dma((total,)), dma((4,)),
        ],
        compiler_params=pltpu.CompilerParams(collective_id=1, has_side_effects=True),
        name="spread",
    )(xh, s0, s1, wo, vec)


def turn(values, rot):
    return (
        values * rot[0]
        + pltpu.roll(values, values.shape[1] - 8, 1) * rot[1]
        + pltpu.roll(values, 8, 1) * rot[2]
    )


def turn_back(values, rot):
    return (
        values * rot[0]
        + pltpu.roll(values * rot[1], 8, 1)
        + pltpu.roll(values * rot[2], values.shape[1] - 8, 1)
    )


def head_parts(values, head_dim):
    lane = lax.broadcasted_iota(jnp.int32, values.shape, 1)
    zero = jnp.zeros_like(values)
    return [
        jnp.where((lane >= h * head_dim) & (lane < (h + 1) * head_dim), values, zero)
        for h in range(values.shape[1] // head_dim)
    ]


def forward_kernel(head_dim, lens, xh, w, wo, gains, b_in, b_up, rot, part, qkv, prob, ctx, act, slope):
    width = qkv.shape[2] // 3
    ff = act.shape[2]
    rows = xh.shape[1]
    values = xh[0].astype(F32)
    normed = (values * gains[0:1] + gains[1:2]).astype(BF)
    mixed = nn_dot(normed, w[:, : 3 * width]) + b_in[...]
    queries = (turn(mixed[:, :width], rot).astype(BF).astype(F32) * head_dim ** (-0.5)).astype(BF)
    keys = turn(mixed[:, width : 2 * width], rot).astype(BF)
    vals = mixed[:, 2 * width :].astype(BF)
    qkv[0, :, :width] = queries
    qkv[0, :, width : 2 * width] = keys
    qkv[0, :, 2 * width :] = vals
    length = lens[pl.program_id(0)]
    row = lax.broadcasted_iota(jnp.int32, (rows, rows), 0)
    col = lax.broadcasted_iota(jnp.int32, (rows, rows), 1)
    allowed = (col <= row) & (col < length)
    total = None
    for h, (q_h, v_h) in enumerate(zip(head_parts(queries, head_dim), head_parts(vals, head_dim))):
        scores = jnp.where(allowed, nt_dot(q_h, keys), MASKED_SCORE)
        weights = jnp.exp(scores - jnp.max(scores, -1, keepdims=True))
        probability = (weights / jnp.sum(weights, -1, keepdims=True)).astype(BF)
        prob[0, h] = probability
        term = nn_dot(probability, v_h)
        total = term if total is None else total + term
    context = total.astype(BF)
    ctx[0] = context
    normed = (values * gains[2:3] + gains[3:4]).astype(BF)
    expanded = nn_dot(normed, w[:, 3 * width : 3 * width + ff]) + b_up[...]
    spread_to = 0.5 * (1.0 + lax.erf(expanded * 0.7071067811865476))
    active = (expanded * spread_to).astype(BF)
    act[0] = active
    slope[0] = (spread_to + expanded * (0.3989422804014327 * jnp.exp(-0.5 * expanded * expanded))).astype(BF)
    part[0] = (nn_dot(context, wo[...]) + nt_dot(active, w[:, 3 * width + ff :])).astype(BF)


def block_of(shape):
    return pl.BlockSpec((1,) + shape, lambda s, *_: (s,) + (0,) * len(shape))


def whole_of(shape):
    return pl.BlockSpec(shape, lambda s, *_: (0,) * len(shape))


def forward_layer(head_dim, lens, xg, w, wo, gains, b_in, b_up, rot):
    seqs, rows, width = xg.shape
    local = b_in.shape[1] // 3
    ff = b_up.shape[1]
    heads = local // head_dim
    outs = ((rows, width), (rows, 3 * local), (heads, rows, rows), (rows, local), (rows, ff), (rows, ff))
    return pl.pallas_call(
        functools.partial(forward_kernel, head_dim),
        grid_spec=pltpu.PrefetchScalarGridSpec(
            num_scalar_prefetch=1,
            grid=(seqs,),
            in_specs=[block_of((rows, width))]
            + [whole_of(a.shape) for a in (w, wo, gains, b_in, b_up, rot)],
            out_specs=[block_of(shape) for shape in outs],
        ),
        out_shape=[jax.ShapeDtypeStruct((seqs,) + shape, BF) for shape in outs],
        compiler_params=pltpu.CompilerParams(vmem_limit_bytes=VMEM_BYTES),
        cost_estimate=pl.CostEstimate(
            flops=2 * seqs * rows * width * 12 * local, bytes_accessed=24 << 20, transcendentals=0
        ),
        name="forward_layer",
    )(lens, xg, w, wo, gains, b_in, b_up, rot)


def backward_kernel(head_dim, gg, qkv, prob, ctx_unused, slope, w, wo, gains, rot, part, mixes, sums):
    width = qkv.shape[2] // 3
    ff = slope.shape[2]
    grad = gg[0]
    active_grad = nn_dot(grad, w[:, 3 * width + ff :])
    expanded_grad = (slope[0].astype(F32) * active_grad).astype(BF)
    total = nt_dot(expanded_grad, w[:, 3 * width : 3 * width + ff]) * gains[2:3]
    context_grad = nt_dot(grad, wo[...]).astype(BF)
    queries = qkv[0, :, :width]
    keys = qkv[0, :, width : 2 * width]
    vals = qkv[0, :, 2 * width :]
    query_grad = key_grad = value_grad = 0.0
    for h, (c_h, q_h, k_h) in enumerate(
        zip(head_parts(context_grad, head_dim), head_parts(queries, head_dim), head_parts(keys, head_dim))
    ):
        prob_b = prob[0, h]
        probability = prob_b.astype(F32)
        prob_grad = nt_dot(c_h, vals)
        value_grad = value_grad + tn_dot(prob_b, c_h)
        inner = jnp.sum(probability * prob_grad, -1, keepdims=True)
        score_grad = (probability * (prob_grad - inner)).astype(BF)
        query_grad = query_grad + nn_dot(score_grad, k_h)
        key_grad = key_grad + tn_dot(score_grad, q_h)
    query_grad = query_grad * head_dim ** (-0.5)
    pieces = [turn_back(query_grad, rot).astype(BF), turn_back(key_grad, rot).astype(BF), value_grad.astype(BF)]
    for i, piece in enumerate(pieces):
        mixes[0, :, i * width : (i + 1) * width] = piece
    mixes[0, :, 3 * width :] = expanded_grad
    for i, piece in enumerate(pieces):
        total = total + nt_dot(piece, w[:, i * width : (i + 1) * width]) * gains[0:1]
    part[0] = total.astype(BF)

    @pl.when(pl.program_id(0) == 0)
    def _():
        sums[...] = jnp.zeros_like(sums)

    for i, piece in enumerate(pieces):
        sums[:, i * width : (i + 1) * width] += jnp.sum(
            piece.astype(F32).reshape(-1, 8, width), axis=0
        )
    sums[:, 3 * width :] += jnp.sum(expanded_grad.astype(F32).reshape(-1, 8, ff), axis=0)


def backward_layer(head_dim, gg, qkv, prob, ctx, slope, w, wo, gains, rot):
    seqs, rows, width = gg.shape
    local = ctx.shape[2]
    ff = slope.shape[2]
    mix = 3 * local + ff
    return pl.pallas_call(
        functools.partial(backward_kernel, head_dim),
        grid=(seqs,),
        in_specs=[block_of(a.shape[1:]) for a in (gg, qkv, prob, ctx, slope)]
        + [whole_of(a.shape) for a in (w, wo, gains, rot)],
        out_specs=[block_of((rows, width)), block_of((rows, mix)), whole_of((8, mix))],
        out_shape=[
            jax.ShapeDtypeStruct((seqs, rows, width), BF),
            jax.ShapeDtypeStruct((seqs, rows, mix), BF),
            jax.ShapeDtypeStruct((8, mix), F32),
        ],
        compiler_params=pltpu.CompilerParams(vmem_limit_bytes=VMEM_BYTES),
        cost_estimate=pl.CostEstimate(
            flops=2 * seqs * rows * width * 14 * local, bytes_accessed=24 << 20, transcendentals=0
        ),
        name="backward_layer",
    )(gg, qkv, prob, ctx, slope, w, wo, gains, rot)


CHUNK = 32


def exchange_kernel(forward, gather, part, own, extra, *refs):
    if gather:
        out, gathered, met, joined, landed, ps, pr, bs, br, gs, gr, loc = refs
    else:
        out, met, joined, landed, ps, pr, bs, br = refs
        gathered = None
    grp, tp = place()
    core, chip = tp // HALF, lax.rem(tp, HALF)
    partner = lax.rem(tp + HALF, TP)
    rows, width = own.shape
    peers = [core * HALF + lax.rem(chip + step, HALF) for step in range(HALF)]
    greet([(grp, partner)] + [(grp, peer) for peer in peers[1:]])
    other_core = 1 - core
    order = [1, 2, 3, 0]
    to_partner = []
    for step in order:
        block = lax.rem(chip + step, HALF)
        copy = remote(part.at[other_core * HALF + block], met.at[step], ps.at[step], pr.at[step], (grp, partner))
        copy.start()
        to_partner.append(copy)
    sends = []
    for index, step in enumerate(order):
        to_partner[index].wait_recv()
        block = core * HALF + lax.rem(chip + step, HALF)

        def join(i, carry):
            at = pl.ds(pl.multiple_of(i * CHUNK, CHUNK), CHUNK)
            joined[step, at] = (part[block, at].astype(F32) + met[step, at].astype(F32)).astype(BF)
            return carry

        lax.fori_loop(0, rows // CHUNK, join, 0)
        if step:
            copy = remote(joined.at[step], landed.at[step], bs.at[step], br.at[step], (grp, peers[step]))
            copy.start()
            sends.append(copy)
    for copy in sends:
        copy.wait_recv()

    def finish(i, carry):
        at = pl.ds(pl.multiple_of(i * CHUNK, CHUNK), CHUNK)
        total = joined[0, at].astype(F32)
        for step in range(1, HALF):
            total = total + landed[step, at].astype(F32)
        if forward:
            result = (own[at].astype(F32) + total + extra[...]).astype(BF)
            out[at] = result
            values = result.astype(F32)
        else:
            values = own[at].astype(F32)
        centred = values - jnp.mean(values, -1, keepdims=True)
        scale = lax.rsqrt(jnp.mean(centred * centred, -1, keepdims=True) + NORM_EPSILON)
        if forward:
            gathered[tp, at] = (centred * scale).astype(BF)
        else:
            xhat = centred * scale
            mean_one = jnp.mean(total, -1, keepdims=True)
            mean_two = jnp.mean(total * xhat, -1, keepdims=True)
            result = (extra[at].astype(F32) + scale * (total - mean_one - xhat * mean_two)).astype(BF)
            out[at] = result
            if gather:
                gathered[tp, at] = result
        return carry

    lax.fori_loop(0, rows // CHUNK, finish, 0)
    for copy in to_partner + sends:
        copy.wait_send()
    if not gather:
        return
    first = [remote(gathered.at[tp], gathered.at[tp], gs.at[0], gr.at[0], (grp, partner))]
    for step in range(1, HALF):
        first.append(remote(gathered.at[tp], gathered.at[tp], gs.at[step], gr.at[step], (grp, peers[step])))
    for copy in first[1:] + first[:1]:
        copy.start()
    passed = []
    for step in range(1, HALF):
        source = core * HALF + lax.rem(chip + HALF - step, HALF)
        remote(gathered.at[source], gathered.at[source], gs.at[step], gr.at[step], (grp, tp)).wait_recv()
        copy = remote(
            gathered.at[source], gathered.at[source], gs.at[HALF + step], gr.at[HALF + step], (grp, partner)
        )
        copy.start()
        passed.append(copy)
    first[0].wait_recv()
    for copy in passed:
        copy.wait()
    for copy in first:
        copy.wait_send()


def exchange(part, own, extra, forward, gather, ident):
    seqs, rows, width = part.shape
    dma = pltpu.SemaphoreType.DMA
    out_shape = [jax.ShapeDtypeStruct((rows, width), BF)]
    scratch = [pltpu.VMEM((HALF, rows, width), BF)] * 3 + [dma((HALF,))] * 4
    if gather:
        out_shape.append(jax.ShapeDtypeStruct((seqs, rows, width), BF))
        scratch += [dma((TP,)), dma((TP,)), dma((1,))]
    return pl.pallas_call(
        functools.partial(exchange_kernel, forward, gather),
        out_shape=out_shape,
        in_specs=[VMEM] * 3,
        out_specs=[VMEM] * len(out_shape),
        scratch_shapes=scratch,
        compiler_params=pltpu.CompilerParams(
            collective_id=ident, has_side_effects=True, vmem_limit_bytes=VMEM_BYTES
        ),
        name="exchange",
    )(part, own, extra)


def settle_kernel(groups, owners, g0, h1, go, vec, r0, r1, ro, rv,
                  ss, sr, ts, tr, os, orr, vs, vr, loc):
    grp, tp = place()
    me = grp * TP + tp
    total = groups * TP
    greet_all(groups)

    def to(step):
        other = lax.rem(me + step, total)
        return other // TP, lax.rem(other, TP)

    def block_copy(step):
        g, t = to(step)
        return remote(g0.at[g * TP + t], r0.at[me], ss.at[step], sr.at[step], (g, t))

    def vec_copy(step):
        g, t = to(step)
        return remote(vec.at[g * TP + t], rv.at[me], vs.at[step], vr.at[step], (g, t))

    def plane_copy(step):
        peer = lax.rem(tp + step, TP)
        return remote(h1.at[peer], r1.at[tp], ts.at[step], tr.at[step], (grp, peer))

    def start_all(step, carry):
        vec_copy(step).start()
        block_copy(step).start()
        return carry

    lax.fori_loop(1, total, start_all, 0)

    def start_plane(step, carry):
        plane_copy(step).start()
        return carry

    lax.fori_loop(1, TP, start_plane, 0)
    own = [
        pltpu.make_async_copy(g0.at[me], r0.at[me], loc.at[0]),
        pltpu.make_async_copy(h1.at[tp], r1.at[tp], loc.at[1]),
        pltpu.make_async_copy(vec.at[me], rv.at[me], loc.at[2]),
    ]
    for copy in own:
        copy.start()
    for j in range(owners):
        owner = tp * owners + j

        @pl.when(owner != me)
        def _():
            remote(go.at[j], ro.at[grp], os.at[j], orr.at[grp], (owner // TP, lax.rem(owner, TP))).start()

        @pl.when(owner == me)
        def _():
            pltpu.make_async_copy(go.at[j], ro.at[grp], orr.at[grp]).start()

    for copy in own:
        copy.wait()

    def wait_all(step, carry):
        vec_copy(step).wait()
        block_copy(step).wait()
        return carry

    lax.fori_loop(1, total, wait_all, 0)

    def wait_plane(step, carry):
        plane_copy(step).wait()
        return carry

    lax.fori_loop(1, TP, wait_plane, 0)
    for j in range(owners):
        owner = tp * owners + j

        @pl.when(owner != me)
        def _():
            remote(go.at[j], ro.at[grp], os.at[j], orr.at[grp], (owner // TP, lax.rem(owner, TP))).wait_send()

    for g in range(groups):
        pltpu.make_async_copy(go.at[0], ro.at[g], orr.at[g]).wait()


def settle(groups, g0, h1, go, vec):
    total = groups * TP
    owners = go.shape[0]
    dma = pltpu.SemaphoreType.DMA
    return pl.pallas_call(
        functools.partial(settle_kernel, groups, owners),
        out_shape=(
            jax.ShapeDtypeStruct(g0.shape, BF),
            jax.ShapeDtypeStruct(h1.shape, BF),
            jax.ShapeDtypeStruct((groups,) + go.shape[1:], BF),
            jax.ShapeDtypeStruct(vec.shape, F32),
        ),
        in_specs=[ANY] * 4,
        out_specs=(ANY,) * 4,
        scratch_shapes=[
            dma((total,)), dma((total,)), dma((TP,)), dma((TP,)),
            dma((owners,)), dma((groups,)), dma((total,)), dma((total,)), dma((3,)),
        ],
        compiler_params=pltpu.CompilerParams(collective_id=4, has_side_effects=True),
        name="settle",
    )(g0, h1, go, vec)


def rotary(row_count, width, head_dim):
    rot_dim = head_dim // 4
    half_rot = rot_dim // 2
    column = jnp.arange(width, dtype=jnp.int32) % head_dim
    freq_slot = (column % half_rot).astype(F32)
    frequency = 10000.0 ** (-(freq_slot * 2.0) / rot_dim)
    angles = jnp.arange(row_count, dtype=F32)[:, None] * frequency[None, :]
    inside = (column < rot_dim)[None, :]
    first_half = (column < half_rot)[None, :]
    sine = jnp.sin(angles)
    return jnp.stack(
        [
            jnp.where(inside, jnp.cos(angles), 1.0),
            jnp.where(first_half, -sine, 0.0),
            jnp.where(inside & jnp.logical_not(first_half), sine, 0.0),
        ]
    )


def standard(values):
    centred = values - jnp.mean(values, -1, keepdims=True)
    return centred * lax.rsqrt(jnp.mean(centred * centred, -1, keepdims=True) + NORM_EPSILON)


def adam_update(weight, moment, square, gradient, first_fix, second_fix):
    moment = BETA_FIRST * moment + (1.0 - BETA_FIRST) * gradient
    square = BETA_SECOND * square + (1.0 - BETA_SECOND) * gradient * gradient
    change = -LEARNING * (
        moment / first_fix / (jnp.sqrt(square / second_fix) + ADAM_EPSILON) + DECAY_RATE * weight
    )
    return (change, moment, square)


def per_device(
    groups,
    tokens,
    cotangent,
    seq_lengths,
    seq_device,
    step_count,
    *state,
):
    params, moments, squares = state[0:5], state[5:10], state[10:15]
    attend_in, attend_out, expand_weight, reduce_weight, layer_vectors = params
    grp, tp = place()
    me = grp * TP + tp
    total = groups * TP
    rows, width = tokens.shape
    shard = attend_in.shape[1]
    head_dim = width // HEADS
    local = width // TP
    ff = expand_weight.shape[2] // TP
    vec_part = layer_vectors.shape[1]
    owners = local // shard
    plane_ids = grp * TP + jnp.arange(TP, dtype=jnp.int32)
    lens = jnp.sum(jnp.where(plane_ids[:, None] == seq_device[None, :], seq_lengths[None, :], 0), 1)
    own_length = jnp.sum(jnp.where(seq_device == me, seq_lengths, 0))
    valid = jnp.arange(rows, dtype=jnp.int32)[:, None] < own_length
    rot = rotary(rows, local, head_dim)

    blocks = [
        jnp.concatenate(
            [
                attend_in[l].astype(BF).reshape(shard, 3, TP, local).transpose(2, 0, 1, 3).reshape(TP, shard, 3 * local),
                expand_weight[l].astype(BF).reshape(shard, TP, ff).transpose(1, 0, 2),
                reduce_weight[l].astype(BF).reshape(shard, TP, ff).transpose(1, 0, 2),
            ],
            2,
        )
        for l in range(LAYERS)
    ]
    vec = jnp.pad(layer_vectors.astype(BF).astype(F32).reshape(-1), (0, 8 * 128 - 2 * vec_part)).reshape(8, 128)
    xhat_own = standard(tokens.astype(F32)).astype(BF)
    grad_own = jnp.where(valid, cotangent, jnp.zeros_like(cotangent))
    xg, w0, w1, wog, vecg = spread(groups, xhat_own, blocks[0], blocks[1], attend_out.astype(BF), vec)
    grads_all = lax.all_gather(grad_own, "tp", axis=0)
    weights = [w0.reshape(width, -1), lax.all_gather(w1, "grp", axis=0).reshape(width, -1)]
    out_rows = wog.transpose(1, 0, 2, 3).reshape(LAYERS, local, width)
    vectors = vecg.reshape(total, -1)[:, : 2 * vec_part].reshape(total, LAYERS, vec_part)
    vectors = vectors.transpose(1, 0, 2).reshape(LAYERS, -1)
    gains, b_in, b_up, b_rest = [], [], [], []
    for l in range(LAYERS):
        v = vectors[l]
        gains.append(v[: 4 * width].reshape(4, width))
        b_in.append(
            lax.dynamic_slice_in_dim(v[4 * width : 7 * width].reshape(3, width), tp * local, local, 1).reshape(1, -1)
        )
        b_up.append(lax.dynamic_slice_in_dim(v[8 * width : -width].reshape(1, -1), tp * ff, ff, 1))
        b_rest.append((v[7 * width : 8 * width] + v[-width:])[None, :])

    part0, *kept0 = forward_layer(head_dim, lens, xg, weights[0], out_rows[0], gains[0], b_in[0], b_up[0], rot)
    hidden0, xg1 = exchange(part0, tokens, b_rest[0], True, True, 2)
    part1, *kept1 = forward_layer(head_dim, lens, xg1, weights[1], out_rows[1], gains[1], b_in[1], b_up[1], rot)
    summed1 = lax.psum_scatter(part1, "tp", scatter_dimension=0, tiled=True)[0]
    hidden1 = (hidden0.astype(F32) + summed1.astype(F32) + b_rest[1]).astype(BF)

    def layer_back(l, xhats, gg, grad_rows, kept):
        qkv, prob, ctx, act, slope = kept
        part, mixes, sums = backward_layer(
            head_dim, gg, qkv, prob, ctx, slope, weights[l], out_rows[l], gains[l], rot
        )
        flat = lambda a: a.reshape(-1, a.shape[-1])
        sums = jnp.sum(sums, 0)
        cross = tn_dot(flat(xhats), flat(mixes))
        gain_one, shift_one, gain_two, shift_two = (gains[l][i][:, None] for i in range(4))
        split = 3 * local
        w_in, w_up = weights[l][:, :split].astype(F32), weights[l][:, split : split + ff].astype(F32)
        in_grad = gain_one * cross[:, :split] + shift_one * sums[None, :split]
        up_grad = gain_two * cross[:, split:] + shift_two * sums[None, split:]
        down_grad = tn_dot(flat(gg), flat(act))
        out_grad = tn_dot(flat(ctx), flat(gg)).astype(BF)
        packed = jnp.concatenate([in_grad.astype(BF), up_grad.astype(BF), down_grad.astype(BF)], 1)
        norm_sums = [
            jnp.sum(w_in * cross[:, :split], 1),
            jnp.sum(w_in * sums[None, :split], 1),
            jnp.sum(w_up * cross[:, split:], 1),
            jnp.sum(w_up * sums[None, split:], 1),
        ]
        here = (jnp.arange(TP) == tp)
        in_bias = jnp.where(here[None, :, None], sums[:split].reshape(3, 1, local), 0.0).reshape(-1)
        up_bias = jnp.where(here[:, None], sums[None, split:], 0.0).reshape(-1)
        bias_sums = jnp.sum(grad_rows.astype(F32), 0)
        vector = jnp.concatenate(norm_sums + [in_bias, bias_sums, up_bias, bias_sums])
        return part, packed, out_grad, vector

    part, packed1, out_grad1, vector1 = layer_back(1, xg1, grads_all, grad_own, kept1)
    reduced1 = lax.psum_scatter(packed1, "grp", scatter_dimension=0, tiled=True).reshape(TP, shard, -1)
    grad0, gg0 = exchange(part, hidden0, grad_own, False, True, 3)
    part, packed0, out_grad0, vector0 = layer_back(0, xg, gg0, grad0, kept0)
    (input_grad,) = exchange(part, tokens, grad0, False, False, 5)
    out_grads = jnp.stack([out_grad0, out_grad1]).reshape(LAYERS, owners, shard, width).transpose(1, 0, 2, 3)
    vec_send = jnp.stack([vector0, vector1]).reshape(LAYERS, total, vec_part).transpose(1, 0, 2).reshape(total, -1)
    vec_send = jnp.pad(vec_send, ((0, 0), (0, 8 * 128 - 2 * vec_part))).reshape(total, 8, 128)
    r0, r1, ro, rv = settle(groups, packed0.reshape(total, shard, -1), reduced1, out_grads, vec_send)
    split = 3 * local
    sum0 = jnp.sum(r0.reshape(groups, TP, shard, -1).astype(F32), 0)
    sums = [sum0, r1.astype(F32)]
    grad_in = jnp.stack(
        [s[:, :, :split].reshape(TP, shard, 3, local).transpose(1, 2, 0, 3).reshape(shard, -1) for s in sums]
    )
    grad_up = jnp.stack([s[:, :, split : split + ff].transpose(1, 0, 2).reshape(shard, -1) for s in sums])
    grad_down = jnp.stack([s[:, :, split + ff :].transpose(1, 0, 2).reshape(shard, -1) for s in sums])
    grad_out = jnp.sum(ro.astype(F32), 0)
    grad_vec = jnp.sum(rv, 0).reshape(-1)[: 2 * vec_part].reshape(LAYERS, vec_part)
    grads = (grad_in, grad_out, grad_up, grad_down, grad_vec)
    step_float = step_count[0].astype(F32)
    first_fix = 1.0 - jnp.power(BETA_FIRST, step_float)
    second_fix = 1.0 - jnp.power(BETA_SECOND, step_float)
    updated = [
        adam_update(params[i], moments[i], squares[i], grads[i], first_fix, second_fix) for i in range(5)
    ]
    return (
        jnp.stack([hidden0, hidden1]),
        input_grad,
        *grads,
        *(u[0] for u in updated),
        *(u[1] for u in updated),
        *(u[2] for u in updated),
    )


def solution(mesh):
    devices = mesh.devices.reshape(-1, TP)
    groups = devices.shape[0]
    flat = Mesh(devices, ("grp", "tp"))
    axes = ("grp", "tp")
    by_row = P(axes, None)
    by_dim = [P(None, axes, None)] * 4 + [P(None, axes)]
    return jax.shard_map(
        functools.partial(per_device, groups),
        mesh=flat,
        in_specs=(by_row, by_row, P(), P(), P(), *(by_dim * 3)),
        out_specs=(P(None, axes, None), by_row, *(by_dim * 4)),
        check_vma=False,
    )
```

time: 2920 us -> 572 us (0.20)
  waiting for transfers between devices: 2300 us -> 32.9 us
  Pallas kernels: 0 us -> 422 us
  matrix products: 184 us -> 24.2 us
  blocking collectives: 130 us -> 0 us
  local copies, waits for them, and re-layouts: 153 us -> 30.9 us
  loops' own time: 53.8 us -> 0 us
    reduce_scatter x8 -> x2, waiting for transfers between devices: 2040 us -> 32.8 us  [the longest x1 32.8 us: per_device(): lax.psum_scatter(packed1, 'grp', scatter_dimension=0, tiled=True)]
    pallas_call x0 -> x9, Pallas kernels: none -> 422 us  [the longest x3 173 us: exchange(): pl.pallas_call(functools.partial(exchange_kernel, forward, gather), out_s...]
    all_gather x8 -> x2, waiting for transfers between devices: 213 us -> 0.04 us  [the longest x1 0.02 us: per_device(): grads_all = lax.all_gather(grad_own, 'tp', axis=0)]
    dot_general x136 -> x6, matrix products: 184 us -> 24.2 us  [tn_dot(): return lax.dot_general(a, b, TN, preferred_element_type=F32)]
    all_gather x2 -> x0, blocking collectives: 130 us -> none  [per_device(): lax.all_gather(pieces[4], ('dp', 'fsdp'), axis=0, tiled=True)]
    dynamic_slice x144 -> x0, local copies, waits for them, and re-layouts: 95.7 us -> none  [the longest x112 77 us: block_slice(): lax.dynamic_slice_in_dim(matrix, block_index * block_width, block_width, 1)]
    another operation x4 -> x0, loops' own time: 53.8 us -> none  [the longest x2 42.6 us: attention_backward(): lax.map(one_block, jnp.arange(block_count))]
    unnamed x18 -> x4, waiting for transfers between devices: 49.6 us -> 0.07 us
  transfers between devices with their start and end apart: 17 -> 4, of which waited for: 14 -> 1; matrix products, arithmetic and copies ran while one was open for 10% -> 9% of each run, Pallas kernels for 0% -> 45%
where the time goes in v1:
time: 572 us; the launch traced here: 564 us
  Pallas kernels  422 us (74%)
  other arithmetic  38.5 us (7%)
  waiting for transfers between devices  32.9 us (6%)
  local copies, waits for them, and re-layouts  30.9 us (5%)
  matrix products  24.2 us (4%)
  between operations  15.6 us (3%)
    pallas_call x3, Pallas kernels, exchange(): pl.pallas_call(functools.partial(exchange_kernel, forward, gather), out_s...  173 us
    pallas_call x1, Pallas kernels, spread(): pl.pallas_call(functools.partial(spread_kernel, groups, owners), out_shap...  88.2 us
    pallas_call x1, Pallas kernels, settle(): pl.pallas_call(functools.partial(settle_kernel, groups, owners), out_shap...  79.9 us
    pallas_call x2, Pallas kernels, backward_layer(): pl.pallas_call(functools.partial(backward_kernel, head_dim), grid=(seqs,)...  41.7 us
    pallas_call x2, Pallas kernels, forward_layer(): pl.pallas_call(functools.partial(forward_kernel, head_dim), grid_spec=plt...  38.7 us
    reduce_scatter x1, waiting for transfers between devices, per_device(): lax.psum_scatter(packed1, 'grp', scatter_dimension=0, tiled=True)  32.8 us
    dot_general x6, matrix products, tn_dot(): return lax.dot_general(a, b, TN, preferred_element_type=F32)  24.2 us
  transfers between devices with their start and end apart: 4, of which 1 were waited for; matrix products, arithmetic and copies ran while one was open for 9% of the time, Pallas kernels for 45%

profile of v1, /device:TPU:1, one launch (start us, length us, event | category | flops | bytes accessed | tf_op | source)
XLA Modules:
  0.0 564.2 jit_solution(862486845419840222)
XLA Ops:
  7.2 1.2 convert_reduce_fusion.1
  8.4 1.4 fusion.12
  9.8 0.7 convert_element_type.137
  11.2 1.6 convert_element_type.136.wo
  12.8 1.3 convert.18
  14.8 1.0 fusion.13.xh
  16.8 0.9 pad_maximum_fusion.3.s0
  17.7 0.9 pad_maximum_fusion.4.s1
  18.7 88.2 %spread.1 = (bf16[8,256,1024]{2,1,0:T(8,128)(2,1)}, bf16[32,32,1408]{2,1,0:T(8,128)(2,1)}, bf16[8,32,1408]{2,1,0:T(8,128)(2,1)}, bf16[4,2,32,1024]{3,2,1,0:T(8,128)(2,1)}, f32[32,8,128]{2,1,0:T(8,128)}) custom-call(bf16[256,1024]{1,0:T(8,128)(2,1)} %fusion.13.xh, bf16[8,32,1408]{2,1,0:T(8,128)(2,1)} %pad_maximum_fusion.3.s0, ...), custom_call_target="tpu_custom_call" | custom-call | tf_op jit(solution)/shard_map/spread/pallas_call | solution.py:186
  108.3 1.0 convert_reduce_fusion.3
  109.3 0.9 copy.230
  113.6 0.7 dynamic-slice.7
  114.9 0.7 select_reduce_fusion.lens
  116.1 0.8 pad_maximum_fusion.5.rot
  117.5 0.8 fusion.36
  118.3 19.3 %forward_layer.2 = (bf16[8,256,1024]{2,1,0:T(8,128)(2,1)}, bf16[8,256,384]{2,1,0:T(8,128)(2,1)}, bf16[8,2,256,256]{3,2,1,0:T(8,128)(2,1)}, bf16[8,256,128]{2,1,0...) custom-call(s32[8]{0:T(128)} %select_reduce_fusion.lens, ...), custom_call_target="tpu_custom_call" | custom-call | flops 6442450944 | bytes 25165824 | tf_op jit(solution)/shard_map/forward_layer/pallas_call | solution.py:281
  137.7 66.6 %exchange.3 = (bf16[256,1024]{1,0:T(8,128)(2,1)}, bf16[8,256,1024]{2,1,0:T(8,128)(2,1)}) custom-call(bf16[8,256,1024]{2,1,0:T(8,128)(2,1)} %get-tuple-element.57.part, bf16[256,1024]{1,0:T(8,128)(2,1)} %own.3, f32[1,1024]{1,0:T(1,128)} %bitcast.191), custom_call_target="tpu_custom_call" | custom-call | tf_op jit(solution)/shard_map/exchange/pallas_call | solution.py:466
  204.3 19.4 %forward_layer.3 = (bf16[8,256,1024]{2,1,0:T(8,128)(2,1)}, bf16[8,256,384]{2,1,0:T(8,128)(2,1)}, bf16[8,2,256,256]{3,2,1,0:T(8,128)(2,1)}, bf16[8,256,128]{2,1,0...) custom-call(s32[8]{0:T(128)} %select_reduce_fusion.lens, ...), custom_call_target="tpu_custom_call" | custom-call | flops 6442450944 | bytes 25165824 | tf_op jit(solution)/shard_map/forward_layer/pallas_call | solution.py:281
  224.7 20.8 %backward_layer.2 = (bf16[8,256,1024]{2,1,0:T(8,128)(2,1)}, bf16[8,256,896]{2,1,0:T(8,128)(2,1)}, f32[8,896]{1,0:T(8,128)}) custom-call(bf16[8,256,1024]{2,1,0:T(8,128)(2,1)} %bitcast.150, bf16[8,256,384]{2,1,0:T(8,128)(2,1)} %get-tuple-element.62.qkv, bf16[8,2,256,256]{3,2,1,0:T(8,128)(2,1)} %get-tuple-element.63.prob, ...), custom_call_target="tpu_custom_call" | custom-call | flops 7516192768 | bytes 25165824 | tf_op jit(solution)/shard_map/backward_layer/pallas_call | solution.py:347
  245.5 0.8 reduce_sum.176
  246.3 73.0 %exchange.4 = (bf16[256,1024]{1,0:T(8,128)(2,1)}, bf16[8,256,1024]{2,1,0:T(8,128)(2,1)}) custom-call(bf16[8,256,1024]{2,1,0:T(8,128)(2,1)} %get-tuple-element.66.part, bf16[256,1024]{1,0:T(8,128)(2,1)} %get-tuple-element.58.own, bf16[256,1024]{1,0:T(8,128)(2,1)} %get-tuple-element.110.extra), custom_call_target="tpu_custom_call" | custom-call | tf_op jit(solution)/shard_map/exchange/pallas_call | solution.py:466
  319.3 20.9 %backward_layer.3 = (bf16[8,256,1024]{2,1,0:T(8,128)(2,1)}, bf16[8,256,896]{2,1,0:T(8,128)(2,1)}, f32[8,896]{1,0:T(8,128)}) custom-call(bf16[8,256,1024]{2,1,0:T(8,128)(2,1)} %get-tuple-element.67.gg, bf16[8,256,384]{2,1,0:T(8,128)(2,1)} %get-tuple-element.68.qkv, bf16[8,2,256,256]{3,2,1,0:T(8,128)(2,1)} %get-tuple-element.69.prob, ...), custom_call_target="tpu_custom_call" | custom-call | flops 7516192768 | bytes 25165824 | tf_op jit(solution)/shard_map/backward_layer/pallas_call | solution.py:347
  340.2 33.8 %exchange.5 = bf16[256,1024]{1,0:T(8,128)(2,1)} custom-call(bf16[8,256,1024]{2,1,0:T(8,128)(2,1)} %get-tuple-element.72.part, bf16[256,1024]{1,0:T(8,128)(2,1)} %own.3, bf16[256,1024]{1,0:T(8,128)(2,1)} %get-tuple-element.73.extra), custom_call_target="tpu_custom_call" | custom-call | tf_op jit(solution)/shard_map/exchange/pallas_call | solution.py:466
  374.2 7.5 %convolution_bitcast_fusion = f32[1024,896]{1,0:T(8,128)S(1)} fusion(bf16[8,256,1024]{2,1,0:T(8,128)(2,1)} %get-tuple-element.59.xh, bf16[8,256,896]{2,1,0:T(8,128)(2,1)} %get-tuple-element.77), kind=kOutput, calls=%fused_computation.15 | convolution fusion | flops 3758096384 | bytes 11534336 | tf_op jit(solution)/shard_map/dot_general | solution.py:47
  381.7 0.8 fusion.7
  382.6 1.0 fusion.3
  383.6 1.3 copy-done.3
  384.9 2.4 bitcast_convert_fusion
  387.3 1.8 pad_maximum_fusion.1
  389.1 7.8 %convolution_bitcast_fusion.1 = f32[1024,896]{1,0:T(8,128)S(1)} fusion(bf16[8,256,1024]{2,1,0:T(8,128)(2,1)} %get-tuple-element.53.xh, bf16[8,256,896]{2,1,0:T(8,128)(2,1)} %get-tuple-element.74), kind=kOutput, calls=%fused_computation.16 | convolution fusion | flops 3758096384 | bytes 11534336 | tf_op jit(solution)/shard_map/dot_general | solution.py:47
  396.9 0.8 fusion.5
  397.8 1.0 fusion.1
  399.7 0.7 copy.218
  400.4 3.4 fusion.11
  403.8 0.8 fusion.10
  404.6 0.8 maximum_bitcast_fusion.go
  405.4 2.4 bitcast_convert_fusion.1
  407.8 1.8 pad_maximum_fusion
  409.6 1.2 fusion.19
  410.9 1.1 pad_maximum_fusion.2
  412.0 32.8 %reduce-scatter.5.cloned.1.call-done = bf16[256,1408]{1,0:T(8,128)(2,1)} async-done(((bf16[1024,1408]{1,0:T(8,128)(2,1)}), bf16[256,1408]{1,0:T(8,128)(2,1)}) %reduce-scatter.5.cloned.1.call-update) | async-done | bytes 720912 | tf_op jit(solution)/shard_map/reduce_scatter | solution.py:707
  444.7 79.9 %settle.1 = (bf16[32,32,1408]{2,1,0:T(8,128)(2,1)}, bf16[8,32,1408]{2,1,0:T(8,128)(2,1)}, bf16[4,2,32,1024]{3,2,1,0:T(8,128)(2,1)}, f32[32,8,128]{2,1,0:T(8,128)}) custom-call(bf16[32,32,1408]{2,1,0:T(8,128)(2,1)} %bitcast.148, bf16[8,32,1408]{2,1,0:T(8,128)(2,1)} %bitcast.178, bf16[4,2,32,1024]{3,2,1,0:T(8,128)(2,1)} %maximum_bitcast_fusion.go, ...), custom_call_target="tpu_custom_call" | custom-call | tf_op jit(solution)/shard_map/settle/pallas_call | solution.py:562
  524.6 2.4 convert_reduce_fusion
  527.0 0.9 slice_bitcast_fusion.1
  528.0 0.8 slice.302
  529.0 1.8 convert_reduce_fusion.2
  530.9 1.3 copy.189
  532.8 0.8 constant_dynamic-update-slice_fusion.3
  533.6 1.1 reshape.493
  535.0 0.8 stack_reshape.19
  535.8 0.8 constant_dynamic-update-slice_fusion.7
  537.0 0.8 constant_dynamic-update-slice_fusion.5
  537.9 0.9 slice_bitcast_fusion
  539.3 2.4 copy.188
  541.6 2.0 stack_reshape.21
  543.7 1.9 constant_dynamic-update-slice_fusion.2
  545.7 1.5 constant_dynamic-update-slice_fusion.4
  547.2 0.7 add_multiply_fusion.4
  548.0 1.0 add_multiply_fusion.3
  549.0 1.8 add_multiply_fusion.2
  551.7 2.2 add_multiply_fusion.1
  553.9 0.8 copy-done.25
  554.7 2.2 add_multiply_fusion
  556.8 0.8 copy.252
  (190 shorter events, 12.9 us)
Async XLA Ops:
  7.2 197.1 %all-gather.5.cloned.1.call-start = ((), (), s32[]{:S(2)}) async-start(), calls=%async_computation.4 | async-start | bytes 3604480 | tf_op jit(solution)/shard_map/all_gather | solution.py:657
  8.4 6.4 %copy-start = (bf16[256,1024]{1,0:T(8,128)(2,1)S(1)}, bf16[256,1024]{1,0:T(8,128)(2,1)}, u32[]{:S(2)}) copy-start(bf16[256,1024]{1,0:T(8,128)(2,1)} %own.3) | copy-start | bytes 1572868
  12.8 3.0 copy-start.5
  14.5 1.6 copy-start.7
  16.8 90.2 %copy-start.40 = (s32[32]{0:T(128)S(1)}, s32[32]{0:T(128)}, u32[]{:S(2)}) copy-start(s32[32]{0:T(128)} %param.22) | copy-start | bytes 388
  16.8 90.2 %copy-start.41 = (s32[32]{0:T(128)S(1)}, s32[32]{0:T(128)}, u32[]{:S(2)}) copy-start(s32[32]{0:T(128)} %param.23) | copy-start | bytes 388
  16.8 91.5 %copy-start.31 = (bf16[256,1024]{1,0:T(8,128)(2,1)S(1)}, bf16[256,1024]{1,0:T(8,128)(2,1)}, u32[]{:S(2)}) copy-start(bf16[256,1024]{1,0:T(8,128)(2,1)} %param.21) | copy-start | bytes 1572868
  106.9 10.6 %copy-start.30 = (bf16[4,2,32,1024]{3,2,1,0:T(8,128)(2,1)S(1)}, bf16[4,2,32,1024]{3,2,1,0:T(8,128)(2,1)}, u32[]{:S(2)}) copy-start(bf16[4,2,32,1024]{3,2,1,0:T(8,128)(2,1)} %get-tuple-element.55) | copy-start | bytes 1572868
  106.9 117.8 %all-gather.7.cloned.1.call-start = ((), (), s32[]{:S(2)}) async-start(), calls=%async_computation.5 | async-start | bytes 4718592 | tf_op jit(solution)/shard_map/all_gather | solution.py:656
  109.3 300.4 %reduce-scatter.3.cloned.1.call-start = ((), (), s32[]{:S(2)}) async-start(), calls=%async_computation.2 | async-start | bytes 4718592 | tf_op jit(solution)/shard_map/reduce_scatter | solution.py:674
  223.6 221.1 %reduce-scatter.5.cloned.1.call-start = ((), (), s32[]{:S(2)}) async-start(), calls=%async_computation.3 | async-start | bytes 3604480 | tf_op jit(solution)/shard_map/reduce_scatter | solution.py:707
  340.2 33.8 %copy-start.35 = (f32[8,896]{1,0:T(8,128)S(1)}, f32[8,896]{1,0:T(8,128)}, u32[]{:S(2)}) copy-start(f32[8,896]{1,0:T(8,128)} %get-tuple-element.75) | copy-start | bytes 86020
  374.1 7.6 %copy-start.19 = (bf16[32,32,1408]{2,1,0:T(8,128)(2,1)S(1)}, bf16[32,32,1408]{2,1,0:T(8,128)(2,1)}, u32[]{:S(2)}) copy-start(bf16[32,32,1408]{2,1,0:T(8,128)(2,1)} %all-gather.5.cloned.1.call-done) | copy-start | bytes 8650756
  381.7 1.9 copy-start.43
  382.5 2.3 copy-start.3
  389.1 7.8 %copy-start.18 = (bf16[32,32,1408]{2,1,0:T(8,128)(2,1)S(1)}, bf16[32,32,1408]{2,1,0:T(8,128)(2,1)}, u32[]{:S(2)}) copy-start(bf16[32,32,1408]{2,1,0:T(8,128)(2,1)} %get-tuple-element.54) | copy-start | bytes 8650756
  397.7 1.1 copy-start.15
  397.7 2.6 copy-start.29
  399.5 4.3 copy-start.28
  399.7 4.1 copy-start.4
  403.8 1.6 copy-start.42
  407.8 1.8 copy-start.2
  524.6 3.4 copy-start.17
  527.0 1.9 copy-start.1
  527.0 1.9 copy-start.34
  528.9 3.4 slice-start
  529.0 18.1 %copy-start.37 = (f32[2,416]{1,0:T(2,128)}, f32[2,416]{1,0:T(2,128)S(1)}, u32[]{:S(2)}) copy-start(f32[2,416]{1,0:T(2,128)S(1)} %reshape.495) | copy-start | bytes 9988
  538.8 6.8 %copy-start.10 = (f32[2,32,4096]{2,1,0:T(8,128)S(1)}, f32[2,32,4096]{2,1,0:T(8,128)}, u32[]{:S(2)}) copy-start(f32[2,32,4096]{2,1,0:T(8,128)} %constant_dynamic-update-slice_fusion.7) | copy-start | bytes 3145732
  538.8 6.8 %copy-start.12 = (f32[2,32,4096]{2,1,0:T(8,128)S(1)}, f32[2,32,4096]{2,1,0:T(8,128)}, u32[]{:S(2)}) copy-start(f32[2,32,4096]{2,1,0:T(8,128)} %constant_dynamic-update-slice_fusion.5) | copy-start | bytes 3145732
  539.1 8.1 %copy-start.36 = (f32[2,416]{1,0:T(2,128)S(1)}, f32[2,416]{1,0:T(2,128)}, u32[]{:S(2)}) copy-start(f32[2,416]{1,0:T(2,128)} %param.29) | copy-start | bytes 9988
  539.1 8.1 %copy-start.38 = (f32[2,416]{1,0:T(2,128)S(1)}, f32[2,416]{1,0:T(2,128)}, u32[]{:S(2)}) copy-start(f32[2,416]{1,0:T(2,128)} %param.39) | copy-start | bytes 9988
  539.1 8.1 %copy-start.39 = (f32[2,416]{1,0:T(2,128)S(1)}, f32[2,416]{1,0:T(2,128)}, u32[]{:S(2)}) copy-start(f32[2,416]{1,0:T(2,128)} %param.34) | copy-start | bytes 9988
  541.6 7.3 %copy-start.9 = (f32[2,32,3072]{2,1,0:T(8,128)S(1)}, f32[2,32,3072]{2,1,0:T(8,128)}, u32[]{:S(2)}) copy-start(f32[2,32,3072]{2,1,0:T(8,128)} %param.25) | copy-start | bytes 2359300
  543.6 4.3 copy-start.20
  543.6 4.3 copy-start.21
  543.6 4.3 copy-start.32
  543.6 4.3 copy-start.33
  543.6 5.3 copy-start.26
  543.7 5.3 copy-start.27
  545.6 3.4 copy-start.16
  545.6 8.2 %copy-start.11 = (f32[2,32,4096]{2,1,0:T(8,128)}, f32[2,32,4096]{2,1,0:T(8,128)S(1)}, u32[]{:S(2)}) copy-start(f32[2,32,4096]{2,1,0:T(8,128)S(1)} %constant_dynamic-update-slice_fusion.6) | copy-start | bytes 3145732
  547.2 3.6 copy-start.13
  549.0 1.8 copy-start.6
  549.0 2.4 copy-start.22
  549.0 2.7 copy-start.23
  551.7 2.2 copy-start.8
  551.7 2.2 copy-start.24
  551.7 3.0 copy-start.25
  554.7 2.2 copy-start.14
Sparse Core Ops, SparseCore 0:
  107.0 58.3 all-gather.4
  167.9 47.0 all-gather.6
  223.8 85.0 reduce-scatter.2
  389.2 55.4 reduce-scatter.4

commit v2 on v1

v2 whole, which is shorter than its diff:
```python
import functools

import jax
import jax.numpy as jnp
from jax import lax
from jax.experimental import pallas as pl
from jax.experimental.pallas import tpu as pltpu
from jax.sharding import Mesh
from jax.sharding import PartitionSpec as P

HEADS = 16
LAYERS = 2
NORM_EPSILON = 1e-05
ADAM_EPSILON = 1e-08
LEARNING = 0.02
BETA_FIRST = 0.9
BETA_SECOND = 0.95
DECAY_RATE = 0.1
MASKED_SCORE = -1e30

TP = 8
HALF = TP // 2
BF = jnp.bfloat16
F32 = jnp.float32
MESH = pl.DeviceIdType.MESH
NT = (((1,), (1,)), ((), ()))
TN = (((0,), (0,)), ((), ()))
ANY = pl.BlockSpec(memory_space=pl.ANY)
VMEM = pl.BlockSpec(memory_space=pltpu.VMEM)
SMEM = pl.BlockSpec(memory_space=pltpu.SMEM)
VMEM_BYTES = 60 * 1024 * 1024


def place():
    return lax.axis_index("grp"), lax.axis_index("tp")


def nn_dot(a, b):
    return jnp.dot(a, b, preferred_element_type=F32)


def nt_dot(a, b):
    return lax.dot_general(a, b, NT, preferred_element_type=F32)


def tn_dot(a, b):
    return lax.dot_general(a, b, TN, preferred_element_type=F32)


def remote(src, dst, send, recv, target):
    return pltpu.make_async_remote_copy(
        src_ref=src, dst_ref=dst, send_sem=send, recv_sem=recv, device_id=target, device_id_type=MESH
    )


def greet(targets):
    barrier = pltpu.get_barrier_semaphore()
    for target in targets:
        pl.semaphore_signal(barrier, inc=1, device_id=target, device_id_type=MESH)
    pl.semaphore_wait(barrier, len(targets))


def greet_all(groups):
    grp, tp = place()
    me = grp * TP + tp
    total = groups * TP
    barrier = pltpu.get_barrier_semaphore()

    def signal(step, carry):
        other = lax.rem(me + step, total)
        pl.semaphore_signal(
            barrier, inc=1, device_id=(other // TP, lax.rem(other, TP)), device_id_type=MESH
        )
        return carry

    lax.fori_loop(1, total, signal, 0)
    pl.semaphore_wait(barrier, total - 1)


def spread_kernel(groups, owners, xh, s0, s1, wo, vec, xg, w0, w1, wog, vecg,
                  xs, xr, ss, sr, ts, tr, os, orr, vs, vr, loc):
    grp, tp = place()
    me = grp * TP + tp
    total = groups * TP
    core, chip = tp // HALF, lax.rem(tp, HALF)
    partner = lax.rem(tp + HALF, TP)
    greet_all(groups)
    own = [
        pltpu.make_async_copy(xh, xg.at[tp], loc.at[0]),
        pltpu.make_async_copy(s0.at[tp], w0.at[me], loc.at[1]),
        pltpu.make_async_copy(s1.at[tp], w1.at[tp], loc.at[2]),
        pltpu.make_async_copy(vec, vecg.at[me], loc.at[3]),
    ]
    first = []
    for step in range(1, HALF):
        peer = core * HALF + lax.rem(chip + step, HALF)
        first.append(remote(xh, xg.at[tp], xs.at[step], xr.at[step], (grp, peer)))
    first.append(remote(xh, xg.at[tp], xs.at[0], xr.at[0], (grp, partner)))
    for copy in first:
        copy.start()

    def to(step):
        other = lax.rem(me + step, total)
        return other // TP, lax.rem(other, TP)

    def block_copy(step):
        g, t = to(step)
        return remote(s0.at[t], w0.at[me], ss.at[step], sr.at[step], (g, t))

    def vec_copy(step):
        return remote(vec, vecg.at[me], vs.at[step], vr.at[step], to(step))

    def plane_copy(step):
        peer = lax.rem(tp + step, TP)
        return remote(s1.at[peer], w1.at[tp], ts.at[step], tr.at[step], (grp, peer))

    def start_all(step, carry):
        vec_copy(step).start()
        block_copy(step).start()
        return carry

    lax.fori_loop(1, total, start_all, 0)

    def start_plane(step, carry):
        plane_copy(step).start()
        return carry

    lax.fori_loop(1, TP, start_plane, 0)
    for copy in own:
        copy.start()
    slot = lax.rem(me, owners)
    user = me // owners
    for g in range(groups):
        target_self = (user == tp) & (g == grp)

        @pl.when(jnp.logical_not(target_self))
        def _():
            remote(wo, wog.at[slot], os.at[g], orr.at[slot], (g, user)).start()

        @pl.when(target_self)
        def _():
            pltpu.make_async_copy(wo, wog.at[slot], orr.at[slot]).start()

    passed = []
    for step in range(1, HALF):
        source = core * HALF + lax.rem(chip + HALF - step, HALF)
        remote(xh, xg.at[source], xs.at[step], xr.at[step], (grp, tp)).wait_recv()
        copy = remote(xg.at[source], xg.at[source], xs.at[HALF + step], xr.at[HALF + step], (grp, partner))
        copy.start()
        passed.append(copy)
    for copy in first:
        copy.wait_send()
    first[-1].wait_recv()
    for copy in passed:
        copy.wait()
    for copy in own:
        copy.wait()

    def wait_all(step, carry):
        vec_copy(step).wait()
        block_copy(step).wait()
        return carry

    lax.fori_loop(1, total, wait_all, 0)

    def wait_plane(step, carry):
        plane_copy(step).wait()
        return carry

    lax.fori_loop(1, TP, wait_plane, 0)
    for g in range(groups):

        @pl.when(jnp.logical_not((user == tp) & (g == grp)))
        def _():
            remote(wo, wog.at[slot], os.at[g], orr.at[slot], (g, user)).wait_send()

    for j in range(owners):
        pltpu.make_async_copy(wo, wog.at[j], orr.at[j]).wait()


def spread(groups, xh, s0, s1, wo, vec):
    total = groups * TP
    rows = s0.shape[1]
    owners = wo.shape[2] // TP // rows
    dma = pltpu.SemaphoreType.DMA
    return pl.pallas_call(
        functools.partial(spread_kernel, groups, owners),
        out_shape=(
            jax.ShapeDtypeStruct((TP,) + xh.shape, BF),
            jax.ShapeDtypeStruct((total,) + s0.shape[1:], BF),
            jax.ShapeDtypeStruct(s1.shape, BF),
            jax.ShapeDtypeStruct((owners,) + wo.shape, BF),
            jax.ShapeDtypeStruct((total,) + vec.shape, F32),
        ),
        in_specs=[ANY] * 5,
        out_specs=(ANY,) * 5,
        scratch_shapes=[
            dma((TP,)), dma((TP,)), dma((total,)), dma((total,)), dma((TP,)), dma((TP,)),
            dma((groups,)), dma((owners,)), dma((total,)), dma((total,)), dma((4,)),
        ],
        compiler_params=pltpu.CompilerParams(collective_id=1, has_side_effects=True),
        name="spread",
    )(xh, s0, s1, wo, vec)


def turn(values, rot):
    return (
        values * rot[0]
        + pltpu.roll(values, values.shape[1] - 8, 1) * rot[1]
        + pltpu.roll(values, 8, 1) * rot[2]
    )


def turn_back(values, rot):
    return (
        values * rot[0]
        + pltpu.roll(values * rot[1], 8, 1)
        + pltpu.roll(values * rot[2], values.shape[1] - 8, 1)
    )


def head_parts(values, head_dim):
    lane = lax.broadcasted_iota(jnp.int32, values.shape, 1)
    zero = jnp.zeros_like(values)
    return [
        jnp.where((lane >= h * head_dim) & (lane < (h + 1) * head_dim), values, zero)
        for h in range(values.shape[1] // head_dim)
    ]


def bias_slices(vec, tp, local, ff):
    width = vec.shape[1]
    b_in = vec[4:7, pl.ds(pl.multiple_of(tp * local, local), local)]
    per_row = width // ff
    row = 8 + tp // per_row
    b_up = vec[pl.ds(row, 1), pl.ds(pl.multiple_of(lax.rem(tp, per_row) * ff, ff), ff)]
    return b_in, b_up


def seq_forward(values, lengths, head_dim, w, wo, vec, b_in, b_up, rot):
    rows = values.shape[0]
    local = wo.shape[0]
    ff = b_up.shape[1]
    values = values.astype(F32)
    normed = (values * vec[0:1] + vec[1:2]).astype(BF)
    mixed = nn_dot(normed, w[:, : 3 * local])
    parts = [mixed[:, i * local : (i + 1) * local] + b_in[i : i + 1] for i in range(3)]
    queries = (turn(parts[0], rot).astype(BF).astype(F32) * head_dim ** (-0.5)).astype(BF)
    keys = turn(parts[1], rot).astype(BF)
    vals = parts[2].astype(BF)
    row = lax.broadcasted_iota(jnp.int32, (rows, rows), 0)
    col = lax.broadcasted_iota(jnp.int32, (rows, rows), 1)
    allowed = (col <= row) & (col < lengths)
    total, probs = None, []
    for q_h, v_h in zip(head_parts(queries, head_dim), head_parts(vals, head_dim)):
        scores = jnp.where(allowed, nt_dot(q_h, keys), MASKED_SCORE)
        weights = jnp.exp(scores - jnp.max(scores, -1, keepdims=True))
        probability = (weights / jnp.sum(weights, -1, keepdims=True)).astype(BF)
        probs.append(probability)
        term = nn_dot(probability, v_h)
        total = term if total is None else total + term
    context = total.astype(BF)
    normed = (values * vec[2:3] + vec[3:4]).astype(BF)
    expanded = nn_dot(normed, w[:, 3 * local : 3 * local + ff]) + b_up
    spread_to = 0.5 * (1.0 + lax.erf(expanded * 0.7071067811865476))
    active = (expanded * spread_to).astype(BF)
    slope = (spread_to + expanded * (0.3989422804014327 * jnp.exp(-0.5 * expanded * expanded))).astype(BF)
    part = nn_dot(context, wo[...]) + nt_dot(active, w[:, 3 * local + ff :])
    return part, (queries, keys, vals), probs, context, active, slope


def seq_backward(grad, qkv, probs, slope, head_dim, w, wo, vec, rot):
    local = wo.shape[0]
    ff = slope.shape[1]
    queries, keys, vals = qkv
    active_grad = nn_dot(grad, w[:, 3 * local + ff :])
    expanded_grad = (slope.astype(F32) * active_grad).astype(BF)
    total = nt_dot(expanded_grad, w[:, 3 * local : 3 * local + ff]) * vec[2:3]
    context_grad = nt_dot(grad, wo[...]).astype(BF)
    query_grad = key_grad = value_grad = 0.0
    for prob_b, c_h, q_h, k_h in zip(
        probs, head_parts(context_grad, head_dim), head_parts(queries, head_dim), head_parts(keys, head_dim)
    ):
        probability = prob_b.astype(F32)
        prob_grad = nt_dot(c_h, vals)
        value_grad = value_grad + tn_dot(prob_b, c_h)
        inner = jnp.sum(probability * prob_grad, -1, keepdims=True)
        score_grad = (probability * (prob_grad - inner)).astype(BF)
        query_grad = query_grad + nn_dot(score_grad, k_h)
        key_grad = key_grad + tn_dot(score_grad, q_h)
    query_grad = query_grad * head_dim ** (-0.5)
    pieces = [turn_back(query_grad, rot).astype(BF), turn_back(key_grad, rot).astype(BF), value_grad.astype(BF)]
    mixed_grad = jnp.concatenate(pieces, 1)
    total = total + nt_dot(mixed_grad, w[:, : 3 * local]) * vec[0:1]
    return total, mixed_grad, expanded_grad


def fold_rows(values):
    return jnp.sum(values.astype(F32).reshape(-1, 8, values.shape[1]), axis=0)


def across(chip, step):
    x = lax.rem(lax.rem(chip, 2) + lax.rem(step, 2), 2)
    y = lax.rem(chip // 2 + step // 2, 2)
    return 2 * y + x


def pick(core, other):
    return core + (1 - 2 * core) * other


CHUNK = 32


def chunks(rows, body):
    def step(i, carry):
        body(pl.ds(pl.multiple_of(i * CHUNK, CHUNK), CHUNK))
        return carry

    lax.fori_loop(0, rows // CHUNK, step, 0)


def norm_parts(values):
    centred = values - jnp.mean(values, -1, keepdims=True)
    return centred, lax.rsqrt(jnp.mean(centred * centred, -1, keepdims=True) + NORM_EPSILON)


class Exchange:
    def __init__(self, both, met, landed, sems):
        self.joined, self.mine, self.met, self.landed = both.at[0], both.at[1], met, landed
        self.ps, self.pr, self.bs, self.br = sems
        self.grp, tp = place()
        self.core, self.chip = tp // HALF, lax.rem(tp, HALF)
        self.partner = lax.rem(tp + HALF, TP)

    def to_partner(self, k):
        return remote(
            self.mine.at[k], self.met.at[k], self.ps.at[k], self.pr.at[k], (self.grp, self.partner)
        )

    def to_owner(self, k):
        owner = self.core * HALF + across(self.chip, k)
        return remote(
            self.joined.at[k], self.landed.at[k], self.bs.at[k], self.br.at[k], (self.grp, owner)
        )

    def join(self, k):
        self.to_partner(k).wait_recv()

        def add(at):
            self.joined[k, at] = (self.joined[k, at].astype(F32) + self.met[k, at].astype(F32)).astype(BF)

        chunks(self.met.shape[1], add)

    def hand_over(self, k):
        self.join(k)
        if k:
            self.to_owner(k).start()

    def total(self, at):
        value = self.joined[0, at].astype(F32)
        for k in range(1, HALF):
            value = value + self.landed[k, at].astype(F32)
        return value

    def wait_landed(self):
        for k in range(1, HALF):
            self.to_owner(k).wait_recv()

    def drain(self):
        for k in range(HALF):
            self.to_partner(k).wait_send()
        for k in range(1, HALF):
            self.to_owner(k).wait_send()


class Gather:
    def __init__(self, own, buffer, sems):
        self.own, self.buffer = own, buffer
        self.gs, self.gr, self.fs, self.fr = sems
        self.grp, self.tp = place()
        self.core, self.chip = self.tp // HALF, lax.rem(self.tp, HALF)
        self.partner = lax.rem(self.tp + HALF, TP)

    def to_peer(self, k):
        if isinstance(k, int) and k == 0:
            target = self.partner
        else:
            target = self.core * HALF + across(self.chip, k)
        return remote(self.own, self.buffer.at[self.tp], self.gs.at[k], self.gr.at[k], (self.grp, target))

    def start(self, local):
        pltpu.make_async_copy(self.own, self.buffer.at[self.tp], local).start()
        for k in (1, 2, 3, 0):
            self.to_peer(k).start()
        pltpu.make_async_copy(self.own, self.buffer.at[self.tp], local).wait()

    def pass_on(self, k):
        source = self.core * HALF + across(self.chip, k)
        block = self.buffer.at[source]
        return remote(block, block, self.fs.at[k], self.fr.at[k], (self.grp, self.partner))

    def arrived(self, source, sem):
        block = self.buffer.at[source]
        remote(block, block, sem, sem, (self.grp, self.partner)).wait_recv()

    def wait_block(self, k):
        self.arrived(self.core * HALF + across(self.chip, k), self.gr.at[k])
        self.pass_on(k).start()

    def wait_partner(self):
        self.arrived(self.partner, self.gr.at[0])

    def wait_passed(self, k):
        self.arrived((1 - self.core) * HALF + across(self.chip, k), self.fr.at[k])

    def settle(self, k, work):
        block = across(self.chip, k)
        for other in range(2):
            work[other] = self.buffer[pick(self.core, other) * HALF + block]

    def drain(self):
        for k in range(HALF):
            self.to_peer(k).wait_send()
        for k in range(1, HALF):
            self.pass_on(k).wait_send()


def greet_plane():
    grp, tp = place()
    core, chip = tp // HALF, lax.rem(tp, HALF)
    targets = [lax.rem(tp + HALF, TP)] + [core * HALF + across(chip, k) for k in range(1, HALF)]
    greet([(grp, target) for target in targets])


def first_kernel(head_dim, lens, xg, w, wo, vec, rot, own,
                 out, xnext, qkv_h, prob_h, ctx_h, act_h, slope_h,
                 qkv, prob, ctx, act, slope, both, met, landed, keep, *sems):
    grp, tp = place()
    core, chip = tp // HALF, lax.rem(tp, HALF)
    local, ff = wo.shape[0], act.shape[2]
    swap = Exchange(both, met, landed, sems)
    kept = [(qkv, qkv_h), (prob, prob_h), (ctx, ctx_h), (act, act_h), (slope, slope_h)]
    greet_plane()
    b_in, b_up = bias_slices(vec, tp, local, ff)

    def one(seq):
        part, mixed, probs, context, active, sl = seq_forward(
            xg[seq], lens[seq], head_dim, w, wo, vec, b_in, b_up, rot
        )
        for i, piece in enumerate(mixed):
            qkv[seq, :, i * local : (i + 1) * local] = piece
        for h, p in enumerate(probs):
            prob[seq, h] = p
        ctx[seq] = context
        act[seq] = active
        slope[seq] = sl
        return part

    for k in reversed(range(HALF)):
        block = across(chip, k)

        def part_of(other, carry):
            both[other, k] = one(pick(core, other) * HALF + block).astype(BF)
            return carry

        lax.fori_loop(0, 2, part_of, 0)
        swap.to_partner(k).start()
        if k + 1 < HALF:
            swap.hand_over(k + 1)
    swap.hand_over(0)
    saved = [pltpu.make_async_copy(a, b, keep.at[i]) for i, (a, b) in enumerate(kept)]
    for copy in saved:
        copy.start()
    swap.wait_landed()

    def finish(at):
        result = (own[at].astype(F32) + swap.total(at) + (vec[7:8] + vec[12:13])).astype(BF)
        out[at] = result
        centred, scale = norm_parts(result.astype(F32))
        xnext[at] = (centred * scale).astype(BF)

    chunks(own.shape[0], finish)
    swap.drain()
    for copy in saved:
        copy.wait()


def first_layer(head_dim, lens, xg, w, wo, vec, rot, own):
    seqs, rows, width = xg.shape
    local = wo.shape[0]
    ff = (w.shape[1] - 3 * local) // 2
    dma = pltpu.SemaphoreType.DMA
    kept = [
        (seqs, rows, 3 * local), (seqs, local // head_dim, rows, rows), (seqs, rows, local), (seqs, rows, ff),
        (seqs, rows, ff),
    ]
    block = pltpu.VMEM((HALF, rows, width), BF)
    pair = pltpu.VMEM((2, HALF, rows, width), BF)
    return pl.pallas_call(
        functools.partial(first_kernel, head_dim),
        out_shape=[jax.ShapeDtypeStruct((rows, width), BF)] * 2 + [jax.ShapeDtypeStruct(s, BF) for s in kept],
        in_specs=[VMEM] * 7,
        out_specs=[VMEM] * 2 + [ANY] * 5,
        scratch_shapes=[pltpu.VMEM(s, BF) for s in kept] + [pair, block, block] + [dma((5,))] + [dma((HALF,))] * 4,
        compiler_params=pltpu.CompilerParams(
            collective_id=2, has_side_effects=True, vmem_limit_bytes=VMEM_BYTES
        ),
        name="first_layer",
    )(lens, xg, w, wo, vec, rot, own)


def weight_grads(xg, gg, mixes, act, ctx, w, vec, sums, packed, out_grad, vrows, grad_rows, tp):
    local, width = out_grad.shape[0] * out_grad.shape[1], out_grad.shape[2]
    total, shard, cols = packed.shape
    ff = act.shape[2]
    split = 3 * local
    rows = xg.shape[0] * xg.shape[1]
    flat = lambda ref, cut: ref[:, :, cut].reshape(rows, -1)
    everything = slice(None)
    col_sums = jnp.sum(sums[...], axis=0, keepdims=True)
    half = width // 2
    ones = jnp.ones((8, split), F32)
    wide = jnp.ones((8, ff), F32)
    exact = lambda a, b: lax.dot_general(a, b, NT, preferred_element_type=F32, precision=lax.Precision.HIGHEST)
    for c in range(2):
        cut = slice(c * half, (c + 1) * half)
        lines = slice(c * half // shard, (c + 1) * half // shard)
        gains = vec[0:4, cut].T
        cross = tn_dot(flat(xg, cut), flat(mixes, everything))
        in_cross, up_cross = cross[:, :split], cross[:, split:]
        in_grad = gains[:, 0:1] * in_cross + gains[:, 1:2] * col_sums[:, :split]
        up_grad = gains[:, 2:3] * up_cross + gains[:, 3:4] * col_sums[:, split:]
        down_grad = tn_dot(flat(gg, cut), flat(act, everything))
        packed[lines, :, :split] = in_grad.astype(BF).reshape(-1, shard, split)
        packed[lines, :, split : split + ff] = up_grad.astype(BF).reshape(-1, shard, ff)
        packed[lines, :, split + ff :] = down_grad.astype(BF).reshape(-1, shard, ff)
        w_in = w[cut, :split].astype(F32)
        w_up = w[cut, split : split + ff].astype(F32)
        norm_rows = [
            exact(ones, w_in * in_cross)[0:1],
            exact(jnp.broadcast_to(col_sums[:, :split], (8, split)), w_in)[0:1],
            exact(wide, w_up * up_cross)[0:1],
            exact(jnp.broadcast_to(col_sums[:, split:], (8, ff)), w_up)[0:1],
        ]
        for i, line in enumerate(norm_rows):
            for j in range(half // 128):
                vrows[i * (width // 128) + c * (half // 128) + j] = line[:, j * 128 : (j + 1) * 128]
        part = tn_dot(flat(ctx, everything), flat(gg, cut)).astype(BF)
        out_grad[:, :, cut] = part.reshape(-1, shard, half)
    per = width // 128
    base = 4 * per

    def clear(i, carry):
        vrows[base + i] = jnp.zeros((1, 128), F32)
        return carry

    lax.fori_loop(0, vrows.shape[0] - base, clear, 0)
    step = local // 128
    for i in range(3):
        for j in range(step):
            vrows[base + i * per + tp * step + j] = col_sums[:, i * local + j * 128 : i * local + (j + 1) * 128]
    base = 8 * per
    for j in range(ff // 128):
        vrows[base + tp * (ff // 128) + j] = col_sums[:, split + j * 128 : split + (j + 1) * 128]
    bias = jnp.sum(grad_rows.astype(F32), axis=0, keepdims=True)
    for j in range(per):
        vrows[7 * per + j] = bias[:, j * 128 : (j + 1) * 128]
        vrows[12 * per + j] = bias[:, j * 128 : (j + 1) * 128]


def second_kernel(head_dim, lens, xown, gg, w, wo, vec, rot, hidden,
                  out, grad_next, packed, out_grad, vrows,
                  xg, work, mixes, act, ctx, sums, both, met, landed, both_e, met_e, landed_e,
                  loc, *sems):
    grp, tp = place()
    core, chip = tp // HALF, lax.rem(tp, HALF)
    local, ff = wo.shape[0], act.shape[2]
    swap = Exchange(both, met, landed, sems[0:4])
    swap_e = Exchange(both_e, met_e, landed_e, sems[4:8])
    gather = Gather(xown, xg, sems[8:12])
    greet_plane()
    gather.start(loc.at[0])
    sums[...] = jnp.zeros_like(sums)
    b_in, b_up = bias_slices(vec, tp, local, ff)

    def one(other, seq):
        part, mixed, probs, context, active, sl = seq_forward(
            work[other], lens[seq], head_dim, w, wo, vec, b_in, b_up, rot
        )
        ctx[seq] = context
        act[seq] = active
        back, mixed_grad, expanded_grad = seq_backward(
            gg[seq], mixed, probs, sl, head_dim, w, wo, vec, rot
        )
        mixes[seq, :, : 3 * local] = mixed_grad
        mixes[seq, :, 3 * local :] = expanded_grad
        sums[:, : 3 * local] += fold_rows(mixed_grad)
        sums[:, 3 * local :] += fold_rows(expanded_grad)
        return part, back

    for k in range(HALF):
        if k:
            gather.wait_block(k)
            swap_e.hand_over(k - 1)
            swap.hand_over(k - 1)
            gather.wait_passed(k)
        else:
            gather.wait_partner()
        block = across(chip, k)
        gather.settle(k, work)

        def part_of(other, carry):
            part, back = one(other, pick(core, other) * HALF + block)
            both[other, k] = part.astype(BF)
            both_e[other, k] = back.astype(BF)
            return carry

        lax.fori_loop(0, 2, part_of, 0)
        swap_e.to_partner(k).start()
        swap.to_partner(k).start()
    swap_e.hand_over(HALF - 1)
    swap.hand_over(HALF - 1)
    weight_grads(xg, gg, mixes, act, ctx, w, vec, sums, packed, out_grad, vrows, gg[tp], tp)
    swap_e.wait_landed()

    def finish_back(at):
        total = swap_e.total(at)
        centred, scale = norm_parts(hidden[at].astype(F32))
        xhat = centred * scale
        mean_one = jnp.mean(total, -1, keepdims=True)
        mean_two = jnp.mean(total * xhat, -1, keepdims=True)
        grad_next[at] = (
            gg[tp, at].astype(F32) + scale * (total - mean_one - xhat * mean_two)
        ).astype(BF)

    chunks(hidden.shape[0], finish_back)
    swap.wait_landed()

    def finish(at):
        out[at] = (hidden[at].astype(F32) + swap.total(at) + (vec[7:8] + vec[12:13])).astype(BF)

    chunks(hidden.shape[0], finish)
    gather.drain()
    swap.drain()
    swap_e.drain()


def second_layer(head_dim, owners, shard, lens, xown, gg, w, wo, vec, rot, hidden):
    seqs, rows, width = gg.shape
    local = wo.shape[0]
    ff = (w.shape[1] - 3 * local) // 2
    mix = 3 * local + ff
    dma = pltpu.SemaphoreType.DMA
    block = pltpu.VMEM((HALF, rows, width), BF)
    pair = pltpu.VMEM((2, HALF, rows, width), BF)
    return pl.pallas_call(
        functools.partial(second_kernel, head_dim),
        out_shape=[
            jax.ShapeDtypeStruct((rows, width), BF),
            jax.ShapeDtypeStruct((rows, width), BF),
            jax.ShapeDtypeStruct((width // shard, shard, w.shape[1]), BF),
            jax.ShapeDtypeStruct((owners, shard, width), BF),
            jax.ShapeDtypeStruct((13 * width // 128, 1, 128), F32),
        ],
        in_specs=[VMEM] * 8,
        out_specs=[VMEM] * 5,
        scratch_shapes=[
            pltpu.VMEM((seqs, rows, width), BF),
            pltpu.VMEM((2, rows, width), BF),
            pltpu.VMEM((seqs, rows, mix), BF),
            pltpu.VMEM((seqs, rows, ff), BF),
            pltpu.VMEM((seqs, rows, local), BF),
            pltpu.VMEM((8, mix), F32),
        ]
        + [pair, block, block] * 2
        + [dma((1,))]
        + [dma((HALF,))] * 12,
        compiler_params=pltpu.CompilerParams(
            collective_id=3, has_side_effects=True, vmem_limit_bytes=VMEM_BYTES
        ),
        name="second_layer",
    )(lens, xown, gg, w, wo, vec, rot, hidden)


def vector_rows(vec_part):
    step = 128
    while vec_part % step:
        step //= 2
    return (128 - step + vec_part + 127) // 128


def third_kernel(head_dim, groups, owners, gown, w, wo, vec, rot, tokens, xg,
                 qkv_h, prob_h, ctx_h, act_h, slope_h, packed1, out_grad1, vrows1,
                 out, r0, r1, ro, rv,
                 gg, work, mixes, sums, qkv, prob, ctx, act, slope, packed0, out_grad0, vrows0,
                 both, met, landed, loc, keep, ss, sr, os, orr, vs, vr, own_sem, *sems):
    grp, tp = place()
    me = grp * TP + tp
    total = groups * TP
    core, chip = tp // HALF, lax.rem(tp, HALF)
    local, ff = wo.shape[0], act.shape[2]
    swap = Exchange(both, met, landed, sems[0:4])
    gather = Gather(gown, gg, sems[4:8])
    kept = [(qkv_h, qkv), (prob_h, prob), (slope_h, slope), (act_h, act), (ctx_h, ctx)]
    rows_sent = rv.shape[2]
    vec_part = 13 * gown.shape[1] // total
    greet_all(groups)
    gather.start(loc.at[0])

    loads = [pltpu.make_async_copy(a, b, keep.at[i]) for i, (a, b) in enumerate(kept)]
    for copy in loads:
        copy.start()

    def to(step):
        other = lax.rem(me + step, total)
        return other // TP, lax.rem(other, TP), other

    def block_copy(layer, source, landing, step):
        g, t, other = to(step)
        return remote(source.at[other], landing.at[me], ss.at[layer, step], sr.at[layer, step], (g, t))

    def vec_copy(layer, source, step):
        g, t, other = to(step)
        first = (other * vec_part) // 128
        return remote(
            source.at[pl.ds(first, rows_sent)], rv.at[layer, me], vs.at[layer, step], vr.at[layer, step], (g, t)
        )

    def own_copies(layer, source, landing, vrows):
        first = (me * vec_part) // 128
        return [
            pltpu.make_async_copy(source.at[me], landing.at[me], own_sem.at[layer, 0]),
            pltpu.make_async_copy(vrows.at[pl.ds(first, rows_sent)], rv.at[layer, me], own_sem.at[layer, 1]),
        ]

    def out_copy(layer, source, j):
        owner = tp * owners + j
        return remote(
            source.at[j], ro.at[layer, grp], os.at[layer, j], orr.at[layer, grp], (owner // TP, lax.rem(owner, TP))
        )

    def send(layer, source, landing, out_grad, vrows):
        def start_all(step, carry):
            vec_copy(layer, vrows, step).start()
            block_copy(layer, source, landing, step).start()
            return carry

        lax.fori_loop(1, total, start_all, 0)
        for copy in own_copies(layer, source, landing, vrows):
            copy.start()
        for j in range(owners):
            owner = tp * owners + j

            @pl.when(owner != me)
            def _():
                out_copy(layer, out_grad, j).start()

            @pl.when(owner == me)
            def _():
                pltpu.make_async_copy(out_grad.at[j], ro.at[layer, grp], orr.at[layer, grp]).start()

    def collect(layer, source, landing, out_grad, vrows):
        def wait_all(step, carry):
            vec_copy(layer, vrows, step).wait()
            block_copy(layer, source, landing, step).wait()
            return carry

        lax.fori_loop(1, total, wait_all, 0)
        for copy in own_copies(layer, source, landing, vrows):
            copy.wait()
        for j in range(owners):
            owner = tp * owners + j

            @pl.when(owner != me)
            def _():
                out_copy(layer, out_grad, j).wait_send()

        for g in range(groups):
            pltpu.make_async_copy(out_grad.at[0], ro.at[layer, g], orr.at[layer, g]).wait()

    send(1, packed1, r1, out_grad1, vrows1)
    sums[...] = jnp.zeros_like(sums)
    for copy in loads[:3]:
        copy.wait()

    def one(other, seq):
        mixed = [qkv[seq, :, i * local : (i + 1) * local] for i in range(3)]
        probs = [prob[seq, h] for h in range(local // head_dim)]
        back, mixed_grad, expanded_grad = seq_backward(
            work[other], mixed, probs, slope[seq], head_dim, w, wo, vec, rot
        )
        mixes[seq, :, : 3 * local] = mixed_grad
        mixes[seq, :, 3 * local :] = expanded_grad
        sums[:, : 3 * local] += fold_rows(mixed_grad)
        sums[:, 3 * local :] += fold_rows(expanded_grad)
        return back

    for k in range(HALF):
        if k:
            gather.wait_block(k)
            swap.hand_over(k - 1)
            gather.wait_passed(k)
        else:
            gather.wait_partner()
        block = across(chip, k)
        gather.settle(k, work)

        def part_of(other, carry):
            both[other, k] = one(other, pick(core, other) * HALF + block).astype(BF)
            return carry

        lax.fori_loop(0, 2, part_of, 0)
        swap.to_partner(k).start()
    for copy in loads[3:]:
        copy.wait()
    weight_grads(xg, gg, mixes, act, ctx, w, vec, sums, packed0, out_grad0, vrows0, gg[tp], tp)
    send(0, packed0, r0, out_grad0, vrows0)
    swap.hand_over(HALF - 1)
    swap.wait_landed()

    def finish_back(at):
        value = swap.total(at)
        centred, scale = norm_parts(tokens[at].astype(F32))
        xhat = centred * scale
        mean_one = jnp.mean(value, -1, keepdims=True)
        mean_two = jnp.mean(value * xhat, -1, keepdims=True)
        out[at] = (gg[tp, at].astype(F32) + scale * (value - mean_one - xhat * mean_two)).astype(BF)

    chunks(tokens.shape[0], finish_back)
    gather.drain()
    swap.drain()
    collect(1, packed1, r1, out_grad1, vrows1)
    collect(0, packed0, r0, out_grad0, vrows0)


def third_layer(head_dim, groups, gown, w, wo, vec, rot, tokens, xg, kept, packed1, out_grad1, vrows1):
    seqs, rows, width = xg.shape
    local = wo.shape[0]
    ff = (w.shape[1] - 3 * local) // 2
    mix = 3 * local + ff
    total = groups * TP
    owners, shard = out_grad1.shape[:2]
    dma = pltpu.SemaphoreType.DMA
    block = pltpu.VMEM((HALF, rows, width), BF)
    pair = pltpu.VMEM((2, HALF, rows, width), BF)
    sent = vector_rows(13 * width // total)
    return pl.pallas_call(
        functools.partial(third_kernel, head_dim, groups, owners),
        out_shape=[
            jax.ShapeDtypeStruct((rows, width), BF),
            jax.ShapeDtypeStruct(packed1.shape, BF),
            jax.ShapeDtypeStruct(packed1.shape, BF),
            jax.ShapeDtypeStruct((LAYERS, groups, shard, width), BF),
            jax.ShapeDtypeStruct((LAYERS, total, sent, 1, 128), F32),
        ],
        in_specs=[VMEM] * 7 + [ANY] * 8,
        out_specs=[VMEM] + [ANY] * 4,
        scratch_shapes=[
            pltpu.VMEM((seqs, rows, width), BF),
            pltpu.VMEM((2, rows, width), BF),
            pltpu.VMEM((seqs, rows, mix), BF),
            pltpu.VMEM((8, mix), F32),
        ]
        + [pltpu.VMEM(a.shape, BF) for a in kept]
        + [pltpu.VMEM(packed1.shape, BF), pltpu.VMEM(out_grad1.shape, BF), pltpu.VMEM(vrows1.shape, F32)]
        + [pair, block, block]
        + [
            dma((1,)), dma((5,)), dma((LAYERS, total)), dma((LAYERS, total)),
            dma((LAYERS, owners)), dma((LAYERS, groups)), dma((LAYERS, total)), dma((LAYERS, total)),
            dma((LAYERS, 2)),
        ]
        + [dma((HALF,))] * 8,
        compiler_params=pltpu.CompilerParams(
            collective_id=4, has_side_effects=True, vmem_limit_bytes=VMEM_BYTES
        ),
        name="third_layer",
    )(gown, w, wo, vec, rot, tokens, xg, *kept, packed1, out_grad1, vrows1)


def adam_kernel(groups, local, ff, fixes, r0, r1, ro, *refs):
    params, moments, squares = refs[0:4], refs[4:8], refs[8:12]
    grads, changes, new_moments, new_squares = refs[12:16], refs[16:20], refs[20:24], refs[24:28]
    first_fix, second_fix = fixes[0], fixes[1]

    def update(which, at, gradient):
        moment = BETA_FIRST * moments[which][0, :, at] + (1.0 - BETA_FIRST) * gradient
        square = BETA_SECOND * squares[which][0, :, at] + (1.0 - BETA_SECOND) * gradient * gradient
        grads[which][0, :, at] = gradient
        new_moments[which][0, :, at] = moment
        new_squares[which][0, :, at] = square
        changes[which][0, :, at] = -LEARNING * (
            moment / first_fix / (jnp.sqrt(square / second_fix) + ADAM_EPSILON)
            + DECAY_RATE * params[which][0, :, at]
        )

    def layer(source):
        for p in range(TP):
            value = source[p].astype(F32)
            for g in range(1, groups):
                value = value + source[g * TP + p].astype(F32)
            for i in range(3):
                start = i * TP * local + p * local
                update(0, slice(start, start + local), value[:, i * local : (i + 1) * local])
            split = 3 * local
            at = slice(p * ff, (p + 1) * ff)
            update(2, at, value[:, split : split + ff])
            update(3, at, value[:, split + ff :])
        value = ro[0, 0].astype(F32)
        for g in range(1, groups):
            value = value + ro[0, g].astype(F32)
        update(1, slice(None), value)

    @pl.when(pl.program_id(0) == 0)
    def _():
        layer(r0)

    @pl.when(pl.program_id(0) == 1)
    def _():
        layer(r1)


def adam_step(groups, local, ff, fixes, r0, r1, ro, params, moments, squares):
    shard = ro.shape[2]
    part = 8
    specs = [pl.BlockSpec((1, part, a.shape[2]), lambda l, r: (l, r, 0)) for a in params]
    source = lambda layer: pl.BlockSpec(
        (r0.shape[0], part, r0.shape[2]), lambda l, r: (0, jnp.where(l == layer, r, (1 - layer) * (shard // part - 1)), 0)
    )
    outs = [jax.ShapeDtypeStruct(a.shape, F32) for a in params]
    return pl.pallas_call(
        functools.partial(adam_kernel, groups, local, ff),
        grid=(LAYERS, shard // part),
        in_specs=[SMEM, source(0), source(1), pl.BlockSpec((1, groups, part, ro.shape[3]), lambda l, r: (l, 0, r, 0))]
        + specs * 3,
        out_specs=specs * 4,
        out_shape=outs * 4,
        compiler_params=pltpu.CompilerParams(vmem_limit_bytes=VMEM_BYTES),
        name="adam_step",
    )(fixes, r0, r1, ro, *params, *moments, *squares)


def rotary(row_count, width, head_dim):
    rot_dim = head_dim // 4
    half_rot = rot_dim // 2
    column = jnp.arange(width, dtype=jnp.int32) % head_dim
    freq_slot = (column % half_rot).astype(F32)
    frequency = 10000.0 ** (-(freq_slot * 2.0) / rot_dim)
    angles = jnp.arange(row_count, dtype=F32)[:, None] * frequency[None, :]
    inside = (column < rot_dim)[None, :]
    first_half = (column < half_rot)[None, :]
    sine = jnp.sin(angles)
    return jnp.stack(
        [
            jnp.where(inside, jnp.cos(angles), 1.0),
            jnp.where(first_half, -sine, 0.0),
            jnp.where(inside & jnp.logical_not(first_half), sine, 0.0),
        ]
    )


def standard(values):
    centred = values - jnp.mean(values, -1, keepdims=True)
    return centred * lax.rsqrt(jnp.mean(centred * centred, -1, keepdims=True) + NORM_EPSILON)


def adam_update(weight, moment, square, gradient, first_fix, second_fix):
    moment = BETA_FIRST * moment + (1.0 - BETA_FIRST) * gradient
    square = BETA_SECOND * square + (1.0 - BETA_SECOND) * gradient * gradient
    change = -LEARNING * (
        moment / first_fix / (jnp.sqrt(square / second_fix) + ADAM_EPSILON) + DECAY_RATE * weight
    )
    return (change, moment, square)


def per_device(
    groups,
    tokens,
    cotangent,
    seq_lengths,
    seq_device,
    step_count,
    *state,
):
    params, moments, squares = state[0:5], state[5:10], state[10:15]
    attend_in, attend_out, expand_weight, reduce_weight, layer_vectors = params
    grp, tp = place()
    me = grp * TP + tp
    total = groups * TP
    rows, width = tokens.shape
    shard = attend_in.shape[1]
    head_dim = width // HEADS
    local = width // TP
    ff = expand_weight.shape[2] // TP
    vec_part = layer_vectors.shape[1]
    owners = local // shard
    plane_ids = grp * TP + jnp.arange(TP, dtype=jnp.int32)
    lens = jnp.sum(jnp.where(plane_ids[:, None] == seq_device[None, :], seq_lengths[None, :], 0), 1)
    lens = jnp.broadcast_to(lens[:, None, None], (TP, 1, rows))
    own_length = jnp.sum(jnp.where(seq_device == me, seq_lengths, 0))
    valid = jnp.arange(rows, dtype=jnp.int32)[:, None] < own_length
    rot = rotary(rows, local, head_dim)

    blocks = [
        jnp.concatenate(
            [
                attend_in[l].astype(BF).reshape(shard, 3, TP, local).transpose(2, 0, 1, 3).reshape(TP, shard, 3 * local),
                expand_weight[l].astype(BF).reshape(shard, TP, ff).transpose(1, 0, 2),
                reduce_weight[l].astype(BF).reshape(shard, TP, ff).transpose(1, 0, 2),
            ],
            2,
        )
        for l in range(LAYERS)
    ]
    vec = jnp.pad(layer_vectors.astype(BF).astype(F32).reshape(-1), (0, 8 * 128 - 2 * vec_part)).reshape(8, 128)
    xhat_own = standard(tokens.astype(F32)).astype(BF)
    grad_own = jnp.where(valid, cotangent, jnp.zeros_like(cotangent))
    grads_all = lax.all_gather(grad_own, "tp", axis=0)
    xg, w0, w1, wog, vecg = spread(groups, xhat_own, blocks[0], blocks[1], attend_out.astype(BF), vec)
    w1, grads_all = lax.optimization_barrier((w1, grads_all))
    w1 = lax.all_gather(w1, "grp", axis=0).reshape(width, -1)
    w0 = w0.reshape(width, -1)
    out_rows = wog.transpose(1, 0, 2, 3).reshape(LAYERS, local, width)
    vectors = vecg.reshape(total, -1)[:, : 2 * vec_part].reshape(total, LAYERS, vec_part)
    vectors = vectors.transpose(1, 0, 2).reshape(LAYERS, 13, width)
    vectors = jnp.pad(vectors, ((0, 0), (0, 3), (0, 0)))

    hidden0, xnext, *kept = first_layer(
        head_dim, lens, xg, w0, out_rows[0], vectors[0], rot, tokens
    )
    hidden1, grad0, packed1, out_grad1, vrows1 = second_layer(
        head_dim, owners, shard, lens, xnext, grads_all, w1, out_rows[1], vectors[1], rot, hidden0
    )
    input_grad, r0, r1, ro, rv = third_layer(
        head_dim, groups, grad0, w0, out_rows[0], vectors[0], rot, tokens, xg, kept, packed1, out_grad1, vrows1
    )
    step_float = step_count[0].astype(F32)
    first_fix = 1.0 - jnp.power(BETA_FIRST, step_float)
    second_fix = 1.0 - jnp.power(BETA_SECOND, step_float)
    big = adam_step(
        groups, local, ff, jnp.stack([first_fix, second_fix]), r0, r1, ro, params[:4], moments[:4], squares[:4]
    )
    vec_rows = jnp.sum(rv, 1).reshape(LAYERS, -1)
    grad_vec = lax.dynamic_slice_in_dim(vec_rows, lax.rem(me * vec_part, 128), vec_part, 1)
    small = (grad_vec,) + adam_update(params[4], moments[4], squares[4], grad_vec, first_fix, second_fix)
    results = []
    for i in range(4):
        results += list(big[4 * i : 4 * i + 4]) + [small[i]]
    return (jnp.stack([hidden0, hidden1]), input_grad, *results)


def solution(mesh):
    devices = mesh.devices.reshape(-1, TP)
    groups = devices.shape[0]
    flat = Mesh(devices, ("grp", "tp"))
    axes = ("grp", "tp")
    by_row = P(axes, None)
    by_dim = [P(None, axes, None)] * 4 + [P(None, axes)]
    return jax.shard_map(
        functools.partial(per_device, groups),
        mesh=flat,
        in_specs=(by_row, by_row, P(), P(), P(), *(by_dim * 3)),
        out_specs=(P(None, axes, None), by_row, *(by_dim * 4)),
        check_vma=False,
    )
```

time: 572 us -> 445 us (0.78)
  Pallas kernels: 422 us -> 393 us
  other arithmetic: 38.5 us -> 13.7 us
  matrix products: 24.2 us -> 0 us
  local copies, waits for them, and re-layouts: 30.9 us -> 7.82 us
  waiting for transfers between devices: 32.9 us -> 9.9 us
    pallas_call x8 -> x4, Pallas kernels: 334 us -> 296 us  [the longest x1 152 us: third_layer(): pl.pallas_call(functools.partial(third_kernel, head_dim, groups, owners),...]
    reduce_scatter x2 -> x0, waiting for transfers between devices: 32.8 us -> none  [the longest x1 32.8 us: per_device(): lax.psum_scatter(packed1, 'grp', scatter_dimension=0, tiled=True)]
    dot_general x6 -> x0, matrix products: 24.2 us -> none  [tn_dot(): return lax.dot_general(a, b, TN, preferred_element_type=F32)]
    all_gather x1, waiting for transfers between devices: 0.02 us -> 9.85 us  [per_device(): w1 = lax.all_gather(w1, 'grp', axis=0).reshape(width, -1)]
    pallas_call x1, Pallas kernels: 88.2 us -> 97.5 us  [spread(): pl.pallas_call(functools.partial(spread_kernel, groups, owners), out_shap...]
    reduce_sum x11 -> x1, other arithmetic: 9.84 us -> 1.01 us  [per_device(): vec_rows = jnp.sum(rv, 1).reshape(LAYERS, -1)]
    another operation x13 -> x0, local copies, waits for them, and re-layouts: 8.18 us -> none  [the longest x3 3.6 us: per_device(): jnp.stack([s[:, :, split:split + ff].transpose(1, 0, 2).reshape(shard, -1...]
    mul x5 -> x1, other arithmetic: 7.82 us -> 0.69 us  [adam_update(): -LEARNING]
  transfers between devices with their start and end apart: 4 -> 2, of which waited for: 1 -> 1; matrix products, arithmetic and copies ran while one was open for 9% -> 3% of each run, Pallas kernels for 45% -> 31%
where the time goes in v2:
time: 445 us; the launch traced here: 440 us
  Pallas kernels  393 us (88%)
  between operations  15.4 us (3%)
  other arithmetic  13.7 us (3%)
  waiting for transfers between devices  9.9 us (2%)
  local copies, waits for them, and re-layouts  7.82 us (2%)
    pallas_call x1, Pallas kernels, third_layer(): pl.pallas_call(functools.partial(third_kernel, head_dim, groups, owners),...  152 us
    pallas_call x1, Pallas kernels, spread(): pl.pallas_call(functools.partial(spread_kernel, groups, owners), out_shap...  97.5 us
    pallas_call x1, Pallas kernels, second_layer(): pl.pallas_call(functools.partial(second_kernel, head_dim), out_shape=[jax...  89.8 us
    pallas_call x1, Pallas kernels, first_layer(): pl.pallas_call(functools.partial(first_kernel, head_dim), out_shape=[jax....  40.8 us
    pallas_call x1, Pallas kernels, adam_step(): pl.pallas_call(functools.partial(adam_kernel, groups, local, ff), grid=(L...  12.9 us
    all_gather x1, waiting for transfers between devices, per_device(): w1 = lax.all_gather(w1, 'grp', axis=0).reshape(width, -1)  9.85 us
  transfers between devices with their start and end apart: 2, of which 1 were waited for; matrix products, arithmetic and copies ran while one was open for 3% of the time, Pallas kernels for 31%

profile of v2, /device:TPU:1, one launch (start us, length us, event | category | flops | bytes accessed | tf_op | source)
XLA Modules:
  0.0 440.1 jit_solution(16882648371530855788)
XLA Ops:
  7.2 0.0 copy-start.2
  7.2 0.0 all-gather.5.cloned.1.call-start
  7.3 1.4 fusion.14
  8.6 0.6 iota_compare_fusion
  9.3 1.9 broadcast_select_fusion
  11.2 0.0 all-gather.5.cloned.1.call-update
  11.3 0.0 copy-start.1
  11.3 0.0 all-gather.7.cloned.1.call-start
  11.3 0.0 copy-done.2
  11.3 0.1 convert.17
  11.4 0.1 copy.69
  11.5 1.0 copy-done.1
  12.5 0.1 convert.18
  12.6 0.1 copy.70
  12.7 0.9 copy-done.3
  13.8 0.0 copy-start.5
  13.8 0.1 copy.81
  13.9 0.0 copy-start.9
  13.9 0.0 copy-start
  13.9 0.2 reshape.336
  14.1 0.1 copy.66
  14.2 0.1 copy.67
  14.3 0.1 copy.82
  14.4 0.2 reshape.335
  14.6 0.1 copy-done.5
  14.7 0.7 convert_element_type.70.wo
  15.4 0.0 copy-done.9
  15.4 0.1 reshape.337
  15.5 0.6 bitcast_convert_fusion.vec
  16.1 0.0 copy-done
  16.1 0.1 convert_reduce_fusion
  16.2 0.3 fusion.2
  16.5 0.2 copy_bitcast_fusion
  16.7 0.2 copy_bitcast_fusion.3
  16.9 0.9 pad_maximum_fusion.2.s1
  17.8 0.9 pad_maximum_fusion.1.s0
  18.7 1.0 fusion.3.xh
  19.8 97.5 %spread.1 = (bf16[8,256,1024]{2,1,0:T(8,128)(2,1)}, bf16[32,32,1408]{2,1,0:T(8,128)(2,1)}, bf16[8,32,1408]{2,1,0:T(8,128)(2,1)}, bf16[4,2,32,1024]{3,2,1,0:T(8,128)(2,1)}, f32[32,8,128]{2,1,0:T(8,128)}) custom-call(bf16[256,1024]{1,0:T(8,128)(2,1)} %fusion.3.xh, bf16[8,32,1408]{2,1,0:T(8,128)(2,1)} %pad_maximum_fusion.1.s0, ...), custom_call_target="tpu_custom_call" | custom-call | tf_op jit(solution)/shard_map/spread/pallas_call | solution.py:186
  117.3 0.0 all-gather.5.cloned.1.call-done
  117.4 0.0 all-gather.7.cloned.1.call-update
  117.4 1.0 copy.83
  118.4 0.2 reshape.342
  118.6 0.1 reshape.343
  119.5 0.2 select_reduce_fusion
  119.7 0.7 fusion.7
  120.4 0.5 cosine_select_fusion
  120.9 0.8 pad_maximum_fusion.3.rot
  121.7 0.8 fusion.17
  122.5 0.7 broadcast_in_dim.71.lens
  123.2 40.8 %first_layer.1 = (bf16[256,1024]{1,0:T(8,128)(2,1)}, bf16[256,1024]{1,0:T(8,128)(2,1)}, bf16[8,256,384]{2,1,0:T(8,128)(2,1)}, bf16[8,2,256,256]{3,2,1,0:T(8,128)...) custom-call(s32[8,1,256]{2,1,0:T(1,128)} %broadcast_in_dim.71.lens, ...), custom_call_target="tpu_custom_call" | custom-call | tf_op jit(solution)/shard_map/first_layer/pallas_call | solution.py:500
  164.0 0.7 pad_maximum_fusion.4.fixes
  164.7 9.8 %all-gather.7.cloned.1.call-done = bf16[32,32,1408]{2,1,0:T(8,128)(2,1)} async-done(((bf16[8,32,1408]{2,1,0:T(8,128)(2,1)}), bf16[32,32,1408]{2,1,0:T(8,128)(2,1)}) %all-gather.7.cloned.1.call-update) | async-done | bytes 2883600 | tf_op jit(solution)/shard_map/all_gather | solution.py:1021
  174.5 89.8 %second_layer.1 = (bf16[256,1024]{1,0:T(8,128)(2,1)}, bf16[256,1024]{1,0:T(8,128)(2,1)}, bf16[32,32,1408]{2,1,0:T(8,128)(2,1)}, bf16[4,32,1024]{2,1,0:T(8,128)(2,1)}, f32[104,1,128]{2,1,0:T(1,128)}) custom-call(s32[8,1,256]{2,1,0:T(1,128)} %broadcast_in_dim.71.lens, bf16[256,1024]{1,0:T(8,128)(2,1)} %get-tuple-element.67.xown, ...), custom_call_target="tpu_custom_call" | custom-call | tf_op jit(solution)/shard_map/second_layer/pallas_call | solution.py:657
  264.3 0.0 copy-start.4
  264.3 0.0 copy-start.8
  264.3 152.2 %third_layer.1 = (bf16[256,1024]{1,0:T(8,128)(2,1)}, bf16[32,32,1408]{2,1,0:T(8,128)(2,1)}, bf16[32,32,1408]{2,1,0:T(8,128)(2,1)}, bf16[2,4,32,1024]{3,2,1,0:T(8,128)(2,1)}, f32[2,32,4,1,128]{4,3,2,1,0:T(1,128)}) custom-call(bf16[256,1024]{1,0:T(8,128)(2,1)} %get-tuple-element.72.gown, bf16[1024,1408]{1,0:T(8,128)(2,1)} %bitcast.63, ...), custom_call_target="tpu_custom_call" | custom-call | tf_op jit(solution)/shard_map/third_layer/pallas_call | solution.py:848
  416.6 0.0 copy-start.10
  416.6 0.0 copy-start.11
  416.6 1.0 reduce_sum.49
  417.6 0.0 copy-done.4
  417.6 1.1 pad_maximum_fusion
  418.7 0.7 add_multiply_fusion
  419.4 12.9 %adam_step.1 = (f32[2,32,3072]{2,1,0:T(8,128)}, f32[2,32,1024]{2,1,0:T(8,128)}, f32[2,32,4096]{2,1,0:T(8,128)}, f32[2,32,4096]{2,1,0:T(8,128)}, f32[2,32,3072]{2...) custom-call(f32[2]{0:T(128)} %pad_maximum_fusion.4.fixes, ...), custom_call_target="tpu_custom_call" | custom-call | tf_op jit(solution)/shard_map/adam_step/pallas_call | solution.py:931
  432.3 0.8 copy.87
  (28 shorter events, 0.3 us)
Async XLA Ops:
  7.2 4.1 copy-start.2
  7.2 110.1 %all-gather.5.cloned.1.call-start = ((), (), s32[]{:S(2)}) async-start(), calls=%async_computation | async-start | bytes 4718592 | tf_op jit(solution)/shard_map/all_gather | solution.py:1018
  11.3 1.2 copy-start.1
  11.3 163.2 %all-gather.7.cloned.1.call-start = ((), (), s32[]{:S(2)}) async-start(), calls=%async_computation.1 | async-start | bytes 3604480 | tf_op jit(solution)/shard_map/all_gather | solution.py:1021
  12.5 1.1 copy-start.3
  13.8 1.0 copy-start.5
  13.9 1.5 copy-start.9
  13.9 2.2 copy-start
  19.8 99.8 %copy-start.12 = (s32[32]{0:T(128)S(1)}, s32[32]{0:T(128)}, u32[]{:S(2)}) copy-start(s32[32]{0:T(128)} %param.22) | copy-start | bytes 388
  19.8 99.8 %copy-start.13 = (s32[32]{0:T(128)S(1)}, s32[32]{0:T(128)}, u32[]{:S(2)}) copy-start(s32[32]{0:T(128)} %param.23) | copy-start | bytes 388
  117.3 4.3 copy-start.6
  264.3 153.3 %copy-start.4 = (bf16[256,1024]{1,0:T(8,128)(2,1)S(1)}, bf16[256,1024]{1,0:T(8,128)(2,1)}, u32[]{:S(2)}) copy-start(bf16[256,1024]{1,0:T(8,128)(2,1)} %get-tuple-element.66.hidden) | copy-start | bytes 1572868
  264.3 153.3 %copy-start.8 = (bf16[256,1024]{1,0:T(8,128)(2,1)S(1)}, bf16[256,1024]{1,0:T(8,128)(2,1)}, u32[]{:S(2)}) copy-start(bf16[256,1024]{1,0:T(8,128)(2,1)} %get-tuple-element.71) | copy-start | bytes 1572868
  416.6 2.1 copy-start.10
  416.6 2.1 copy-start.11
  419.4 12.9 %copy-start.7 = (bf16[256,1024]{1,0:T(8,128)(2,1)S(1)}, bf16[256,1024]{1,0:T(8,128)(2,1)}, u32[]{:S(2)}) copy-start(bf16[256,1024]{1,0:T(8,128)(2,1)} %get-tuple-element.148) | copy-start | bytes 1572868
Sparse Core Ops, SparseCore 0:
  11.4 93.3 all-gather.4
  117.5 56.9 all-gather.6

commit v3 on v2

--- a/solution.py
+++ b/solution.py
@@ -28,11 +28,41 @@
 ANY = pl.BlockSpec(memory_space=pl.ANY)
 VMEM = pl.BlockSpec(memory_space=pltpu.VMEM)
 SMEM = pl.BlockSpec(memory_space=pltpu.SMEM)
-VMEM_BYTES = 60 * 1024 * 1024
-
-
-def place():
-    return lax.axis_index("grp"), lax.axis_index("tp")
+VMEM_BYTES = 67043328
+
+
+AXES = ("far", "near", "core", "y", "x")
+
+
+class Place:
+    def __init__(self):
+        self.far, near, core, self.y, x = (lax.axis_index(name) for name in AXES)
+        self.fars, self.ys = lax.axis_size("far"), lax.axis_size("y")
+        self.tp = core * HALF + near * 2 + x
+        self.row = near * 2 + core
+        self.x = x
+        self.core, self.chip = core, near * 2 + x
+        self.partner = (1 - core) * HALF + self.chip
+        self.groups, self.total = self.fars * self.ys, self.fars * self.ys * TP
+        self.me = self.flat(self.far, self.y, self.tp)
+
+    def flat(self, far, y, tp):
+        near, core, x = lax.rem(tp // 2, 2), tp // HALF, lax.rem(tp, 2)
+        return (((far * 2 + near) * 2 + core) * self.ys + y) * 2 + x
+
+    def device(self, tp, far=None, y=None):
+        far = self.far if far is None else far
+        y = self.y if y is None else y
+        return far, lax.rem(tp // 2, 2), tp // HALF, y, lax.rem(tp, 2)
+
+    def device_of(self, flat):
+        rest = flat // 2
+        y, rest = lax.rem(rest, self.ys), rest // self.ys
+        core, rest = lax.rem(rest, 2), rest // 2
+        return rest // 2, lax.rem(rest, 2), core, y, lax.rem(flat, 2)
+
+    def tp_of(self, row, x):
+        return (row % 2) * HALF + (row // 2) * 2 + x
 
 
 def nn_dot(a, b):
@@ -60,144 +90,168 @@
     pl.semaphore_wait(barrier, len(targets))
 
 
-def greet_all(groups):
-    grp, tp = place()
-    me = grp * TP + tp
-    total = groups * TP
+def greet_all(here):
     barrier = pltpu.get_barrier_semaphore()
 
     def signal(step, carry):
-        other = lax.rem(me + step, total)
-        pl.semaphore_signal(
-            barrier, inc=1, device_id=(other // TP, lax.rem(other, TP)), device_id_type=MESH
-        )
+        other = lax.rem(here.me + step, here.total)
+        pl.semaphore_signal(barrier, inc=1, device_id=here.device_of(other), device_id_type=MESH)
         return carry
 
-    lax.fori_loop(1, total, signal, 0)
-    pl.semaphore_wait(barrier, total - 1)
-
-
-def spread_kernel(groups, owners, xh, s0, s1, wo, vec, xg, w0, w1, wog, vecg,
-                  xs, xr, ss, sr, ts, tr, os, orr, vs, vr, loc):
-    grp, tp = place()
-    me = grp * TP + tp
-    total = groups * TP
-    core, chip = tp // HALF, lax.rem(tp, HALF)
-    partner = lax.rem(tp + HALF, TP)
-    greet_all(groups)
-    own = [
-        pltpu.make_async_copy(xh, xg.at[tp], loc.at[0]),
-        pltpu.make_async_copy(s0.at[tp], w0.at[me], loc.at[1]),
-        pltpu.make_async_copy(s1.at[tp], w1.at[tp], loc.at[2]),
-        pltpu.make_async_copy(vec, vecg.at[me], loc.at[3]),
-    ]
-    first = []
-    for step in range(1, HALF):
-        peer = core * HALF + lax.rem(chip + step, HALF)
-        first.append(remote(xh, xg.at[tp], xs.at[step], xr.at[step], (grp, peer)))
-    first.append(remote(xh, xg.at[tp], xs.at[0], xr.at[0], (grp, partner)))
-    for copy in first:
-        copy.start()
-
-    def to(step):
-        other = lax.rem(me + step, total)
-        return other // TP, lax.rem(other, TP)
-
-    def block_copy(step):
-        g, t = to(step)
-        return remote(s0.at[t], w0.at[me], ss.at[step], sr.at[step], (g, t))
+    lax.fori_loop(1, here.total, signal, 0)
+    pl.semaphore_wait(barrier, here.total - 1)
+
+
+def spread_kernel(owners, xh, s0, s1, wo, vec, xg, w0, w1, wog, vecg,
+                  ps, pr, zs, zr, ys, yr, os, orr, vs, vr, loc, *sems):
+    here = Place()
+    far, y, tp, row, x = here.far, here.y, here.tp, here.row, here.x
+    gather_x = Gather(here, xh, xg, sems[0:4])
+    layers = ((s0, w0), (s1, w1))
+    greet_all(here)
+
+    def within(l, step):
+        source, w = layers[l]
+        peer = lax.rem(tp + step, TP)
+        return remote(
+            source.at[peer], w.at[far, row, y, x], ps.at[l, step], pr.at[l, tp], here.device(peer)
+        )
+
+    def start_layer(l):
+        source, w = layers[l]
+        for step in range(1, TP):
+            within(l, step).start()
+        pltpu.make_async_copy(source.at[tp], w.at[far, row, y, x], pr.at[l, tp]).start()
 
     def vec_copy(step):
-        return remote(vec, vecg.at[me], vs.at[step], vr.at[step], to(step))
-
-    def plane_copy(step):
-        peer = lax.rem(tp + step, TP)
-        return remote(s1.at[peer], w1.at[tp], ts.at[step], tr.at[step], (grp, peer))
-
-    def start_all(step, carry):
+        other = lax.rem(here.me + step, here.total)
+        return remote(vec, vecg.at[here.me], vs.at[step], vr.at[step], here.device_of(other))
+
+    def start_vec(step, carry):
         vec_copy(step).start()
-        block_copy(step).start()
         return carry
 
-    lax.fori_loop(1, total, start_all, 0)
-
-    def start_plane(step, carry):
-        plane_copy(step).start()
+    def wait_vec(step, carry):
+        vec_copy(step).wait()
         return carry
 
-    lax.fori_loop(1, TP, start_plane, 0)
-    for copy in own:
-        copy.start()
-    slot = lax.rem(me, owners)
-    user = me // owners
-    for g in range(groups):
-        target_self = (user == tp) & (g == grp)
-
-        @pl.when(jnp.logical_not(target_self))
+    start_layer(0)
+    start_layer(1)
+    lax.fori_loop(1, here.total, start_vec, 0)
+    own_vec = pltpu.make_async_copy(vec, vecg.at[here.me], loc.at[1])
+    own_vec.start()
+    slot = lax.rem(here.me, owners)
+    user = here.me // owners
+
+    def out_copy(f, v):
+        return remote(wo, wog.at[slot], os.at[f, v], orr.at[slot], here.device(user, f, v))
+
+    def is_own(f, v):
+        return (user == tp) & (f == far) & (v == y)
+
+    blocks = [(f, v) for f in range(here.fars) for v in range(here.ys)]
+    for f, v in blocks:
+
+        @pl.when(jnp.logical_not(is_own(f, v)))
         def _():
-            remote(wo, wog.at[slot], os.at[g], orr.at[slot], (g, user)).start()
-
-        @pl.when(target_self)
+            out_copy(f, v).start()
+
+        @pl.when(is_own(f, v))
         def _():
             pltpu.make_async_copy(wo, wog.at[slot], orr.at[slot]).start()
 
-    passed = []
-    for step in range(1, HALF):
-        source = core * HALF + lax.rem(chip + HALF - step, HALF)
-        remote(xh, xg.at[source], xs.at[step], xr.at[step], (grp, tp)).wait_recv()
-        copy = remote(xg.at[source], xg.at[source], xs.at[HALF + step], xr.at[HALF + step], (grp, partner))
-        copy.start()
-        passed.append(copy)
-    for copy in first:
-        copy.wait_send()
-    first[-1].wait_recv()
-    for copy in passed:
-        copy.wait()
-    for copy in own:
-        copy.wait()
-
-    def wait_all(step, carry):
-        vec_copy(step).wait()
-        block_copy(step).wait()
-        return carry
-
-    lax.fori_loop(1, total, wait_all, 0)
-
-    def wait_plane(step, carry):
-        plane_copy(step).wait()
-        return carry
-
-    lax.fori_loop(1, TP, wait_plane, 0)
-    for g in range(groups):
-
-        @pl.when(jnp.logical_not((user == tp) & (g == grp)))
-        def _():
-            remote(wo, wog.at[slot], os.at[g], orr.at[slot], (g, user)).wait_send()
-
+    def along_far(l, i, r):
+        part = layers[l][1].at[far, r, y]
+        target = lax.rem(far + i, here.fars)
+        return remote(part, part, zs.at[l, i, r], zr.at[l, i, r], here.device(tp, far=target))
+
+    def along_y(l, j, i, r):
+        part = layers[l][1].at[lax.rem(far + here.fars - i, here.fars), r, y]
+        target = lax.rem(y + j, here.ys)
+        return remote(part, part, ys.at[l, j, i, r], yr.at[l, j, i, r], here.device(tp, y=target))
+
+    def landed(l, f, r, v, sem):
+        part = layers[l][1].at[f, r, v]
+        remote(part, part, sem, sem, here.device(here.partner)).wait_recv()
+
+    def first_hop(l):
+        source, w = layers[l]
+        for r in range(HALF):
+            for side in range(2):
+                t = here.tp_of(r, side)
+                pltpu.make_async_copy(source.at[0], w.at[far, r, y, side], pr.at[l, t]).wait()
+            for i in range(1, here.fars):
+                along_far(l, i, r).start()
+            for j in range(1, here.ys):
+                along_y(l, j, 0, r).start()
+
+    first_hop(0)
+    first_hop(1)
+    gather_x.start(loc.at[0])
+    for l in range(LAYERS):
+        for r in range(HALF):
+            for i in range(1, here.fars):
+                landed(l, lax.rem(far + here.fars - i, here.fars), r, y, zr.at[l, i, r])
+                for j in range(1, here.ys):
+                    along_y(l, j, i, r).start()
+    for k in range(1, HALF):
+        gather_x.wait_block(k)
+    gather_x.wait_partner()
+    for k in range(1, HALF):
+        gather_x.wait_passed(k)
+    for l in range(LAYERS):
+        for j in range(1, here.ys):
+            for i in range(here.fars):
+                for r in range(HALF):
+                    landed(
+                        l, lax.rem(far + here.fars - i, here.fars), r, lax.rem(y + here.ys - j, here.ys),
+                        yr.at[l, j, i, r],
+                    )
+    lax.fori_loop(1, here.total, wait_vec, 0)
+    own_vec.wait()
     for j in range(owners):
         pltpu.make_async_copy(wo, wog.at[j], orr.at[j]).wait()
-
-
-def spread(groups, xh, s0, s1, wo, vec):
-    total = groups * TP
-    rows = s0.shape[1]
+    gather_x.drain()
+    for l in range(LAYERS):
+        for step in range(1, TP):
+            within(l, step).wait_send()
+        for r in range(HALF):
+            for i in range(1, here.fars):
+                along_far(l, i, r).wait_send()
+            for j in range(1, here.ys):
+                for i in range(here.fars):
+                    along_y(l, j, i, r).wait_send()
+    for f, v in blocks:
+
+        @pl.when(jnp.logical_not(is_own(f, v)))
+        def _():
+            out_copy(f, v).wait_send()
+
+
+def spread(here, xh, s0, s1, wo, vec):
+    rows, cols = s0.shape[1:]
     owners = wo.shape[2] // TP // rows
     dma = pltpu.SemaphoreType.DMA
+    whole = jax.ShapeDtypeStruct((here.fars, HALF, here.ys, 2, rows, cols), BF)
+    gathered = jax.ShapeDtypeStruct((TP,) + xh.shape, BF)
     return pl.pallas_call(
-        functools.partial(spread_kernel, groups, owners),
+        functools.partial(spread_kernel, owners),
         out_shape=(
-            jax.ShapeDtypeStruct((TP,) + xh.shape, BF),
-            jax.ShapeDtypeStruct((total,) + s0.shape[1:], BF),
-            jax.ShapeDtypeStruct(s1.shape, BF),
+            gathered,
+            whole,
+            whole,
             jax.ShapeDtypeStruct((owners,) + wo.shape, BF),
-            jax.ShapeDtypeStruct((total,) + vec.shape, F32),
+            jax.ShapeDtypeStruct((here.total,) + vec.shape, F32),
         ),
-        in_specs=[ANY] * 5,
+        in_specs=[VMEM] + [ANY] * 4,
         out_specs=(ANY,) * 5,
         scratch_shapes=[
-            dma((TP,)), dma((TP,)), dma((total,)), dma((total,)), dma((TP,)), dma((TP,)),
-            dma((groups,)), dma((owners,)), dma((total,)), dma((total,)), dma((4,)),
-        ],
+            dma((LAYERS, TP)), dma((LAYERS, TP)),
+            dma((LAYERS, here.fars, HALF)), dma((LAYERS, here.fars, HALF)),
+            dma((LAYERS, here.ys, here.fars, HALF)), dma((LAYERS, here.ys, here.fars, HALF)),
+            dma((here.fars, here.ys)), dma((owners,)), dma((here.total,)), dma((here.total,)), dma((2,)),
+        ]
+        + [dma((HALF,))] * 4,
         compiler_params=pltpu.CompilerParams(collective_id=1, has_side_effects=True),
         name="spread",
     )(xh, s0, s1, wo, vec)
@@ -326,22 +380,21 @@
 
 
 class Exchange:
-    def __init__(self, both, met, landed, sems):
+    def __init__(self, here, both, met, landed, sems):
+        self.here = here
         self.joined, self.mine, self.met, self.landed = both.at[0], both.at[1], met, landed
         self.ps, self.pr, self.bs, self.br = sems
-        self.grp, tp = place()
-        self.core, self.chip = tp // HALF, lax.rem(tp, HALF)
-        self.partner = lax.rem(tp + HALF, TP)
+        self.core, self.chip, self.partner = here.core, here.chip, here.partner
 
     def to_partner(self, k):
         return remote(
-            self.mine.at[k], self.met.at[k], self.ps.at[k], self.pr.at[k], (self.grp, self.partner)
+            self.mine.at[k], self.met.at[k], self.ps.at[k], self.pr.at[k], self.here.device(self.partner)
         )
 
     def to_owner(self, k):
         owner = self.core * HALF + across(self.chip, k)
         return remote(
-            self.joined.at[k], self.landed.at[k], self.bs.at[k], self.br.at[k], (self.grp, owner)
+            self.joined.at[k], self.landed.at[k], self.bs.at[k], self.br.at[k], self.here.device(owner)
         )
 
     def join(self, k):
@@ -375,19 +428,17 @@
 
 
 class Gather:
-    def __init__(self, own, buffer, sems):
-        self.own, self.buffer = own, buffer
+    def __init__(self, here, own, buffer, sems):
+        self.here, self.own, self.buffer = here, own, buffer
         self.gs, self.gr, self.fs, self.fr = sems
-        self.grp, self.tp = place()
-        self.core, self.chip = self.tp // HALF, lax.rem(self.tp, HALF)
-        self.partner = lax.rem(self.tp + HALF, TP)
+        self.tp, self.core, self.chip, self.partner = here.tp, here.core, here.chip, here.partner
 
     def to_peer(self, k):
         if isinstance(k, int) and k == 0:
             target = self.partner
         else:
             target = self.core * HALF + across(self.chip, k)
-        return remote(self.own, self.buffer.at[self.tp], self.gs.at[k], self.gr.at[k], (self.grp, target))
+        return remote(self.own, self.buffer.at[self.tp], self.gs.at[k], self.gr.at[k], self.here.device(target))
 
     def start(self, local):
         pltpu.make_async_copy(self.own, self.buffer.at[self.tp], local).start()
@@ -398,11 +449,11 @@
     def pass_on(self, k):
         source = self.core * HALF + across(self.chip, k)
         block = self.buffer.at[source]
-        return remote(block, block, self.fs.at[k], self.fr.at[k], (self.grp, self.partner))
+        return remote(block, block, self.fs.at[k], self.fr.at[k], self.here.device(self.partner))
 
     def arrived(self, source, sem):
         block = self.buffer.at[source]
-        remote(block, block, sem, sem, (self.grp, self.partner)).wait_recv()
+        remote(block, block, sem, sem, self.here.device(self.partner)).wait_recv()
 
     def wait_block(self, k):
         self.arrived(self.core * HALF + across(self.chip, k), self.gr.at[k])
@@ -426,22 +477,21 @@
             self.pass_on(k).wait_send()
 
 
-def greet_plane():
-    grp, tp = place()
-    core, chip = tp // HALF, lax.rem(tp, HALF)
-    targets = [lax.rem(tp + HALF, TP)] + [core * HALF + across(chip, k) for k in range(1, HALF)]
-    greet([(grp, target) for target in targets])
-
-
-def first_kernel(head_dim, lens, xg, w, wo, vec, rot, own,
-                 out, xnext, qkv_h, prob_h, ctx_h, act_h, slope_h,
+def greet_block(here):
+    targets = [here.partner] + [here.core * HALF + across(here.chip, k) for k in range(1, HALF)]
+    greet([here.device(target) for target in targets])
+
+
+def first_kernel(head_dim, lens, xg, w, wo, vec, rot, own, gr,
+                 out, xnext, gg, qkv_h, prob_h, ctx_h, act_h, slope_h,
                  qkv, prob, ctx, act, slope, both, met, landed, keep, *sems):
-    grp, tp = place()
-    core, chip = tp // HALF, lax.rem(tp, HALF)
+    here = Place()
+    tp, core, chip = here.tp, here.core, here.chip
     local, ff = wo.shape[0], act.shape[2]
-    swap = Exchange(both, met, landed, sems)
+    swap = Exchange(here, both, met, landed, sems[0:4])
+    gather = Gather(here, gr, gg, sems[4:8])
     kept = [(qkv, qkv_h), (prob, prob_h), (ctx, ctx_h), (act, act_h), (slope, slope_h)]
-    greet_plane()
+    greet_block(here)
     b_in, b_up = bias_slices(vec, tp, local, ff)
 
     def one(seq):
@@ -468,10 +518,14 @@
         swap.to_partner(k).start()
         if k + 1 < HALF:
             swap.hand_over(k + 1)
+        if k == 0:
+            gather.start(keep.at[5])
     swap.hand_over(0)
     saved = [pltpu.make_async_copy(a, b, keep.at[i]) for i, (a, b) in enumerate(kept)]
     for copy in saved:
         copy.start()
+    for k in range(1, HALF):
+        gather.wait_block(k)
     swap.wait_landed()
 
     def finish(at):
@@ -481,12 +535,16 @@
         xnext[at] = (centred * scale).astype(BF)
 
     chunks(own.shape[0], finish)
+    gather.wait_partner()
+    for k in range(1, HALF):
+        gather.wait_passed(k)
+    gather.drain()
     swap.drain()
     for copy in saved:
         copy.wait()
 
 
-def first_layer(head_dim, lens, xg, w, wo, vec, rot, own):
+def first_layer(head_dim, lens, xg, w, wo, vec, rot, own, gr):
     seqs, rows, width = xg.shape
     local = wo.shape[0]
     ff = (w.shape[1] - 3 * local) // 2
@@ -499,20 +557,21 @@
     pair = pltpu.VMEM((2, HALF, rows, width), BF)
     return pl.pallas_call(
         functools.partial(first_kernel, head_dim),
-        out_shape=[jax.ShapeDtypeStruct((rows, width), BF)] * 2 + [jax.ShapeDtypeStruct(s, BF) for s in kept],
-        in_specs=[VMEM] * 7,
-        out_specs=[VMEM] * 2 + [ANY] * 5,
-        scratch_shapes=[pltpu.VMEM(s, BF) for s in kept] + [pair, block, block] + [dma((5,))] + [dma((HALF,))] * 4,
+        out_shape=[jax.ShapeDtypeStruct((rows, width), BF)] * 2
+        + [jax.ShapeDtypeStruct(s, BF) for s in [xg.shape] + kept],
+        in_specs=[VMEM] * 8,
+        out_specs=[VMEM] * 2 + [ANY] * 6,
+        scratch_shapes=[pltpu.VMEM(s, BF) for s in kept] + [pair, block, block] + [dma((6,))] + [dma((HALF,))] * 8,
         compiler_params=pltpu.CompilerParams(
             collective_id=2, has_side_effects=True, vmem_limit_bytes=VMEM_BYTES
         ),
         name="first_layer",
-    )(lens, xg, w, wo, vec, rot, own)
+    )(lens, xg, w, wo, vec, rot, own, gr)
 
 
 def weight_grads(xg, gg, mixes, act, ctx, w, vec, sums, packed, out_grad, vrows, grad_rows, tp):
     local, width = out_grad.shape[0] * out_grad.shape[1], out_grad.shape[2]
-    total, shard, cols = packed.shape
+    fars, _, ys, _, shard, cols = packed.shape
     ff = act.shape[2]
     split = 3 * local
     rows = xg.shape[0] * xg.shape[1]
@@ -525,16 +584,17 @@
     exact = lambda a, b: lax.dot_general(a, b, NT, preferred_element_type=F32, precision=lax.Precision.HIGHEST)
     for c in range(2):
         cut = slice(c * half, (c + 1) * half)
-        lines = slice(c * half // shard, (c + 1) * half // shard)
+        lines = slice(c * fars // 2, (c + 1) * fars // 2)
+        shape = (fars // 2, HALF, ys, 2, shard)
         gains = vec[0:4, cut].T
         cross = tn_dot(flat(xg, cut), flat(mixes, everything))
         in_cross, up_cross = cross[:, :split], cross[:, split:]
         in_grad = gains[:, 0:1] * in_cross + gains[:, 1:2] * col_sums[:, :split]
         up_grad = gains[:, 2:3] * up_cross + gains[:, 3:4] * col_sums[:, split:]
         down_grad = tn_dot(flat(gg, cut), flat(act, everything))
-        packed[lines, :, :split] = in_grad.astype(BF).reshape(-1, shard, split)
-        packed[lines, :, split : split + ff] = up_grad.astype(BF).reshape(-1, shard, ff)
-        packed[lines, :, split + ff :] = down_grad.astype(BF).reshape(-1, shard, ff)
+        packed[lines, :, :, :, :, :split] = in_grad.astype(BF).reshape(shape + (split,))
+        packed[lines, :, :, :, :, split : split + ff] = up_grad.astype(BF).reshape(shape + (ff,))
+        packed[lines, :, :, :, :, split + ff :] = down_grad.astype(BF).reshape(shape + (ff,))
         w_in = w[cut, :split].astype(F32)
         w_up = w[cut, split : split + ff].astype(F32)
         norm_rows = [
@@ -573,13 +633,13 @@
                   out, grad_next, packed, out_grad, vrows,
                   xg, work, mixes, act, ctx, sums, both, met, landed, both_e, met_e, landed_e,
                   loc, *sems):
-    grp, tp = place()
-    core, chip = tp // HALF, lax.rem(tp, HALF)
+    here = Place()
+    tp, core, chip = here.tp, here.core, here.chip
     local, ff = wo.shape[0], act.shape[2]
-    swap = Exchange(both, met, landed, sems[0:4])
-    swap_e = Exchange(both_e, met_e, landed_e, sems[4:8])
-    gather = Gather(xown, xg, sems[8:12])
-    greet_plane()
+    swap = Exchange(here, both, met, landed, sems[0:4])
+    swap_e = Exchange(here, both_e, met_e, landed_e, sems[4:8])
+    gather = Gather(here, xown, xg, sems[8:12])
+    greet_block(here)
     gather.start(loc.at[0])
     sums[...] = jnp.zeros_like(sums)
     b_in, b_up = bias_slices(vec, tp, local, ff)
@@ -646,7 +706,7 @@
     swap_e.drain()
 
 
-def second_layer(head_dim, owners, shard, lens, xown, gg, w, wo, vec, rot, hidden):
+def second_layer(here, head_dim, owners, shard, lens, xown, gg, w, wo, vec, rot, hidden):
     seqs, rows, width = gg.shape
     local = wo.shape[0]
     ff = (w.shape[1] - 3 * local) // 2
@@ -659,7 +719,7 @@
         out_shape=[
             jax.ShapeDtypeStruct((rows, width), BF),
             jax.ShapeDtypeStruct((rows, width), BF),
-            jax.ShapeDtypeStruct((width // shard, shard, w.shape[1]), BF),
+            jax.ShapeDtypeStruct((here.fars, HALF, here.ys, 2, shard, w.shape[1]), BF),
             jax.ShapeDtypeStruct((owners, shard, width), BF),
             jax.ShapeDtypeStruct((13 * width // 128, 1, 128), F32),
         ],
@@ -690,65 +750,144 @@
     return (128 - step + vec_part + 127) // 128
 
 
-def third_kernel(head_dim, groups, owners, gown, w, wo, vec, rot, tokens, xg,
-                 qkv_h, prob_h, ctx_h, act_h, slope_h, packed1, out_grad1, vrows1,
+class Owners:
+    def __init__(self, here, packed, from_y, acc, from_far, out, sems):
+        self.here, self.packed, self.from_y, self.acc, self.from_far, self.out = (
+            here, packed, from_y, acc, from_far, out
+        )
+        self.ys, self.yr, self.zs, self.zr, self.ps, self.pr = sems
+
+    def line(self, i):
+        return lax.rem(self.here.far + i, self.here.fars)
+
+    def to_y(self, j, i, r):
+        here = self.here
+        y = lax.rem(here.y + j, here.ys)
+        return remote(
+            self.packed.at[self.line(i), r, y], self.from_y.at[j - 1, i, r],
+            self.ys.at[j, i, r], self.yr.at[j, i, r], here.device(here.tp, y=y),
+        )
+
+    def to_far(self, i, r):
+        here = self.here
+        return remote(
+            self.acc.at[i, r], self.from_far.at[i - 1, r], self.zs.at[i, r], self.zr.at[i, r],
+            here.device(here.tp, far=self.line(i)),
+        )
+
+    def start(self):
+        for i in list(range(1, self.here.fars)) + [0]:
+            for r in range(HALF):
+                for j in range(1, self.here.ys):
+                    self.to_y(j, i, r).start()
+
+    def add(self, i, r):
+        here = self.here
+        value = self.packed[self.line(i), r, here.y].astype(F32)
+        for j in range(1, here.ys):
+            self.to_y(j, i, r).wait_recv()
+            value = value + self.from_y[j - 1, i, r].astype(F32)
+        if i == 0:
+            for far in range(1, here.fars):
+                self.to_far(far, r).wait_recv()
+                value = value + self.from_far[far - 1, r].astype(F32)
+        self.acc[i, r] = value.astype(BF)
+
+    def pass_far(self):
+        for i in range(1, self.here.fars):
+            for r in range(HALF):
+                self.add(i, r)
+                self.to_far(i, r).start()
+
+    def to_owner(self, r, x):
+        here = self.here
+        return remote(
+            self.acc.at[0, r, x], self.out.at[here.tp], self.ps.at[r, x], self.pr.at[here.tp],
+            here.device(here.tp_of(r, x)),
+        )
+
+    def hand_out(self):
+        here = self.here
+        for r in range(HALF):
+            self.add(0, r)
+            for x in range(2):
+                own = here.tp == here.tp_of(r, x)
+
+                @pl.when(jnp.logical_not(own))
+                def _():
+                    self.to_owner(r, x).start()
+
+                @pl.when(own)
+                def _():
+                    pltpu.make_async_copy(self.acc.at[0, r, x], self.out.at[here.tp], self.pr.at[here.tp]).start()
+
+    def drain(self):
+        here = self.here
+        for source in range(TP):
+            pltpu.make_async_copy(self.acc.at[0, 0, 0], self.out.at[source], self.pr.at[source]).wait()
+        for r in range(HALF):
+            for i in range(here.fars):
+                for j in range(1, here.ys):
+                    self.to_y(j, i, r).wait_send()
+                if i:
+                    self.to_far(i, r).wait_send()
+            for x in range(2):
+
+                @pl.when(here.tp != here.tp_of(r, x))
+                def _():
+                    self.to_owner(r, x).wait_send()
+
+
+def third_kernel(head_dim, owners, gown, w, wo, vec, rot, tokens, xg, packed1,
+                 qkv_h, prob_h, ctx_h, act_h, slope_h, out_grad1, vrows1,
                  out, r0, r1, ro, rv,
                  gg, work, mixes, sums, qkv, prob, ctx, act, slope, packed0, out_grad0, vrows0,
-                 both, met, landed, loc, keep, ss, sr, os, orr, vs, vr, own_sem, *sems):
-    grp, tp = place()
-    me = grp * TP + tp
-    total = groups * TP
-    core, chip = tp // HALF, lax.rem(tp, HALF)
+                 both, met, landed, from_y0, acc0, from_far0, from_y1, acc1, from_far1,
+                 loc, keep, os, orr, vs, vr, own_sem, *sems):
+    here = Place()
+    tp, core, chip, me, total = here.tp, here.core, here.chip, here.me, here.total
     local, ff = wo.shape[0], act.shape[2]
-    swap = Exchange(both, met, landed, sems[0:4])
-    gather = Gather(gown, gg, sems[4:8])
+    swap = Exchange(here, both, met, landed, sems[0:4])
+    gather = Gather(here, gown, gg, sems[4:8])
+    settle0 = Owners(here, packed0, from_y0, acc0, from_far0, r0, sems[8:14])
+    settle1 = Owners(here, packed1, from_y1, acc1, from_far1, r1, sems[14:20])
     kept = [(qkv_h, qkv), (prob_h, prob), (slope_h, slope), (act_h, act), (ctx_h, ctx)]
     rows_sent = rv.shape[2]
     vec_part = 13 * gown.shape[1] // total
-    greet_all(groups)
+    greet_all(here)
     gather.start(loc.at[0])
-
+    settle1.start()
     loads = [pltpu.make_async_copy(a, b, keep.at[i]) for i, (a, b) in enumerate(kept)]
     for copy in loads:
         copy.start()
 
-    def to(step):
+    def vec_copy(layer, source, step):
         other = lax.rem(me + step, total)
-        return other // TP, lax.rem(other, TP), other
-
-    def block_copy(layer, source, landing, step):
-        g, t, other = to(step)
-        return remote(source.at[other], landing.at[me], ss.at[layer, step], sr.at[layer, step], (g, t))
-
-    def vec_copy(layer, source, step):
-        g, t, other = to(step)
         first = (other * vec_part) // 128
         return remote(
-            source.at[pl.ds(first, rows_sent)], rv.at[layer, me], vs.at[layer, step], vr.at[layer, step], (g, t)
-        )
-
-    def own_copies(layer, source, landing, vrows):
+            source.at[pl.ds(first, rows_sent)], rv.at[layer, me], vs.at[layer, step], vr.at[layer, step],
+            here.device_of(other),
+        )
+
+    def own_vec(layer, vrows):
         first = (me * vec_part) // 128
-        return [
-            pltpu.make_async_copy(source.at[me], landing.at[me], own_sem.at[layer, 0]),
-            pltpu.make_async_copy(vrows.at[pl.ds(first, rows_sent)], rv.at[layer, me], own_sem.at[layer, 1]),
-        ]
+        return pltpu.make_async_copy(vrows.at[pl.ds(first, rows_sent)], rv.at[layer, me], own_sem.at[layer])
+
+    sender = here.far * here.ys + here.y
 
     def out_copy(layer, source, j):
         owner = tp * owners + j
         return remote(
-            source.at[j], ro.at[layer, grp], os.at[layer, j], orr.at[layer, grp], (owner // TP, lax.rem(owner, TP))
-        )
-
-    def send(layer, source, landing, out_grad, vrows):
+            source.at[j], ro.at[layer, sender], os.at[layer, j], orr.at[layer, sender], here.device_of(owner)
+        )
+
+    def send(layer, out_grad, vrows):
         def start_all(step, carry):
             vec_copy(layer, vrows, step).start()
-            block_copy(layer, source, landing, step).start()
             return carry
 
         lax.fori_loop(1, total, start_all, 0)
-        for copy in own_copies(layer, source, landing, vrows):
-            copy.start()
+        own_vec(layer, vrows).start()
         for j in range(owners):
             owner = tp * owners + j
 
@@ -758,17 +897,15 @@
 
             @pl.when(owner == me)
             def _():
-                pltpu.make_async_copy(out_grad.at[j], ro.at[layer, grp], orr.at[layer, grp]).start()
-
-    def collect(layer, source, landing, out_grad, vrows):
+                pltpu.make_async_copy(out_grad.at[j], ro.at[layer, sender], orr.at[layer, sender]).start()
+
+    def collect(layer, out_grad, vrows):
         def wait_all(step, carry):
             vec_copy(layer, vrows, step).wait()
-            block_copy(layer, source, landing, step).wait()
             return carry
 
         lax.fori_loop(1, total, wait_all, 0)
-        for copy in own_copies(layer, source, landing, vrows):
-            copy.wait()
+        own_vec(layer, vrows).wait()
         for j in range(owners):
             owner = tp * owners + j
 
@@ -776,10 +913,10 @@
             def _():
                 out_copy(layer, out_grad, j).wait_send()
 
-        for g in range(groups):
+        for g in range(here.groups):
             pltpu.make_async_copy(out_grad.at[0], ro.at[layer, g], orr.at[layer, g]).wait()
 
-    send(1, packed1, r1, out_grad1, vrows1)
+    send(1, out_grad1, vrows1)
     sums[...] = jnp.zeros_like(sums)
     for copy in loads[:3]:
         copy.wait()
@@ -812,11 +949,16 @@
 
         lax.fori_loop(0, 2, part_of, 0)
         swap.to_partner(k).start()
+        if k == 2:
+            settle1.pass_far()
     for copy in loads[3:]:
         copy.wait()
     weight_grads(xg, gg, mixes, act, ctx, w, vec, sums, packed0, out_grad0, vrows0, gg[tp], tp)
-    send(0, packed0, r0, out_grad0, vrows0)
+    settle0.start()
     swap.hand_over(HALF - 1)
+    settle1.hand_out()
+    send(0, out_grad0, vrows0)
+    settle0.pass_far()
     swap.wait_landed()
 
     def finish_back(at):
@@ -828,33 +970,40 @@
         out[at] = (gg[tp, at].astype(F32) + scale * (value - mean_one - xhat * mean_two)).astype(BF)
 
     chunks(tokens.shape[0], finish_back)
+    settle0.hand_out()
     gather.drain()
     swap.drain()
-    collect(1, packed1, r1, out_grad1, vrows1)
-    collect(0, packed0, r0, out_grad0, vrows0)
-
-
-def third_layer(head_dim, groups, gown, w, wo, vec, rot, tokens, xg, kept, packed1, out_grad1, vrows1):
+    collect(1, out_grad1, vrows1)
+    collect(0, out_grad0, vrows0)
+    settle1.drain()
+    settle0.drain()
+
+
+def third_layer(here, head_dim, gown, w, wo, vec, rot, tokens, xg, kept, packed1, out_grad1, vrows1):
     seqs, rows, width = xg.shape
     local = wo.shape[0]
     ff = (w.shape[1] - 3 * local) // 2
     mix = 3 * local + ff
-    total = groups * TP
+    total, fars, ys = here.total, here.fars, here.ys
     owners, shard = out_grad1.shape[:2]
     dma = pltpu.SemaphoreType.DMA
     block = pltpu.VMEM((HALF, rows, width), BF)
     pair = pltpu.VMEM((2, HALF, rows, width), BF)
+    unit = (HALF, 2, shard, w.shape[1])
+    settle = [pltpu.VMEM(n + unit, BF) for n in ((ys - 1, fars), (fars,), (fars - 1,))]
+    settle_sems = [dma((ys, fars, HALF))] * 2 + [dma((fars, HALF))] * 2 + [dma((HALF, 2)), dma((TP,))]
     sent = vector_rows(13 * width // total)
+    owned = jax.ShapeDtypeStruct((TP, shard, w.shape[1]), BF)
     return pl.pallas_call(
-        functools.partial(third_kernel, head_dim, groups, owners),
+        functools.partial(third_kernel, head_dim, owners),
         out_shape=[
             jax.ShapeDtypeStruct((rows, width), BF),
-            jax.ShapeDtypeStruct(packed1.shape, BF),
-            jax.ShapeDtypeStruct(packed1.shape, BF),
-            jax.ShapeDtypeStruct((LAYERS, groups, shard, width), BF),
+            owned,
+            owned,
+            jax.ShapeDtypeStruct((LAYERS, here.groups, shard, width), BF),
             jax.ShapeDtypeStruct((LAYERS, total, sent, 1, 128), F32),
         ],
-        in_specs=[VMEM] * 7 + [ANY] * 8,
+        in_specs=[VMEM] * 8 + [ANY] * 7,
         out_specs=[VMEM] + [ANY] * 4,
         scratch_shapes=[
             pltpu.VMEM((seqs, rows, width), BF),
@@ -865,17 +1014,18 @@
         + [pltpu.VMEM(a.shape, BF) for a in kept]
         + [pltpu.VMEM(packed1.shape, BF), pltpu.VMEM(out_grad1.shape, BF), pltpu.VMEM(vrows1.shape, F32)]
         + [pair, block, block]
+        + settle * 2
         + [
-            dma((1,)), dma((5,)), dma((LAYERS, total)), dma((LAYERS, total)),
-            dma((LAYERS, owners)), dma((LAYERS, groups)), dma((LAYERS, total)), dma((LAYERS, total)),
-            dma((LAYERS, 2)),
+            dma((1,)), dma((5,)), dma((LAYERS, owners)), dma((LAYERS, here.groups)),
+            dma((LAYERS, total)), dma((LAYERS, total)), dma((LAYERS,)),
         ]
-        + [dma((HALF,))] * 8,
+        + [dma((HALF,))] * 8
+        + settle_sems * 2,
         compiler_params=pltpu.CompilerParams(
             collective_id=4, has_side_effects=True, vmem_limit_bytes=VMEM_BYTES
         ),
         name="third_layer",
-    )(gown, w, wo, vec, rot, tokens, xg, *kept, packed1, out_grad1, vrows1)
+    )(gown, w, wo, vec, rot, tokens, xg, packed1, *kept, out_grad1, vrows1)
 
 
 def adam_kernel(groups, local, ff, fixes, r0, r1, ro, *refs):
@@ -897,8 +1047,6 @@
     def layer(source):
         for p in range(TP):
             value = source[p].astype(F32)
-            for g in range(1, groups):
-                value = value + source[g * TP + p].astype(F32)
             for i in range(3):
                 start = i * TP * local + p * local
                 update(0, slice(start, start + local), value[:, i * local : (i + 1) * local])
@@ -973,20 +1121,11 @@
     return (change, moment, square)
 
 
-def per_device(
-    groups,
-    tokens,
-    cotangent,
-    seq_lengths,
-    seq_device,
-    step_count,
-    *state,
-):
+def per_device(tokens, cotangent, seq_lengths, seq_device, step_count, *state):
     params, moments, squares = state[0:5], state[5:10], state[10:15]
     attend_in, attend_out, expand_weight, reduce_weight, layer_vectors = params
-    grp, tp = place()
-    me = grp * TP + tp
-    total = groups * TP
+    here = Place()
+    tp, me, total, groups = here.tp, here.me, here.total, here.groups
     rows, width = tokens.shape
     shard = attend_in.shape[1]
     head_dim = width // HEADS
@@ -994,7 +1133,7 @@
     ff = expand_weight.shape[2] // TP
     vec_part = layer_vectors.shape[1]
     owners = local // shard
-    plane_ids = grp * TP + jnp.arange(TP, dtype=jnp.int32)
+    plane_ids = here.flat(here.far, here.y, jnp.arange(TP, dtype=jnp.int32))
     lens = jnp.sum(jnp.where(plane_ids[:, None] == seq_device[None, :], seq_lengths[None, :], 0), 1)
     lens = jnp.broadcast_to(lens[:, None, None], (TP, 1, rows))
     own_length = jnp.sum(jnp.where(seq_device == me, seq_lengths, 0))
@@ -1015,24 +1154,21 @@
     vec = jnp.pad(layer_vectors.astype(BF).astype(F32).reshape(-1), (0, 8 * 128 - 2 * vec_part)).reshape(8, 128)
     xhat_own = standard(tokens.astype(F32)).astype(BF)
     grad_own = jnp.where(valid, cotangent, jnp.zeros_like(cotangent))
-    grads_all = lax.all_gather(grad_own, "tp", axis=0)
-    xg, w0, w1, wog, vecg = spread(groups, xhat_own, blocks[0], blocks[1], attend_out.astype(BF), vec)
-    w1, grads_all = lax.optimization_barrier((w1, grads_all))
-    w1 = lax.all_gather(w1, "grp", axis=0).reshape(width, -1)
-    w0 = w0.reshape(width, -1)
+    xg, w0, w1, wog, vecg = spread(here, xhat_own, blocks[0], blocks[1], attend_out.astype(BF), vec)
+    w0, w1 = w0.reshape(width, -1), w1.reshape(width, -1)
     out_rows = wog.transpose(1, 0, 2, 3).reshape(LAYERS, local, width)
     vectors = vecg.reshape(total, -1)[:, : 2 * vec_part].reshape(total, LAYERS, vec_part)
     vectors = vectors.transpose(1, 0, 2).reshape(LAYERS, 13, width)
     vectors = jnp.pad(vectors, ((0, 0), (0, 3), (0, 0)))
 
-    hidden0, xnext, *kept = first_layer(
-        head_dim, lens, xg, w0, out_rows[0], vectors[0], rot, tokens
+    hidden0, xnext, grads_all, *kept = first_layer(
+        head_dim, lens, xg, w0, out_rows[0], vectors[0], rot, tokens, grad_own
     )
     hidden1, grad0, packed1, out_grad1, vrows1 = second_layer(
-        head_dim, owners, shard, lens, xnext, grads_all, w1, out_rows[1], vectors[1], rot, hidden0
+        here, head_dim, owners, shard, lens, xnext, grads_all, w1, out_rows[1], vectors[1], rot, hidden0
     )
     input_grad, r0, r1, ro, rv = third_layer(
-        head_dim, groups, grad0, w0, out_rows[0], vectors[0], rot, tokens, xg, kept, packed1, out_grad1, vrows1
+        here, head_dim, grad0, w0, out_rows[0], vectors[0], rot, tokens, xg, kept, packed1, out_grad1, vrows1
     )
     step_float = step_count[0].astype(F32)
     first_fix = 1.0 - jnp.power(BETA_FIRST, step_float)
@@ -1050,16 +1186,16 @@
 
 
 def solution(mesh):
-    devices = mesh.devices.reshape(-1, TP)
-    groups = devices.shape[0]
-    flat = Mesh(devices, ("grp", "tp"))
-    axes = ("grp", "tp")
-    by_row = P(axes, None)
-    by_dim = [P(None, axes, None)] * 4 + [P(None, axes)]
+    devices = mesh.devices.reshape(-1)
+    blocks = devices.size // TP
+    fars = 1 << ((blocks.bit_length()) // 2)
+    flat = Mesh(devices.reshape(fars, 2, 2, blocks // fars, 2), AXES)
+    by_row = P(AXES, None)
+    by_dim = [P(None, AXES, None)] * 4 + [P(None, AXES)]
     return jax.shard_map(
-        functools.partial(per_device, groups),
+        per_device,
         mesh=flat,
         in_specs=(by_row, by_row, P(), P(), P(), *(by_dim * 3)),
-        out_specs=(P(None, axes, None), by_row, *(by_dim * 4)),
+        out_specs=(P(None, AXES, None), by_row, *(by_dim * 4)),
         check_vma=False,
     )

time: 445 us -> 412 us (0.926)
  Pallas kernels: 393 us -> 379 us
  between operations: 15.4 us -> 1.91 us
  waiting for transfers between devices: 9.9 us -> 0 us
    pallas_call x2, Pallas kernels: 250 us -> 213 us  [the longest x1 118 us: third_layer(): pl.pallas_call(functools.partial(third_kernel, head_dim, owners), out_sha...]
    pallas_call x1, Pallas kernels: 40.8 us -> 63.8 us  [first_layer(): pl.pallas_call(functools.partial(first_kernel, head_dim), out_shape=[jax....]
    all_gather x2 -> x0, waiting for transfers between devices: 9.87 us -> none  [the longest x1 9.85 us: per_device(): w1 = lax.all_gather(w1, 'grp', axis=0).reshape(width, -1)]
  transfers between devices with their start and end apart: 2 -> 0, of which waited for: 1 -> 0; matrix products, arithmetic and copies ran while one was open for 3% -> 0% of each run, Pallas kernels for 31% -> 0%
where the time goes in v3:
time: 412 us; the launch traced here: 404 us
  Pallas kernels  379 us (92%)
  other arithmetic  15.6 us (4%)
  local copies, waits for them, and re-layouts  7.64 us (2%)
    pallas_call x1, Pallas kernels, third_layer(): pl.pallas_call(functools.partial(third_kernel, head_dim, owners), out_sha...  118 us
    pallas_call x1, Pallas kernels, spread(): pl.pallas_call(functools.partial(spread_kernel, owners), out_shape=(gathe...  94.6 us
    pallas_call x1, Pallas kernels, second_layer(): pl.pallas_call(functools.partial(second_kernel, head_dim), out_shape=[jax...  89.9 us
    pallas_call x1, Pallas kernels, first_layer(): pl.pallas_call(functools.partial(first_kernel, head_dim), out_shape=[jax....  63.8 us
    pallas_call x1, Pallas kernels, adam_step(): pl.pallas_call(functools.partial(adam_kernel, groups, local, ff), grid=(L...  12 us

profile of v3, /device:TPU:1, one launch (start us, length us, event | category | flops | bytes accessed | tf_op | source)
XLA Modules:
  0.0 403.7 jit_solution(9038192911935990205)
XLA Ops:
  0.7 0.0 copy-start.2
  0.7 1.4 fusion.19
  2.1 0.6 iota_compare_fusion
  2.8 1.9 broadcast_select_fusion.gr
  4.7 0.0 copy-done.2
  4.7 0.0 copy-start.1
  4.7 0.1 convert.17
  4.8 0.1 copy.62
  4.9 1.0 copy-done.1
  5.9 0.1 convert.18
  6.0 0.0 copy-start.3
  6.0 0.1 copy.63
  6.1 0.2 copy_bitcast_fusion
  6.3 0.8 copy-done.3
  7.2 0.1 copy.74
  7.4 0.2 reshape.366
  7.5 0.9 pad_maximum_fusion.2.s1
  8.5 0.1 copy.59
  8.5 0.1 copy.60
  8.6 0.2 copy_bitcast_fusion.3
  8.8 0.0 copy-start
  8.8 0.1 copy.75
  9.0 0.2 reshape.365
  9.1 0.0 copy-start.4
  9.1 0.9 pad_maximum_fusion.1.s0
  10.1 0.0 copy-done
  10.1 0.0 copy-start.7
  10.1 0.1 convert_reduce_fusion
  10.2 0.3 fusion.2
  10.5 1.1 fusion.3.xh
  11.6 0.0 copy-done.4
  11.6 0.7 convert_element_type.70.wo
  12.3 0.0 copy-done.7
  12.3 0.1 reshape.367
  12.4 0.6 bitcast_convert_fusion.vec
  13.0 94.6 %spread.1 = (bf16[8,256,1024]{2,1,0:T(8,128)(2,1)}, bf16[2,4,2,2,32,1408]{5,4,3,2,1,0:T(8,128)(2,1)}, bf16[2,4,2,2,32,1408]{5,4,3,2,1,0:T(8,128)(2,1)}, bf16[4,2,32,1024]{3,2,1,0:T(8,128)(2,1)}, f32[32,8,128]{2,1,0:T(8,128)}) custom-call(bf16[256,1024]{1,0:T(8,128)(2,1)} %fusion.3.xh, bf16[8,32,1408]{2,1,0:T(8,128)(2,1)} %pad_maximum_fusion.1.s0, ...), custom_call_target="tpu_custom_call" | custom-call | tf_op jit(solution)/shard_map/spread/pallas_call | solution.py:237
  107.5 0.0 copy-start.6
  107.6 1.0 copy.76
  108.6 0.2 reshape.372
  108.8 0.0 copy-start.8
  108.8 0.0 copy-start.9
  108.8 0.1 reshape.373
  108.9 0.7 fusion.7
  109.6 0.0 copy-done.6
  109.6 0.8 fusion.25
  110.5 0.5 cosine_select_fusion
  111.0 0.8 pad_maximum_fusion.3.rot
  111.8 0.0 copy-done.8
  111.8 0.0 copy-done.9
  111.8 0.2 select_reduce_fusion
  112.0 0.7 broadcast_in_dim.71.lens
  112.6 63.8 %first_layer.1 = (bf16[256,1024]{1,0:T(8,128)(2,1)}, bf16[256,1024]{1,0:T(8,128)(2,1)}, bf16[8,256,1024]{2,1,0:T(8,128)(2,1)}, bf16[8,256,384]{2,1,0:T(8,128)(2,...) custom-call(s32[8,1,256]{2,1,0:T(1,128)} %broadcast_in_dim.71.lens, ...), custom_call_target="tpu_custom_call" | custom-call | tf_op jit(solution)/shard_map/first_layer/pallas_call | solution.py:558
  176.4 89.9 %second_layer.1 = (bf16[256,1024]{1,0:T(8,128)(2,1)}, bf16[256,1024]{1,0:T(8,128)(2,1)}, bf16[2,4,2,2,32,1408]{5,4,3,2,1,0:T(8,128)(2,1)}, bf16[4,32,1024]{2,1,0:T(8,128)(2,1)}, f32[104,1,128]{2,1,0:T(1,128)}) custom-call(s32[8,1,256]{2,1,0:T(1,128)} %broadcast_in_dim.71.lens, bf16[256,1024]{1,0:T(8,128)(2,1)} %get-tuple-element.66.xown, ...), custom_call_target="tpu_custom_call" | custom-call | tf_op jit(solution)/shard_map/second_layer/pallas_call | solution.py:717
  266.4 118.3 %third_layer.1 = (bf16[256,1024]{1,0:T(8,128)(2,1)}, bf16[8,32,1408]{2,1,0:T(8,128)(2,1)}, bf16[8,32,1408]{2,1,0:T(8,128)(2,1)}, bf16[2,4,32,1024]{3,2,1,0:T(8,128)(2,1)}, f32[2,32,4,1,128]{4,3,2,1,0:T(1,128)}) custom-call(bf16[256,1024]{1,0:T(8,128)(2,1)} %get-tuple-element.70.gown, bf16[1024,1408]{1,0:T(8,128)(2,1)} %bitcast.62, ...), custom_call_target="tpu_custom_call" | custom-call | tf_op jit(solution)/shard_map/third_layer/pallas_call | solution.py:997
  384.6 1.0 reduce_sum.49
  386.4 1.4 add_multiply_fusion
  387.8 0.6 pad_maximum_fusion.4.fixes
  388.4 12.0 %adam_step.1 = (f32[2,32,3072]{2,1,0:T(8,128)}, f32[2,32,1024]{2,1,0:T(8,128)}, f32[2,32,4096]{2,1,0:T(8,128)}, f32[2,32,4096]{2,1,0:T(8,128)}, f32[2,32,3072]{2...) custom-call(f32[2]{0:T(128)} %pad_maximum_fusion.4.fixes, ...), custom_call_target="tpu_custom_call" | custom-call | tf_op jit(solution)/shard_map/adam_step/pallas_call | solution.py:1079
  400.4 0.0 copy-start.5
  400.4 2.3 pad_maximum_fusion
  402.7 0.0 copy-done.5
  402.7 0.8 copy.80
  (16 shorter events, 0.3 us)
Async XLA Ops:
  0.7 4.0 %copy-start.2 = (f32[2,32,4096]{2,1,0:T(8,128)S(1)}, f32[2,32,4096]{2,1,0:T(8,128)}, u32[]{:S(2)}) copy-start(f32[2,32,4096]{2,1,0:T(8,128)} %refs_2_.1) | copy-start | bytes 3145732
  4.7 1.2 copy-start.1
  6.0 1.1 copy-start.3
  8.8 1.3 copy-start
  9.1 2.5 copy-start.4
  10.1 2.2 copy-start.7
  107.5 2.0 copy-start.6
  108.8 3.0 copy-start.8
  108.8 3.0 copy-start.9
  400.4 2.3 copy-start.5

commit v4 on v3

--- a/solution.py
+++ b/solution.py
@@ -630,13 +630,13 @@
 
 
 def second_kernel(head_dim, lens, xown, gg, w, wo, vec, rot, hidden,
-                  out, grad_next, packed, out_grad, vrows,
-                  xg, work, mixes, act, ctx, sums, both, met, landed, both_e, met_e, landed_e,
+                  shares, grad_next, packed, out_grad, vrows,
+                  xg, work, mixes, act, ctx, sums, both, met, both_e, met_e, landed_e,
                   loc, *sems):
     here = Place()
     tp, core, chip = here.tp, here.core, here.chip
     local, ff = wo.shape[0], act.shape[2]
-    swap = Exchange(here, both, met, landed, sems[0:4])
+    swap = Exchange(here, both, met, None, sems[0:4])
     swap_e = Exchange(here, both_e, met_e, landed_e, sems[4:8])
     gather = Gather(here, xown, xg, sems[8:12])
     greet_block(here)
@@ -663,7 +663,7 @@
         if k:
             gather.wait_block(k)
             swap_e.hand_over(k - 1)
-            swap.hand_over(k - 1)
+            swap.join(k - 1)
             gather.wait_passed(k)
         else:
             gather.wait_partner()
@@ -680,7 +680,9 @@
         swap_e.to_partner(k).start()
         swap.to_partner(k).start()
     swap_e.hand_over(HALF - 1)
-    swap.hand_over(HALF - 1)
+    swap.join(HALF - 1)
+    saved = pltpu.make_async_copy(both.at[0], shares, loc.at[1])
+    saved.start()
     weight_grads(xg, gg, mixes, act, ctx, w, vec, sums, packed, out_grad, vrows, gg[tp], tp)
     swap_e.wait_landed()
 
@@ -695,15 +697,11 @@
         ).astype(BF)
 
     chunks(hidden.shape[0], finish_back)
-    swap.wait_landed()
-
-    def finish(at):
-        out[at] = (hidden[at].astype(F32) + swap.total(at) + (vec[7:8] + vec[12:13])).astype(BF)
-
-    chunks(hidden.shape[0], finish)
     gather.drain()
-    swap.drain()
+    for k in range(HALF):
+        swap.to_partner(k).wait_send()
     swap_e.drain()
+    saved.wait()
 
 
 def second_layer(here, head_dim, owners, shard, lens, xown, gg, w, wo, vec, rot, hidden):
@@ -717,14 +715,14 @@
     return pl.pallas_call(
         functools.partial(second_kernel, head_dim),
         out_shape=[
-            jax.ShapeDtypeStruct((rows, width), BF),
+            jax.ShapeDtypeStruct((HALF, rows, width), BF),
             jax.ShapeDtypeStruct((rows, width), BF),
             jax.ShapeDtypeStruct((here.fars, HALF, here.ys, 2, shard, w.shape[1]), BF),
             jax.ShapeDtypeStruct((owners, shard, width), BF),
             jax.ShapeDtypeStruct((13 * width // 128, 1, 128), F32),
         ],
         in_specs=[VMEM] * 8,
-        out_specs=[VMEM] * 5,
+        out_specs=[ANY] + [VMEM] * 4,
         scratch_shapes=[
             pltpu.VMEM((seqs, rows, width), BF),
             pltpu.VMEM((2, rows, width), BF),
@@ -733,8 +731,8 @@
             pltpu.VMEM((seqs, rows, local), BF),
             pltpu.VMEM((8, mix), F32),
         ]
-        + [pair, block, block] * 2
-        + [dma((1,))]
+        + [pair, block, pair, block, block]
+        + [dma((2,))]
         + [dma((HALF,))] * 12,
         compiler_params=pltpu.CompilerParams(
             collective_id=3, has_side_effects=True, vmem_limit_bytes=VMEM_BYTES
@@ -839,8 +837,8 @@
 
 
 def third_kernel(head_dim, owners, gown, w, wo, vec, rot, tokens, xg, packed1,
-                 qkv_h, prob_h, ctx_h, act_h, slope_h, out_grad1, vrows1,
-                 out, r0, r1, ro, rv,
+                 qkv_h, prob_h, ctx_h, act_h, slope_h, out_grad1, vrows1, shares,
+                 out, r0, r1, ro, rv, rest,
                  gg, work, mixes, sums, qkv, prob, ctx, act, slope, packed0, out_grad0, vrows0,
                  both, met, landed, from_y0, acc0, from_far0, from_y1, acc1, from_far1,
                  loc, keep, os, orr, vs, vr, own_sem, *sems):
@@ -856,6 +854,13 @@
     vec_part = 13 * gown.shape[1] // total
     greet_all(here)
     gather.start(loc.at[0])
+
+    def share_copy(k):
+        owner = core * HALF + across(chip, k)
+        return remote(shares.at[k], rest.at[k - 1], sems[20].at[k], sems[21].at[k], here.device(owner))
+
+    for k in range(1, HALF):
+        share_copy(k).start()
     settle1.start()
     loads = [pltpu.make_async_copy(a, b, keep.at[i]) for i, (a, b) in enumerate(kept)]
     for copy in loads:
@@ -977,9 +982,11 @@
     collect(0, out_grad0, vrows0)
     settle1.drain()
     settle0.drain()
-
-
-def third_layer(here, head_dim, gown, w, wo, vec, rot, tokens, xg, kept, packed1, out_grad1, vrows1):
+    for k in range(1, HALF):
+        share_copy(k).wait()
+
+
+def third_layer(here, head_dim, gown, w, wo, vec, rot, tokens, xg, kept, packed1, out_grad1, vrows1, shares):
     seqs, rows, width = xg.shape
     local = wo.shape[0]
     ff = (w.shape[1] - 3 * local) // 2
@@ -1002,9 +1009,10 @@
             owned,
             jax.ShapeDtypeStruct((LAYERS, here.groups, shard, width), BF),
             jax.ShapeDtypeStruct((LAYERS, total, sent, 1, 128), F32),
+            jax.ShapeDtypeStruct((HALF - 1, rows, width), BF),
         ],
-        in_specs=[VMEM] * 8 + [ANY] * 7,
-        out_specs=[VMEM] + [ANY] * 4,
+        in_specs=[VMEM] * 8 + [ANY] * 8,
+        out_specs=[VMEM] + [ANY] * 5,
         scratch_shapes=[
             pltpu.VMEM((seqs, rows, width), BF),
             pltpu.VMEM((2, rows, width), BF),
@@ -1020,12 +1028,13 @@
             dma((LAYERS, total)), dma((LAYERS, total)), dma((LAYERS,)),
         ]
         + [dma((HALF,))] * 8
-        + settle_sems * 2,
+        + settle_sems * 2
+        + [dma((HALF,))] * 2,
         compiler_params=pltpu.CompilerParams(
             collective_id=4, has_side_effects=True, vmem_limit_bytes=VMEM_BYTES
         ),
         name="third_layer",
-    )(gown, w, wo, vec, rot, tokens, xg, packed1, *kept, out_grad1, vrows1)
+    )(gown, w, wo, vec, rot, tokens, xg, packed1, *kept, out_grad1, vrows1, shares)
 
 
 def adam_kernel(groups, local, ff, fixes, r0, r1, ro, *refs):
@@ -1164,12 +1173,14 @@
     hidden0, xnext, grads_all, *kept = first_layer(
         head_dim, lens, xg, w0, out_rows[0], vectors[0], rot, tokens, grad_own
     )
-    hidden1, grad0, packed1, out_grad1, vrows1 = second_layer(
+    shares, grad0, packed1, out_grad1, vrows1 = second_layer(
         here, head_dim, owners, shard, lens, xnext, grads_all, w1, out_rows[1], vectors[1], rot, hidden0
     )
-    input_grad, r0, r1, ro, rv = third_layer(
-        here, head_dim, grad0, w0, out_rows[0], vectors[0], rot, tokens, xg, kept, packed1, out_grad1, vrows1
+    input_grad, r0, r1, ro, rv, rest = third_layer(
+        here, head_dim, grad0, w0, out_rows[0], vectors[0], rot, tokens, xg, kept, packed1, out_grad1, vrows1, shares
     )
+    hidden1 = hidden0.astype(F32) + (vectors[1, 7:8] + vectors[1, 12:13]) + shares[0].astype(F32)
+    hidden1 = (hidden1 + jnp.sum(rest.astype(F32), 0)).astype(BF)
     step_float = step_count[0].astype(F32)
     first_fix = 1.0 - jnp.power(BETA_FIRST, step_float)
     second_fix = 1.0 - jnp.power(BETA_SECOND, step_float)

time: 412 us -> 413 us (level)
  other arithmetic: 15.6 us -> 19.8 us
    pallas_call x1, Pallas kernels: 89.9 us -> 69.5 us  [second_layer(): pl.pallas_call(functools.partial(second_kernel, head_dim), out_shape=[jax...]
    pallas_call x1, Pallas kernels: 118 us -> 138 us  [third_layer(): pl.pallas_call(functools.partial(third_kernel, head_dim, owners), out_sha...]
where the time goes in v4:
time: 413 us; the launch traced here: 409 us
  Pallas kernels  378 us (92%)
  other arithmetic  19.8 us (5%)
  local copies, waits for them, and re-layouts  9.09 us (2%)
    pallas_call x1, Pallas kernels, third_layer(): pl.pallas_call(functools.partial(third_kernel, head_dim, owners), out_sha...  138 us
    pallas_call x1, Pallas kernels, spread(): pl.pallas_call(functools.partial(spread_kernel, owners), out_shape=(gathe...  94.6 us
    pallas_call x1, Pallas kernels, second_layer(): pl.pallas_call(functools.partial(second_kernel, head_dim), out_shape=[jax...  69.5 us
    pallas_call x1, Pallas kernels, first_layer(): pl.pallas_call(functools.partial(first_kernel, head_dim), out_shape=[jax....  63.7 us
    pallas_call x1, Pallas kernels, adam_step(): pl.pallas_call(functools.partial(adam_kernel, groups, local, ff), grid=(L...  12 us

profile of v4, /device:TPU:1, one launch (start us, length us, event | category | flops | bytes accessed | tf_op | source)
XLA Modules:
  0.0 408.8 jit_solution(570699671035616885)
XLA Ops:
  0.7 0.0 copy-start.4
  1.5 1.3 fusion.22
  2.8 0.6 iota_compare_fusion
  3.5 0.9 select_reduce_fusion
  4.3 0.7 pad_maximum_fusion.4.fixes
  5.0 1.2 convert_reduce_fusion.1
  6.2 1.3 fusion.2
  7.6 0.7 convert_element_type.86
  8.3 0.1 reshape.382
  8.4 0.6 bitcast_convert_fusion.vec
  9.0 0.7 broadcast_in_dim.71.lens
  9.6 1.6 convert_element_type.85.wo
  11.2 0.5 cosine_select_fusion
  11.8 0.8 pad_maximum_fusion.3.rot
  12.5 0.0 copy-done.4
  12.6 0.0 copy-start
  12.7 0.0 copy-start.5
  12.7 0.1 copy.74
  12.8 0.2 reshape.381
  13.0 0.0 copy-start.3
  13.0 0.1 copy.75
  13.1 0.2 reshape.380
  13.3 0.3 copy-done
  13.6 1.0 fusion.3.xh
  14.7 0.0 copy-done.5
  14.7 0.9 broadcast_select_fusion.gr
  15.6 0.0 copy-done.3
  15.6 0.1 convert.18
  15.7 0.1 copy.62
  15.8 0.1 copy.59
  15.9 0.9 copy-done.2
  16.8 0.1 convert.19
  16.9 0.1 copy.63
  17.0 0.1 copy.60
  17.1 0.2 copy_bitcast_fusion.3
  17.3 0.9 pad_maximum_fusion.1.s0
  18.2 0.2 copy_bitcast_fusion
  18.3 0.9 pad_maximum_fusion.2.s1
  19.3 94.6 %spread.1 = (bf16[8,256,1024]{2,1,0:T(8,128)(2,1)}, bf16[2,4,2,2,32,1408]{5,4,3,2,1,0:T(8,128)(2,1)}, bf16[2,4,2,2,32,1408]{5,4,3,2,1,0:T(8,128)(2,1)}, bf16[4,2,32,1024]{3,2,1,0:T(8,128)(2,1)}, f32[32,8,128]{2,1,0:T(8,128)}) custom-call(bf16[256,1024]{1,0:T(8,128)(2,1)} %fusion.3.xh, bf16[8,32,1408]{2,1,0:T(8,128)(2,1)} %pad_maximum_fusion.1.s0, ...), custom_call_target="tpu_custom_call" | custom-call | tf_op jit(solution)/shard_map/spread/pallas_call | solution.py:237
  113.9 1.9 fusion.28
  115.8 0.9 copy.76
  116.7 0.2 reshape.387
  116.9 0.1 reshape.388
  117.1 0.6 slice_add_fusion
  117.7 0.7 fusion.10
  118.3 63.7 %first_layer.1 = (bf16[256,1024]{1,0:T(8,128)(2,1)}, bf16[256,1024]{1,0:T(8,128)(2,1)}, bf16[8,256,1024]{2,1,0:T(8,128)(2,1)}, bf16[8,256,384]{2,1,0:T(8,128)(2,...) custom-call(s32[8,1,256]{2,1,0:T(1,128)} %broadcast_in_dim.71.lens, ...), custom_call_target="tpu_custom_call" | custom-call | tf_op jit(solution)/shard_map/first_layer/pallas_call | solution.py:558
  182.1 69.5 %second_layer.1 = (bf16[4,256,1024]{2,1,0:T(8,128)(2,1)}, bf16[256,1024]{1,0:T(8,128)(2,1)}, bf16[2,4,2,2,32,1408]{5,4,3,2,1,0:T(8,128)(2,1)}, bf16[4,32,1024]{2,1,0:T(8,128)(2,1)}, f32[104,1,128]{2,1,0:T(1,128)}) custom-call(s32[8,1,256]{2,1,0:T(1,128)} %broadcast_in_dim.71.lens, bf16[256,1024]{1,0:T(8,128)(2,1)} %get-tuple-element.67.xown, ...), custom_call_target="tpu_custom_call" | custom-call | tf_op jit(solution)/shard_map/second_layer/pallas_call | solution.py:715
  251.6 137.9 %third_layer.1 = (bf16[256,1024]{1,0:T(8,128)(2,1)}, bf16[8,32,1408]{2,1,0:T(8,128)(2,1)}, bf16[8,32,1408]{2,1,0:T(8,128)(2,1)}, bf16[2,4,32,1024]{3,2,1,0:T(8,1...) custom-call(bf16[256,1024]{1,0:T(8,128)(2,1)} %get-tuple-element.71.gown, ...), custom_call_target="tpu_custom_call" | custom-call | tf_op jit(solution)/shard_map/third_layer/pallas_call | solution.py:1004
  389.5 0.0 copy-start.1
  389.5 0.0 copy-start.7
  389.6 1.9 convert_reduce_fusion
  391.5 0.0 copy-done.1
  391.5 0.0 copy-done.7
  391.5 1.3 fusion.6
  392.8 0.0 copy-start.6
  392.8 0.0 copy-start.8
  392.8 0.0 copy-start.9
  392.8 0.0 copy-start.10
  392.8 1.1 pad_maximum_fusion
  393.9 0.1 reduce_sum.59
  394.0 0.0 copy-done.8
  394.0 0.7 add_multiply_fusion
  394.7 12.0 %adam_step.1 = (f32[2,32,3072]{2,1,0:T(8,128)}, f32[2,32,1024]{2,1,0:T(8,128)}, f32[2,32,4096]{2,1,0:T(8,128)}, f32[2,32,4096]{2,1,0:T(8,128)}, f32[2,32,3072]{2...) custom-call(f32[2]{0:T(128)} %pad_maximum_fusion.4.fixes, ...), custom_call_target="tpu_custom_call" | custom-call | tf_op jit(solution)/shard_map/adam_step/pallas_call | solution.py:1088
  406.7 1.9 copy.80
  (19 shorter events, 0.3 us)
Async XLA Ops:
  0.7 11.9 %copy-start.4 = (f32[2,32,3072]{2,1,0:T(8,128)S(1)}, f32[2,32,3072]{2,1,0:T(8,128)}, u32[]{:S(2)}) copy-start(f32[2,32,3072]{2,1,0:T(8,128)} %refs_0_.1) | copy-start | bytes 2359300
  12.6 1.0 copy-start
  12.7 2.0 copy-start.5
  13.0 2.6 copy-start.3
  15.6 1.2 copy-start.2
  389.5 1.9 copy-start.1
  389.5 1.9 copy-start.7
  392.8 1.1 copy-start.6
  392.8 1.2 copy-start.8
  392.8 1.2 copy-start.9
  392.8 1.2 copy-start.10

commit v5 on v3

--- a/solution.py
+++ b/solution.py
@@ -102,11 +102,12 @@
     pl.semaphore_wait(barrier, here.total - 1)
 
 
-def spread_kernel(owners, xh, s0, s1, wo, vec, xg, w0, w1, wog, vecg,
+def spread_kernel(owners, xh, gr, s0, s1, wo, vec, xg, gg, w0, w1, wog, vecg,
                   ps, pr, zs, zr, ys, yr, os, orr, vs, vr, loc, *sems):
     here = Place()
     far, y, tp, row, x = here.far, here.y, here.tp, here.row, here.x
     gather_x = Gather(here, xh, xg, sems[0:4])
+    gather_g = Gather(here, gr, gg, sems[4:8])
     layers = ((s0, w0), (s1, w1))
     greet_all(here)
 
@@ -188,17 +189,20 @@
     first_hop(0)
     first_hop(1)
     gather_x.start(loc.at[0])
+    gather_g.start(loc.at[2])
     for l in range(LAYERS):
         for r in range(HALF):
             for i in range(1, here.fars):
                 landed(l, lax.rem(far + here.fars - i, here.fars), r, y, zr.at[l, i, r])
                 for j in range(1, here.ys):
                     along_y(l, j, i, r).start()
-    for k in range(1, HALF):
-        gather_x.wait_block(k)
-    gather_x.wait_partner()
-    for k in range(1, HALF):
-        gather_x.wait_passed(k)
+    for gather in (gather_x, gather_g):
+        for k in range(1, HALF):
+            gather.wait_block(k)
+    for gather in (gather_x, gather_g):
+        gather.wait_partner()
+        for k in range(1, HALF):
+            gather.wait_passed(k)
     for l in range(LAYERS):
         for j in range(1, here.ys):
             for i in range(here.fars):
@@ -212,6 +216,7 @@
     for j in range(owners):
         pltpu.make_async_copy(wo, wog.at[j], orr.at[j]).wait()
     gather_x.drain()
+    gather_g.drain()
     for l in range(LAYERS):
         for step in range(1, TP):
             within(l, step).wait_send()
@@ -228,7 +233,7 @@
             out_copy(f, v).wait_send()
 
 
-def spread(here, xh, s0, s1, wo, vec):
+def spread(here, xh, gr, s0, s1, wo, vec):
     rows, cols = s0.shape[1:]
     owners = wo.shape[2] // TP // rows
     dma = pltpu.SemaphoreType.DMA
@@ -238,23 +243,24 @@
         functools.partial(spread_kernel, owners),
         out_shape=(
             gathered,
+            gathered,
             whole,
             whole,
             jax.ShapeDtypeStruct((owners,) + wo.shape, BF),
             jax.ShapeDtypeStruct((here.total,) + vec.shape, F32),
         ),
-        in_specs=[VMEM] + [ANY] * 4,
-        out_specs=(ANY,) * 5,
+        in_specs=[VMEM] * 2 + [ANY] * 4,
+        out_specs=(ANY,) * 6,
         scratch_shapes=[
             dma((LAYERS, TP)), dma((LAYERS, TP)),
             dma((LAYERS, here.fars, HALF)), dma((LAYERS, here.fars, HALF)),
             dma((LAYERS, here.ys, here.fars, HALF)), dma((LAYERS, here.ys, here.fars, HALF)),
-            dma((here.fars, here.ys)), dma((owners,)), dma((here.total,)), dma((here.total,)), dma((2,)),
+            dma((here.fars, here.ys)), dma((owners,)), dma((here.total,)), dma((here.total,)), dma((3,)),
         ]
-        + [dma((HALF,))] * 4,
+        + [dma((HALF,))] * 8,
         compiler_params=pltpu.CompilerParams(collective_id=1, has_side_effects=True),
         name="spread",
-    )(xh, s0, s1, wo, vec)
+    )(xh, gr, s0, s1, wo, vec)
 
 
 def turn(values, rot):
@@ -364,6 +370,7 @@
 
 
 CHUNK = 32
+ORDER = (0, 3, 1, 2)
 
 
 def chunks(rows, body):
@@ -442,7 +449,7 @@
 
     def start(self, local):
         pltpu.make_async_copy(self.own, self.buffer.at[self.tp], local).start()
-        for k in (1, 2, 3, 0):
+        for k in ORDER[1:] + ORDER[:1]:
             self.to_peer(k).start()
         pltpu.make_async_copy(self.own, self.buffer.at[self.tp], local).wait()
 
@@ -482,14 +489,13 @@
     greet([here.device(target) for target in targets])
 
 
-def first_kernel(head_dim, lens, xg, w, wo, vec, rot, own, gr,
-                 out, xnext, gg, qkv_h, prob_h, ctx_h, act_h, slope_h,
+def first_kernel(head_dim, lens, xg, w, wo, vec, rot, own,
+                 out, xnext, qkv_h, prob_h, ctx_h, act_h, slope_h,
                  qkv, prob, ctx, act, slope, both, met, landed, keep, *sems):
     here = Place()
     tp, core, chip = here.tp, here.core, here.chip
     local, ff = wo.shape[0], act.shape[2]
-    swap = Exchange(here, both, met, landed, sems[0:4])
-    gather = Gather(here, gr, gg, sems[4:8])
+    swap = Exchange(here, both, met, landed, sems)
     kept = [(qkv, qkv_h), (prob, prob_h), (ctx, ctx_h), (act, act_h), (slope, slope_h)]
     greet_block(here)
     b_in, b_up = bias_slices(vec, tp, local, ff)
@@ -518,14 +524,10 @@
         swap.to_partner(k).start()
         if k + 1 < HALF:
             swap.hand_over(k + 1)
-        if k == 0:
-            gather.start(keep.at[5])
     swap.hand_over(0)
     saved = [pltpu.make_async_copy(a, b, keep.at[i]) for i, (a, b) in enumerate(kept)]
     for copy in saved:
         copy.start()
-    for k in range(1, HALF):
-        gather.wait_block(k)
     swap.wait_landed()
 
     def finish(at):
@@ -535,16 +537,12 @@
         xnext[at] = (centred * scale).astype(BF)
 
     chunks(own.shape[0], finish)
-    gather.wait_partner()
-    for k in range(1, HALF):
-        gather.wait_passed(k)
-    gather.drain()
     swap.drain()
     for copy in saved:
         copy.wait()
 
 
-def first_layer(head_dim, lens, xg, w, wo, vec, rot, own, gr):
+def first_layer(head_dim, lens, xg, w, wo, vec, rot, own):
     seqs, rows, width = xg.shape
     local = wo.shape[0]
     ff = (w.shape[1] - 3 * local) // 2
@@ -558,15 +556,15 @@
     return pl.pallas_call(
         functools.partial(first_kernel, head_dim),
         out_shape=[jax.ShapeDtypeStruct((rows, width), BF)] * 2
-        + [jax.ShapeDtypeStruct(s, BF) for s in [xg.shape] + kept],
-        in_specs=[VMEM] * 8,
-        out_specs=[VMEM] * 2 + [ANY] * 6,
-        scratch_shapes=[pltpu.VMEM(s, BF) for s in kept] + [pair, block, block] + [dma((6,))] + [dma((HALF,))] * 8,
+        + [jax.ShapeDtypeStruct(s, BF) for s in kept],
+        in_specs=[VMEM] * 7,
+        out_specs=[VMEM] * 2 + [ANY] * 5,
+        scratch_shapes=[pltpu.VMEM(s, BF) for s in kept] + [pair, block, block] + [dma((5,))] + [dma((HALF,))] * 4,
         compiler_params=pltpu.CompilerParams(
             collective_id=2, has_side_effects=True, vmem_limit_bytes=VMEM_BYTES
         ),
         name="first_layer",
-    )(lens, xg, w, wo, vec, rot, own, gr)
+    )(lens, xg, w, wo, vec, rot, own)
 
 
 def weight_grads(xg, gg, mixes, act, ctx, w, vec, sums, packed, out_grad, vrows, grad_rows, tp):
@@ -659,11 +657,11 @@
         sums[:, 3 * local :] += fold_rows(expanded_grad)
         return part, back
 
-    for k in range(HALF):
+    for n, k in enumerate(ORDER):
         if k:
             gather.wait_block(k)
-            swap_e.hand_over(k - 1)
-            swap.hand_over(k - 1)
+            swap_e.hand_over(ORDER[n - 1])
+            swap.hand_over(ORDER[n - 1])
             gather.wait_passed(k)
         else:
             gather.wait_partner()
@@ -679,8 +677,8 @@
         lax.fori_loop(0, 2, part_of, 0)
         swap_e.to_partner(k).start()
         swap.to_partner(k).start()
-    swap_e.hand_over(HALF - 1)
-    swap.hand_over(HALF - 1)
+    swap_e.hand_over(ORDER[-1])
+    swap.hand_over(ORDER[-1])
     weight_grads(xg, gg, mixes, act, ctx, w, vec, sums, packed, out_grad, vrows, gg[tp], tp)
     swap_e.wait_landed()
 
@@ -933,10 +931,10 @@
         sums[:, 3 * local :] += fold_rows(expanded_grad)
         return back
 
-    for k in range(HALF):
+    for n, k in enumerate(ORDER):
         if k:
             gather.wait_block(k)
-            swap.hand_over(k - 1)
+            swap.hand_over(ORDER[n - 1])
             gather.wait_passed(k)
         else:
             gather.wait_partner()
@@ -949,13 +947,13 @@
 
         lax.fori_loop(0, 2, part_of, 0)
         swap.to_partner(k).start()
-        if k == 2:
+        if n == 2:
             settle1.pass_far()
     for copy in loads[3:]:
         copy.wait()
     weight_grads(xg, gg, mixes, act, ctx, w, vec, sums, packed0, out_grad0, vrows0, gg[tp], tp)
     settle0.start()
-    swap.hand_over(HALF - 1)
+    swap.hand_over(ORDER[-1])
     settle1.hand_out()
     send(0, out_grad0, vrows0)
     settle0.pass_far()
@@ -1154,15 +1152,17 @@
     vec = jnp.pad(layer_vectors.astype(BF).astype(F32).reshape(-1), (0, 8 * 128 - 2 * vec_part)).reshape(8, 128)
     xhat_own = standard(tokens.astype(F32)).astype(BF)
     grad_own = jnp.where(valid, cotangent, jnp.zeros_like(cotangent))
-    xg, w0, w1, wog, vecg = spread(here, xhat_own, blocks[0], blocks[1], attend_out.astype(BF), vec)
+    xg, grads_all, w0, w1, wog, vecg = spread(
+        here, xhat_own, grad_own, blocks[0], blocks[1], attend_out.astype(BF), vec
+    )
     w0, w1 = w0.reshape(width, -1), w1.reshape(width, -1)
     out_rows = wog.transpose(1, 0, 2, 3).reshape(LAYERS, local, width)
     vectors = vecg.reshape(total, -1)[:, : 2 * vec_part].reshape(total, LAYERS, vec_part)
     vectors = vectors.transpose(1, 0, 2).reshape(LAYERS, 13, width)
     vectors = jnp.pad(vectors, ((0, 0), (0, 3), (0, 0)))
 
-    hidden0, xnext, grads_all, *kept = first_layer(
-        head_dim, lens, xg, w0, out_rows[0], vectors[0], rot, tokens, grad_own
+    hidden0, xnext, *kept = first_layer(
+        head_dim, lens, xg, w0, out_rows[0], vectors[0], rot, tokens
     )
     hidden1, grad0, packed1, out_grad1, vrows1 = second_layer(
         here, head_dim, owners, shard, lens, xnext, grads_all, w1, out_rows[1], vectors[1], rot, hidden0

time: 412 us -> 393 us (0.954); the launches traced: 404 us -> 389 us
  Pallas kernels: 379 us -> 364 us
    pallas_call x1, Pallas kernels: 63.8 us -> 40.4 us  [first_layer(): pl.pallas_call(functools.partial(first_kernel, head_dim), out_shape=[jax....]
    pallas_call x1, Pallas kernels: 94.6 us -> 115 us  [spread(): pl.pallas_call(functools.partial(spread_kernel, owners), out_shape=(gathe...]
    pallas_call x1, Pallas kernels: 89.9 us -> 79.3 us  [second_layer(): pl.pallas_call(functools.partial(second_kernel, head_dim), out_shape=[jax...]
where the time goes in v5:
time: 393 us; the launch traced here: 389 us
  Pallas kernels  364 us (93%)
  other arithmetic  15.6 us (4%)
  local copies, waits for them, and re-layouts  7.64 us (2%)
    pallas_call x1, Pallas kernels, third_layer(): pl.pallas_call(functools.partial(third_kernel, head_dim, owners), out_sha...  117 us
    pallas_call x1, Pallas kernels, spread(): pl.pallas_call(functools.partial(spread_kernel, owners), out_shape=(gathe...  115 us
    pallas_call x1, Pallas kernels, second_layer(): pl.pallas_call(functools.partial(second_kernel, head_dim), out_shape=[jax...  79.3 us
    pallas_call x1, Pallas kernels, first_layer(): pl.pallas_call(functools.partial(first_kernel, head_dim), out_shape=[jax....  40.4 us
    pallas_call x1, Pallas kernels, adam_step(): pl.pallas_call(functools.partial(adam_kernel, groups, local, ff), grid=(L...  12 us

profile of v5, /device:TPU:1, one launch (start us, length us, event | category | flops | bytes accessed | tf_op | source)
XLA Modules:
  0.0 388.9 jit_solution(8274213663155413725)
XLA Ops:
  0.7 0.0 copy-start.2
  0.7 1.4 fusion.14
  2.1 0.6 iota_compare_fusion
  2.8 1.9 broadcast_select_fusion.gr
  4.7 0.0 copy-done.2
  4.7 0.0 copy-start.1
  4.7 0.1 convert.17
  4.8 0.1 copy.62
  4.9 1.0 copy-done.1
  5.9 0.1 convert.18
  6.0 0.0 copy-start.3
  6.0 0.1 copy.63
  6.1 0.2 copy_bitcast_fusion
  6.3 0.8 copy-done.3
  7.2 0.1 copy.74
  7.4 0.2 reshape.366
  7.5 0.9 pad_maximum_fusion.2.s1
  8.5 0.1 copy.59
  8.5 0.1 copy.60
  8.6 0.2 copy_bitcast_fusion.3
  8.8 0.0 copy-start
  8.8 0.1 copy.75
  9.0 0.2 reshape.365
  9.1 0.0 copy-start.4
  9.1 0.9 pad_maximum_fusion.1.s0
  10.1 0.0 copy-done
  10.1 0.0 copy-start.7
  10.1 0.1 convert_reduce_fusion
  10.2 0.3 fusion.2
  10.5 1.1 fusion.3.xh
  11.6 0.0 copy-done.4
  11.6 0.7 convert_element_type.70.wo
  12.3 0.0 copy-done.7
  12.3 0.1 reshape.367
  12.4 0.6 bitcast_convert_fusion.vec
  13.0 115.2 %spread.1 = (bf16[8,256,1024]{2,1,0:T(8,128)(2,1)}, bf16[8,256,1024]{2,1,0:T(8,128)(2,1)}, bf16[2,4,2,2,32,1408]{5,4,3,2,1,0:T(8,128)(2,1)}, bf16[2,4,2,2,32,140...) custom-call(bf16[256,1024]{1,0:T(8,128)(2,1)} %fusion.3.xh, ...), custom_call_target="tpu_custom_call" | custom-call | tf_op jit(solution)/shard_map/spread/pallas_call | solution.py:242
  128.1 0.0 copy-start.6
  128.2 1.0 copy.76
  129.2 0.2 reshape.372
  129.4 0.0 copy-start.8
  129.4 0.0 copy-start.9
  129.4 0.1 reshape.373
  129.5 0.7 fusion.7
  130.2 0.0 copy-done.6
  130.2 0.8 fusion.25
  131.1 0.5 cosine_select_fusion
  131.6 0.8 pad_maximum_fusion.3.rot
  132.4 0.0 copy-done.8
  132.4 0.0 copy-done.9
  132.4 0.2 select_reduce_fusion
  132.6 0.7 broadcast_in_dim.71.lens
  133.2 40.4 %first_layer.1 = (bf16[256,1024]{1,0:T(8,128)(2,1)}, bf16[256,1024]{1,0:T(8,128)(2,1)}, bf16[8,256,384]{2,1,0:T(8,128)(2,1)}, bf16[8,2,256,256]{3,2,1,0:T(8,128)...) custom-call(s32[8,1,256]{2,1,0:T(1,128)} %broadcast_in_dim.71.lens, ...), custom_call_target="tpu_custom_call" | custom-call | tf_op jit(solution)/shard_map/first_layer/pallas_call | solution.py:556
  173.7 79.3 %second_layer.1 = (bf16[256,1024]{1,0:T(8,128)(2,1)}, bf16[256,1024]{1,0:T(8,128)(2,1)}, bf16[2,4,2,2,32,1408]{5,4,3,2,1,0:T(8,128)(2,1)}, bf16[4,32,1024]{2,1,0:T(8,128)(2,1)}, f32[104,1,128]{2,1,0:T(1,128)}) custom-call(s32[8,1,256]{2,1,0:T(1,128)} %broadcast_in_dim.71.lens, bf16[256,1024]{1,0:T(8,128)(2,1)} %get-tuple-element.66.xown, ...), custom_call_target="tpu_custom_call" | custom-call | tf_op jit(solution)/shard_map/second_layer/pallas_call | solution.py:715
  253.0 116.8 %third_layer.1 = (bf16[256,1024]{1,0:T(8,128)(2,1)}, bf16[8,32,1408]{2,1,0:T(8,128)(2,1)}, bf16[8,32,1408]{2,1,0:T(8,128)(2,1)}, bf16[2,4,32,1024]{3,2,1,0:T(8,128)(2,1)}, f32[2,32,4,1,128]{4,3,2,1,0:T(1,128)}) custom-call(bf16[256,1024]{1,0:T(8,128)(2,1)} %get-tuple-element.70.gown, bf16[1024,1408]{1,0:T(8,128)(2,1)} %bitcast.62, ...), custom_call_target="tpu_custom_call" | custom-call | tf_op jit(solution)/shard_map/third_layer/pallas_call | solution.py:995
  370.5 0.6 pad_maximum_fusion.4.fixes
  371.1 12.0 %adam_step.1 = (f32[2,32,3072]{2,1,0:T(8,128)}, f32[2,32,1024]{2,1,0:T(8,128)}, f32[2,32,4096]{2,1,0:T(8,128)}, f32[2,32,4096]{2,1,0:T(8,128)}, f32[2,32,3072]{2...) custom-call(f32[2]{0:T(128)} %pad_maximum_fusion.4.fixes, ...), custom_call_target="tpu_custom_call" | custom-call | tf_op jit(solution)/shard_map/adam_step/pallas_call | solution.py:1077
  383.1 0.0 copy-start.5
  383.1 1.1 reduce_sum.49
  384.2 1.4 add_multiply_fusion
  385.6 2.3 pad_maximum_fusion
  387.9 0.0 copy-done.5
  387.9 0.8 copy.80
  (16 shorter events, 0.3 us)
Async XLA Ops:
  0.7 4.0 %copy-start.2 = (f32[2,32,4096]{2,1,0:T(8,128)S(1)}, f32[2,32,4096]{2,1,0:T(8,128)}, u32[]{:S(2)}) copy-start(f32[2,32,4096]{2,1,0:T(8,128)} %refs_2_.1) | copy-start | bytes 3145732
  4.7 1.2 copy-start.1
  6.0 1.1 copy-start.3
  8.8 1.3 copy-start
  9.1 2.5 copy-start.4
  10.1 2.2 copy-start.7
  128.1 2.0 copy-start.6
  129.4 3.0 copy-start.8
  129.4 3.0 copy-start.9
  383.1 4.8 %copy-start.5 = (bf16[256,1024]{1,0:T(8,128)(2,1)S(1)}, bf16[256,1024]{1,0:T(8,128)(2,1)}, u32[]{:S(2)}) copy-start(bf16[256,1024]{1,0:T(8,128)(2,1)} %get-tuple-element.146) | copy-start | bytes 1572868
